TPU v7x, 512 devices: a whole 4x8x8 slice. The times are simulated.
512 devices in a mesh: rad: 16 (over y_hi, z), ma: 32 (over y_lo, x, core).
Axes of the slice: x: 4, y: 8 (y_hi: 2, y_lo: 4; y = y_hi * 4 + y_lo), z: 8, core: 2. Of those that a mesh axis runs over, the one named last changes fastest.
Arguments:
- spectrum: bfloat16 [4, 512, 512, 384], P(None, 'ma', 'rad'), may hold values from -6 to 6
- radial_table: bfloat16 [12, 384], replicated, may hold values from -0.3125 to 0.3125
- legendre: bfloat16 [512, 512, 512], P('ma', 'rad'), may hold values from -0.375 to 0.375
- order_table: int32 [512], replicated, may hold values from 0 to 511, each once
- cylinder_row: int32 [512, 12], P(('rad', 'ma')), may hold values from 0 to 511
- column_weight: float32 [512, 12], P(('rad', 'ma')), may hold values from 0.5 to 2
Outputs:
- column_buoyancy: float32 [512, 1024], P('ma', 'rad')
- advected: float32 [2, 512, 12, 1024], P(None, ('rad', 'ma'))
Inputs may be any that keep to these rules, and one draw needn't show every extreme that they name: `order_table`: each order appears in exactly one slot.
All inputs are finite; a program needn't handle non-finite values.
Results may differ from a plain program's by a relative error of at most 0.008.
Values may be sent and summed in bfloat16 or wider, within the bound.
No kernel may reach another device: no remote copies, remote signals or barrier semaphores. Data moves between devices by JAX's collectives and lax.ppermute only.
A program may use at most 64 MiB of HBM per device.

v0:
```python
import math

import jax
import jax.numpy as jnp
from jax import lax
from jax.sharding import PartitionSpec as P

L = 512
NPHI = 1024
QROWS = 16


time_step = 0.05
composition_weight = 0.8


def padded(block, sides, width, periodic):
    for axis, dim in sides:
        count = lax.axis_size(axis)
        forward = [(i, i + 1) for i in range(count - 1)]
        if periodic:
            forward.append((count - 1, 0))
        backward = [(target, source) for source, target in forward]
        low = lax.ppermute(
            lax.slice_in_dim(block, block.shape[dim] - width, None, axis=dim), axis, forward
        )
        high = lax.ppermute(lax.slice_in_dim(block, 0, width, axis=dim), axis, backward)
        block = jnp.concatenate([low, block, high], axis=dim)
    return block


def in_order(blocks, dim):
    dims = list(blocks.shape[1:])
    dims[dim] *= blocks.shape[0]
    return jnp.moveaxis(blocks, 0, dim).reshape(dims)


def sent_to_all(value, axis):
    copies = jnp.broadcast_to(value, (lax.axis_size(axis), *value.shape))
    return lax.all_to_all(copies, axis, split_axis=0, concat_axis=0, tiled=True)


def collect(value, axis, dim):
    return in_order(sent_to_all(value, axis), dim)


def in_blocks(value, dim, devices):
    before, after = (value.shape[:dim], value.shape[dim + 1 :])
    return jnp.moveaxis(value.reshape(*before, devices, -1, *after), dim, 0)


def summed_on_arrival(value, axis, dim):
    blocks = in_blocks(value, dim, lax.axis_size(axis))
    arrived = lax.all_to_all(blocks, axis, split_axis=0, concat_axis=0, tiled=True)
    return arrived.sum(axis=0)


def synthesis_tables(order_table):
    longitude = jnp.arange(NPHI, dtype=jnp.int32)
    phase_index = order_table[:, None] * longitude[None, :] % NPHI
    angles = phase_index.astype(jnp.float32) * (2.0 * math.pi / NPHI)
    weights = jnp.where(order_table == 0, 1.0, 2.0).astype(jnp.float32) / math.sqrt(L)
    cosine = jnp.cos(angles) * weights[:, None]
    sine = jnp.sin(angles) * weights[:, None]
    slopes = (order_table.astype(jnp.float32) / L)[:, None]
    values = jnp.stack([cosine, -sine])
    turned = jnp.stack([-sine * slopes, -cosine * slopes])
    return jnp.concatenate([values, turned], axis=2).astype(jnp.bfloat16)


def stream_velocity(outward_diff, around_diff, radius):
    outward = outward_diff / (2.0 * radius[:, None])
    beside_all = -around_diff * 0.5
    return jnp.stack([outward, beside_all]).astype(jnp.bfloat16)


def owner_velocity(owned, row_block, total_rows):
    lon_padded = padded(owned, (("rad", 1),), 1, True)
    row_padded = padded(owned, (("ma", 0),), 1, False)
    row_index = lax.axis_index("ma") * row_block + jnp.arange(row_block, dtype=jnp.int32)
    radius = 0.35 + 0.65 * (row_index.astype(jnp.float32) + 0.5) / total_rows
    local_velocity = stream_velocity(
        lon_padded[:, 2:] - lon_padded[:, :-2], row_padded[2:] - row_padded[:-2], radius
    )
    velocity = collect(local_velocity, "rad", 2)
    return collect(velocity, "ma", 1)


def on_device(spectrum, radial_table, legendre, order_table, cylinder_row, column_weight):
    slot_count = spectrum.shape[1]
    degree_count = spectrum.shape[2]
    level_count = radial_table.shape[0]
    latitude_count = legendre.shape[2]
    rad_count = lax.axis_size("rad")
    ma_count = lax.axis_size("ma")
    total_rows = QROWS * ma_count
    row_block = QROWS
    my_orders = lax.dynamic_slice_in_dim(order_table, lax.axis_index("ma") * slot_count, slot_count)
    my_degrees = lax.axis_index("rad") * degree_count + jnp.arange(degree_count, dtype=jnp.int32)
    allowed = my_degrees[None, :] >= my_orders[:, None]
    masked_table = jnp.where(allowed[:, :, None], legendre, jnp.zeros_like(legendre))
    levels = jnp.einsum(
        "rn,ckln->rckl", radial_table, spectrum, preferred_element_type=jnp.float32
    ).astype(jnp.bfloat16)
    contribution = jnp.einsum(
        "klt,rckl->trck", masked_table, levels, preferred_element_type=jnp.float32
    )
    latitudes = summed_on_arrival(
        contribution.reshape(
            latitude_count // rad_count * lax.axis_size("rad"), level_count * 4 * slot_count
        ),
        "rad",
        0,
    ).astype(jnp.bfloat16)
    received = lax.all_to_all(latitudes, "ma", split_axis=0, concat_axis=1, tiled=True)
    lat_rows = received.shape[0]
    coefficients = received.reshape(lat_rows, ma_count, level_count, 2, 2, slot_count)
    tables = synthesis_tables(order_table).reshape(2, ma_count, slot_count, 2 * NPHI)
    synthesis = jnp.einsum(
        "tsrfik,iskq->ftrq", coefficients, tables, preferred_element_type=jnp.float32
    ).astype(jnp.bfloat16)
    fields = synthesis[..., :NPHI].astype(jnp.float32)
    slope_field = synthesis[..., NPHI:].astype(jnp.float32)
    buoyancy = fields[0] - composition_weight * fields[1]
    weighted = (column_weight[:, :, None] * buoyancy).reshape(-1, NPHI)
    point_rows = cylinder_row.reshape(-1)
    row_ids = jnp.arange(total_rows, dtype=jnp.int32)
    pieces = lax.all_to_all(weighted, "rad", split_axis=1, concat_axis=0, tiled=True)
    piece_rows = collect(point_rows, "rad", 0)
    piece_selector = (row_ids[:, None] == piece_rows[None, :]).astype(jnp.float32)
    block_partial = jnp.dot(
        piece_selector, pieces, precision=lax.Precision.HIGHEST, preferred_element_type=jnp.float32
    )
    owned = summed_on_arrival(block_partial, "ma", 0)
    velocity = owner_velocity(owned, row_block, total_rows)
    chooser = (point_rows[:, None] == row_ids[None, :]).astype(jnp.bfloat16)
    moved = jnp.einsum("pj,cjq->cpq", chooser, velocity, preferred_element_type=jnp.float32)
    moved = moved.reshape(2, lat_rows, level_count, NPHI)
    inverse = 1.0 / (0.35 + 0.65 * (cylinder_row.astype(jnp.float32) + 0.5) / total_rows)
    advected = fields - time_step * inverse[None, :, :, None] * (
        moved[1][None] * slope_field + moved[0][None] * fields
    )
    return (owned, advected)


def solution(mesh):
    return jax.shard_map(
        on_device,
        mesh=mesh,
        in_specs=(
            P(None, "ma", "rad", None),
            P(),
            P("ma", "rad", None),
            P(),
            P(("rad", "ma"), None),
            P(("rad", "ma"), None),
        ),
        out_specs=(P("ma", "rad"), P(None, ("rad", "ma"), None, None)),
        check_vma=False,
    )
```

profile of v0, /device:TPU:1, one launch (start us, length us, event | category | flops | bytes accessed | tf_op | source)
XLA Modules:
  0.0 257.5 jit_solution(8348401022167592019)
XLA Ops:
  2.1 4.2 %convolution_bitcast_fusion = f32[512,12,4,16]{0,1,2,3:T(8,128)} fusion(bf16[4,16,32,384]{3,2,1,0:T(8,128)(2,1)S(1)} %copy-done, bf16[16,32,512]{2,1,0:T(8,128)(2,1)} %param.8, pred[16,32]{1,0:T(8,128)(4,1)S(1)} %broadcast_compare_fusion, bf16[12,384]{1,0:T(8,128)(2,1)} %param.7), kind=kOutput, calls=%fused_computation.20 | convolution fusion | flops 44326912 | bytes 3679744 | tf_op jit(solution)/shard_map/klt,rckl->trck/dot_general | solution.py:105
  6.2 2.5 copy.34
  8.7 3.8 %reshape_reshape.3 = f32[16,32,768]{1,0,2:T(8,128)} reshape(f32[512,12,4,16]{0,3,2,1:T(8,128)S(1)} %copy.34) | data formatting | bytes 3145728 | tf_op jit(solution)/shard_map/reshape;reshape | solution.py:49
  12.5 6.1 %copy.35 = f32[16,32,768]{2,1,0:T(8,128)} copy(f32[16,32,768]{1,0,2:T(8,128)} %reshape_reshape.3) | data formatting | bytes 3145728 | tf_op jit(solution)/shard_map/reshape;reshape | solution.py:49
  18.6 16.3 %all-to-all-start.1 = ((f32[16,32,768]{2,1,0:T(8,128)}), f32[16,32,768]{2,1,0:T(8,128)S(1)}, u32[]{:S(2)}, u32[]{:S(2)}) async-start(f32[16,32,768]{2,1,0:T(8,128)} %copy.35), calls=%async_computation.1 | async-start | bytes 3145728 | tf_op jit(solution)/shard_map/all_to_all | solution.py:54
  35.4 38.3 %all-to-all-done.1 = f32[16,32,768]{2,1,0:T(8,128)S(1)} async-done(((f32[16,32,768]{2,1,0:T(8,128)}), f32[16,32,768]{2,1,0:T(8,128)S(1)}, u32[]{:S(2)}, u32[]{:S(2)}) %all-to-all-start.1) | async-done | bytes 1572896 | tf_op jit(solution)/shard_map/all_to_all | solution.py:54
  75.7 13.7 %all-to-all-start.2 = ((bf16[32,2,384]{2,1,0:T(2,128)(2,1)}), bf16[32,2,384]{2,1,0:T(2,128)(2,1)S(1)}, u32[]{:S(2)}, u32[]{:S(2)}) async-start(bf16[32,2,384]{2,1,0:T(2,128)(2,1)} %reshape.381), calls=%async_computation.2 | async-start | bytes 98304 | tf_op jit(solution)/shard_map/all_to_all | solution.py:115
  89.4 11.2 %fusion.10 = (bf16[1,32,16,1024]{3,1,2,0:T(8,128)(2,1)S(1)}, bf16[1,32,16,1024]{3,1,2,0:T(8,128)(2,1)}, bf16[1,32,16,1024]{3,1,2,0:T(8,128)(2,1)}, bf16[1,32,16,1024]{3,1,2,0:T(8,128)(2,1)}) fusion(f32[32,16]{0,1:T(8,128)S(1)} %copy.31, s32[32,16]{0,1:T(8,128)S(1)} %copy.30, f32[32,16]{0,1:T(8,128)S(1)} %copy.32), kind=kLoop, calls=%fused_computation.18 | loop fusion | flops 12582912 | bytes 4200448 | tf_op jit(solution)/shard_map/convert.8
  101.2 11.8 %all-to-all-start = ((s32[16,1,12]{2,1,0:T(1,128)}), s32[16,1,12]{2,1,0:T(1,128)S(1)}, u32[]{:S(2)}, u32[]{:S(2)}) async-start(s32[16,1,12]{2,1,0:T(1,128)} %broadcast_in_dim.24), calls=%async_computation | async-start | bytes 16384 | tf_op jit(solution)/shard_map/all_to_all | solution.py:40
  113.3 2.7 %fusion.3 = bf16[2,1,12,2048]{3,2,0,1:T(8,128)(2,1)S(1)} fusion(bf16[1,32,16,1024]{3,1,2,0:T(8,128)(2,1)} %get-tuple-element.16, bf16[1,32,16,1024]{3,1,2,0:T(8,128)(2,1)} %get-tuple-element.17, bf16[1,32,16,1024]{3,1,2,0:T(8,128)(2,1)} %get-tuple-element.15, bf16[1,32,16,1024]{3,1,2,0:T(8,128)(2,1)S(1)} %get-tuple-element.14, ...), kind=kOutput, calls=%fused_computation.7 | convolution fusion | flops 117489664 | bytes 4341760 | tf_op jit(solution)/shard_map/tsrfik,iskq->ftrq/dot_general | solution.py:119
  117.0 7.2 %all-to-all-done = s32[16,1,12]{2,1,0:T(1,128)S(1)} async-done(((s32[16,1,12]{2,1,0:T(1,128)}), s32[16,1,12]{2,1,0:T(1,128)S(1)}, u32[]{:S(2)}, u32[]{:S(2)}) %all-to-all-start) | async-done | bytes 800 | tf_op jit(solution)/shard_map/all_to_all | solution.py:40
  124.2 4.3 %all-to-all-start.3 = ((f32[16,1,768]{2,1,0:T(1,128)}), f32[16,1,768]{2,1,0:T(1,128)S(1)}, u32[]{:S(2)}, u32[]{:S(2)}) async-start(f32[16,1,768]{2,1,0:T(1,128)} %reshape.383), calls=%async_computation.3 | async-start | bytes 98304 | tf_op jit(solution)/shard_map/all_to_all | solution.py:128
  129.8 10.0 %all-to-all-done.3 = f32[16,1,768]{2,1,0:T(1,128)S(1)} async-done(((f32[16,1,768]{2,1,0:T(1,128)}), f32[16,1,768]{2,1,0:T(1,128)S(1)}, u32[]{:S(2)}, u32[]{:S(2)}) %all-to-all-start.3) | async-done | bytes 49184 | tf_op jit(solution)/shard_map/all_to_all | solution.py:128
  142.4 9.7 %all-to-all-start.4 = ((f32[32,1,1024]{2,1,0:T(1,128)}), f32[32,1,1024]{2,1,0:T(1,128)S(1)}, u32[]{:S(2)}, u32[]{:S(2)}) async-start(f32[32,1,1024]{2,1,0:T(1,128)} %reshape.385), calls=%async_computation.4 | async-start | bytes 262144 | tf_op jit(solution)/shard_map/all_to_all | solution.py:54
  152.2 8.5 %all-to-all-done.4 = f32[32,1,1024]{2,1,0:T(1,128)S(1)} async-done(((f32[32,1,1024]{2,1,0:T(1,128)}), f32[32,1,1024]{2,1,0:T(1,128)S(1)}, u32[]{:S(2)}, u32[]{:S(2)}) %all-to-all-start.4) | async-done | bytes 131104 | tf_op jit(solution)/shard_map/all_to_all | solution.py:54
  161.8 2.6 %collective-permute-start = (f32[16,1]{1,0:T(8,128)S(1)}, f32[16,1]{1,0:T(8,128)S(1)}, u32[]{:S(2)}, u32[]{:S(2)}) collective-permute-start(f32[16,1]{1,0:T(8,128)S(1)} %get-tuple-element.20), channel_id=1, source_target_pairs={{32,0},{64,32},{96,64},{128,96},{160,128},{192,160},{224,192},{256... | collective-permute-start | bytes 200 | tf_op jit(solution)/shard_map/ppermute | solution.py:27
  164.5 2.5 collective-permute-start.2
  166.9 3.1 %collective-permute-start.3 = (f32[1,64]{1,0:T(1,128)S(1)}, f32[1,64]{1,0:T(1,128)S(1)}, u32[]{:S(2)}, u32[]{:S(2)}) collective-permute-start(f32[1,64]{1,0:T(1,128)S(1)} %get-tuple-element.23), channel_id=1, source_target_pairs={{0,1},{1,2},{2,3},{3,4},{4,5},{5,6},{6,7},{7,8},{8,9},{9,10},{10,1... | collective-permute-start | bytes 776 | tf_op jit(solution)/shard_map/ppermute | solution.py:24
  170.0 2.7 %collective-permute-start.1 = (f32[16,1]{1,0:T(8,128)S(1)}, f32[16,1]{1,0:T(8,128)S(1)}, u32[]{:S(2)}, u32[]{:S(2)}) collective-permute-start(f32[16,1]{1,0:T(8,128)S(1)} %get-tuple-element.21), channel_id=1, source_target_pairs={{0,32},{32,64},{64,96},{96,128},{128,160},{160,192},{192,224},{224... | collective-permute-start | bytes 200 | tf_op jit(solution)/shard_map/ppermute | solution.py:24
  172.7 7.8 %collective-permute-done.1 = f32[16,1]{1,0:T(8,128)S(1)} collective-permute-done((f32[16,1]{1,0:T(8,128)S(1)}, f32[16,1]{1,0:T(8,128)S(1)}, u32[]{:S(2)}, u32[]{:S(2)}) %collective-permute-start.1) | collective-permute-done | bytes 96 | tf_op jit(solution)/shard_map/ppermute | solution.py:24
  180.8 17.4 %all_to_all.52 = bf16[16,2,1024]{2,1,0:T(2,128)(2,1)S(1)} all-to-all(bf16[16,2,1024]{2,1,0:T(2,128)(2,1)S(1)} %reshape.387), channel_id=1, replica_groups=mesh['rad'=16,'ma'=32] {'rad'}, dimensions={0} | all-to-all | bytes 131072 | tf_op jit(solution)/shard_map/all_to_all | solution.py:40
  200.1 6.2 %all-to-all-start.6 = ((bf16[32,2,16,1024]{3,2,1,0:T(8,128)(2,1)}), bf16[32,2,16,1024]{3,2,1,0:T(8,128)(2,1)}, u32[]{:S(2)}, u32[]{:S(2)}) async-start(bf16[32,2,16,1024]{3,2,1,0:T(8,128)(2,1)} %broadcast_in_dim.47), calls=%async_computation.6 | async-start | bytes 4194304 | tf_op jit(solution)/shard_map/all_to_all | solution.py:40
  206.3 48.1 %all-to-all-done.6 = bf16[32,2,16,1024]{3,2,1,0:T(8,128)(2,1)} async-done(((bf16[32,2,16,1024]{3,2,1,0:T(8,128)(2,1)}), bf16[32,2,16,1024]{3,2,1,0:T(8,128)(2,1)}, u32[]{:S(2)}, u32[]{:S(2)}) %all-to-all-start.6) | async-done | bytes 2097184 | tf_op jit(solution)/shard_map/all_to_all | solution.py:40
  254.4 1.8 copy.42
  (67 shorter events, 14.1 us)
Async XLA Ops:
  0.6 1.4 copy-start
  18.6 16.4 %copy-start.2 = (s32[512]{0:T(512)S(1)}, s32[512]{0:T(512)}, u32[]{:S(2)}) copy-start(s32[512]{0:T(512)} %param.9) | copy-start | bytes 6148
  18.6 55.1 %all-to-all-start.1 = ((f32[16,32,768]{2,1,0:T(8,128)}), f32[16,32,768]{2,1,0:T(8,128)S(1)}, u32[]{:S(2)}, u32[]{:S(2)}) async-start(f32[16,32,768]{2,1,0:T(8,128)} %copy.35), calls=%async_computation.1 | async-start | bytes 3145728 | tf_op jit(solution)/shard_map/all_to_all | solution.py:54
  75.7 24.9 %all-to-all-start.2 = ((bf16[32,2,384]{2,1,0:T(2,128)(2,1)}), bf16[32,2,384]{2,1,0:T(2,128)(2,1)S(1)}, u32[]{:S(2)}, u32[]{:S(2)}) async-start(bf16[32,2,384]{2,1,0:T(2,128)(2,1)} %reshape.381), calls=%async_computation.2 | async-start | bytes 98304 | tf_op jit(solution)/shard_map/all_to_all | solution.py:115
  89.4 11.2 %copy-start.3 = (s32[1,12]{1,0:T(1,128)S(1)}, s32[1,12]{1,0:T(1,128)}, u32[]{:S(2)}) copy-start(s32[1,12]{1,0:T(1,128)} %param.10) | copy-start | bytes 148
  101.2 23.0 %all-to-all-start = ((s32[16,1,12]{2,1,0:T(1,128)}), s32[16,1,12]{2,1,0:T(1,128)S(1)}, u32[]{:S(2)}, u32[]{:S(2)}) async-start(s32[16,1,12]{2,1,0:T(1,128)} %broadcast_in_dim.24), calls=%async_computation | async-start | bytes 16384 | tf_op jit(solution)/shard_map/all_to_all | solution.py:40
  113.3 2.9 %copy-start.4 = (f32[1,12]{1,0:T(1,128)S(1)}, f32[1,12]{1,0:T(1,128)}, u32[]{:S(2)}) copy-start(f32[1,12]{1,0:T(1,128)} %param.11) | copy-start | bytes 148
  124.2 15.5 %all-to-all-start.3 = ((f32[16,1,768]{2,1,0:T(1,128)}), f32[16,1,768]{2,1,0:T(1,128)S(1)}, u32[]{:S(2)}, u32[]{:S(2)}) async-start(f32[16,1,768]{2,1,0:T(1,128)} %reshape.383), calls=%async_computation.3 | async-start | bytes 98304 | tf_op jit(solution)/shard_map/all_to_all | solution.py:128
  142.4 18.2 %all-to-all-start.4 = ((f32[32,1,1024]{2,1,0:T(1,128)}), f32[32,1,1024]{2,1,0:T(1,128)S(1)}, u32[]{:S(2)}, u32[]{:S(2)}) async-start(f32[32,1,1024]{2,1,0:T(1,128)} %reshape.385), calls=%async_computation.4 | async-start | bytes 262144 | tf_op jit(solution)/shard_map/all_to_all | solution.py:54
  161.8 38.4 %copy-start.1 = (f32[16,64]{1,0:T(8,128)}, f32[16,64]{1,0:T(8,128)S(1)}, u32[]{:S(2)}) copy-start(f32[16,64]{1,0:T(8,128)S(1)} %reduce_sum.19) | copy-start | bytes 12292
  161.8 10.9 %collective-permute-start = (f32[16,1]{1,0:T(8,128)S(1)}, f32[16,1]{1,0:T(8,128)S(1)}, u32[]{:S(2)}, u32[]{:S(2)}) collective-permute-start(f32[16,1]{1,0:T(8,128)S(1)} %get-tuple-element.20), channel_id=1, source_target_pairs={{32,0},{64,32},{96,64},{128,96},{160,128},{192,160},{224,192},{256... | collective-permute-start | bytes 200 | tf_op jit(solution)/shard_map/ppermute | solution.py:27
  164.5 16.1 %collective-permute-start.2 = (f32[1,64]{1,0:T(1,128)S(1)}, f32[1,64]{1,0:T(1,128)S(1)}, u32[]{:S(2)}, u32[]{:S(2)}) collective-permute-start(f32[1,64]{1,0:T(1,128)S(1)} %get-tuple-element.22), channel_id=1, source_target_pairs={{1,0},{2,1},{3,2},{4,3},{5,4},{6,5},{7,6},{8,7},{9,8},{10,9},{11,1... | collective-permute-start | bytes 776 | tf_op jit(solution)/shard_map/ppermute | solution.py:27
  166.9 13.6 %collective-permute-start.3 = (f32[1,64]{1,0:T(1,128)S(1)}, f32[1,64]{1,0:T(1,128)S(1)}, u32[]{:S(2)}, u32[]{:S(2)}) collective-permute-start(f32[1,64]{1,0:T(1,128)S(1)} %get-tuple-element.23), channel_id=1, source_target_pairs={{0,1},{1,2},{2,3},{3,4},{4,5},{5,6},{6,7},{7,8},{8,9},{9,10},{10,1... | collective-permute-start | bytes 776 | tf_op jit(solution)/shard_map/ppermute | solution.py:24
  170.0 10.5 %collective-permute-start.1 = (f32[16,1]{1,0:T(8,128)S(1)}, f32[16,1]{1,0:T(8,128)S(1)}, u32[]{:S(2)}, u32[]{:S(2)}) collective-permute-start(f32[16,1]{1,0:T(8,128)S(1)} %get-tuple-element.21), channel_id=1, source_target_pairs={{0,32},{32,64},{64,96},{96,128},{128,160},{160,192},{192,224},{224... | collective-permute-start | bytes 200 | tf_op jit(solution)/shard_map/ppermute | solution.py:24
  200.1 54.3 %all-to-all-start.6 = ((bf16[32,2,16,1024]{3,2,1,0:T(8,128)(2,1)}), bf16[32,2,16,1024]{3,2,1,0:T(8,128)(2,1)}, u32[]{:S(2)}, u32[]{:S(2)}) async-start(bf16[32,2,16,1024]{3,2,1,0:T(8,128)(2,1)} %broadcast_in_dim.47), calls=%async_computation.6 | async-start | bytes 4194304 | tf_op jit(solution)/shard_map/all_to_all | solution.py:40
where the time goes:
time: 258 us; the launch traced here: 257 us
  waiting for transfers between devices  120 us (47%)
  starting transfers between devices  72.9 us (28%)
  local copies, waits for them, and re-layouts  23.8 us (9%)
  blocking collectives  17.4 us (7%)
  other arithmetic  14.7 us (6%)
  matrix products  7.72 us (3%)
    all_to_all x2, waiting for transfers between devices, sent_to_all(): return lax.all_to_all(copies, axis, split_axis=0, concat_axis=0, tiled=True)  55.3 us
    all_to_all x2, waiting for transfers between devices, summed_on_arrival(): lax.all_to_all(blocks, axis, split_axis=0, concat_axis=0, tiled=True)  46.8 us
    all_to_all x2, starting transfers between devices, summed_on_arrival(): lax.all_to_all(blocks, axis, split_axis=0, concat_axis=0, tiled=True)  26.1 us
    all_to_all x2, starting transfers between devices, sent_to_all(): return lax.all_to_all(copies, axis, split_axis=0, concat_axis=0, tiled=True)  18 us
    all_to_all x1, blocking collectives, sent_to_all(): return lax.all_to_all(copies, axis, split_axis=0, concat_axis=0, tiled=True)  17.4 us
    all_to_all x1, starting transfers between devices, on_device(): lax.all_to_all(latitudes, 'ma', split_axis=0, concat_axis=1, tiled=True)  13.7 us
    another operation x1, other arithmetic  11.2 us
    all_to_all x1, waiting for transfers between devices, on_device(): lax.all_to_all(weighted, 'rad', split_axis=1, concat_axis=0, tiled=True)  9.98 us
  transfers between devices with their start and end apart: 10, of which 6 were waited for; matrix products, arithmetic and copies ran while one was open for 7% of the time, Pallas kernels for 0%

commit v1 on v0

v1 whole, which is shorter than its diff:
```python
import math

import jax
import jax.numpy as jnp
from jax import lax
from jax.sharding import PartitionSpec as P

NPHI = 1024
NS = 512
TIME_STEP = 0.05
COMPOSITION_WEIGHT = 0.8
BF16 = jnp.bfloat16
F32 = jnp.float32


def exchanged(blocks, axis):
    return lax.all_to_all(blocks, axis, split_axis=0, concat_axis=0, tiled=True)


def to_all(value, axis):
    return exchanged(jnp.broadcast_to(value, (lax.axis_size(axis), *value.shape)), axis)


def value_table(orders):
    longitude = jnp.arange(NPHI, dtype=jnp.int32)
    phase_index = orders[:, None] * longitude[None, :] % NPHI
    angles = phase_index.astype(F32) * (2.0 * math.pi / NPHI)
    weights = jnp.where(orders == 0, 1.0, 2.0).astype(F32) / math.sqrt(NS)
    return (
        (jnp.cos(angles) * weights[:, None]).astype(BF16),
        (-jnp.sin(angles) * weights[:, None]).astype(BF16),
    )


def on_device(spectrum, radial_table, legendre, order_table, cylinder_row, column_weight):
    slots, degrees = spectrum.shape[1:3]
    levels_n = radial_table.shape[0]
    lats = legendre.shape[2]
    n_rad = lax.axis_size("rad")
    n_ma = lax.axis_size("ma")
    lat_block = lats // n_rad
    row_block = NS // n_ma
    lon_block = NPHI // n_rad
    me_rad = lax.axis_index("rad")
    me_ma = lax.axis_index("ma")

    with jax.named_scope("contribute"):
        my_orders = lax.dynamic_slice_in_dim(order_table, me_ma * slots, slots)
        my_degrees = me_rad * degrees + jnp.arange(degrees, dtype=jnp.int32)
        allowed = my_degrees[None, :] >= my_orders[:, None]
        masked = jnp.where(allowed[:, :, None], legendre, jnp.zeros_like(legendre))
        levels = jnp.einsum(
            "rn,ckln->rckl", radial_table, spectrum, preferred_element_type=F32
        ).astype(BF16)
        contribution = jnp.einsum("klt,rckl->trck", masked, levels, preferred_element_type=F32)
        contribution = contribution.astype(BF16).reshape(n_rad, lat_block, levels_n * 4 * slots)
    with jax.named_scope("sum_degrees"):
        arrived = exchanged(contribution, "rad")
    with jax.named_scope("points"):
        info = jnp.concatenate([cylinder_row.astype(F32), column_weight], axis=1)
        infos = to_all(info, "ma").reshape(lat_block, 2 * levels_n)
        rows = infos[:, :levels_n].astype(jnp.int32).reshape(-1)
        weights = infos[:, levels_n:]
    with jax.named_scope("tables"):
        cosines, sines = value_table(order_table)
        table = jnp.stack(
            [cosines.reshape(n_ma, slots, NPHI), sines.reshape(n_ma, slots, NPHI)], axis=1
        )
    with jax.named_scope("latitudes"):
        latitudes = arrived.astype(F32).sum(axis=0).astype(BF16)
    with jax.named_scope("spread_orders"):
        received = exchanged(latitudes.reshape(n_ma, 1, -1), "ma")
    row_ids = jnp.arange(NS, dtype=jnp.int32)
    with jax.named_scope("columns"):
        lat32 = latitudes.astype(F32).reshape(lat_block, levels_n, 2, 2 * slots)
        weighted = (lat32[:, :, 0] - COMPOSITION_WEIGHT * lat32[:, :, 1]) * weights[:, :, None]
        onehot = (rows[:, None] == row_ids[None, :]).astype(F32)
        partial = jnp.einsum(
            "pq,ps->qs",
            weighted.reshape(-1, 2 * slots),
            onehot,
            precision=lax.Precision.HIGHEST,
            preferred_element_type=F32,
        )
    with jax.named_scope("sum_columns"):
        parts = to_all(partial.astype(BF16), "rad").reshape(n_rad, 2 * slots, NS)
        column = parts.astype(F32).sum(axis=0)
    with jax.named_scope("select"):
        step = jnp.sin(my_orders.astype(F32) * (2.0 * math.pi / NPHI))[:, None] * 2.0
        by_part = column.reshape(2, slots, NS)
        outward_hat = jnp.concatenate([-step * by_part[1], step * by_part[0]], axis=0)
        padded = jnp.pad(column, ((0, 0), (1, 1)))
        around_hat = padded[:, 2:] - padded[:, :-2]
        wanted = jnp.concatenate([outward_hat, around_hat, column], axis=0).astype(BF16)
        owned_rows = row_ids.reshape(n_ma, row_block)
        nothing = jnp.full((n_ma, row_block - levels_n), -1, jnp.int32)
        picks = jnp.concatenate([rows.reshape(n_ma, levels_n), nothing, owned_rows], axis=1)
        chooser = (picks.reshape(-1)[:, None] == row_ids[None, :]).astype(BF16)
        chosen = jnp.einsum("ps,qs->pq", chooser, wanted, preferred_element_type=F32).astype(BF16)
    with jax.named_scope("spread_columns"):
        got = exchanged(chosen.reshape(n_ma, 2 * row_block, 6 * slots), "ma")
    with jax.named_scope("synthesis"):
        coefs = received.reshape(n_ma, levels_n, 2, 2, slots)
        slope_scale = (order_table.astype(F32) / NS).reshape(n_ma, 1, 1, slots)
        c32 = coefs.astype(F32)
        slope_coefs = jnp.stack(
            [-c32[:, :, :, 1] * slope_scale, c32[:, :, :, 0] * slope_scale], axis=3
        ).astype(BF16)
        both = jnp.stack([coefs, slope_coefs], axis=1)
        grids = jnp.einsum("bgrfik,bikj->gfrj", both, table, preferred_element_type=F32)
        grids = grids.astype(BF16).astype(F32)
        fields, slope_field = grids[0], grids[1]
    with jax.named_scope("velocity"):
        got = got.reshape(n_ma, 2 * row_block, 3, 2, slots)
        synth = jnp.einsum("bpgik,bikj->gpj", got, table, preferred_element_type=F32)
        outward_diff = synth[0, :levels_n]
        around_diff = synth[1, :levels_n]
        owned = lax.dynamic_slice_in_dim(synth[2, row_block:], me_rad * lon_block, lon_block, axis=1)
    with jax.named_scope("advect"):
        radius = (0.35 + 0.65 * (cylinder_row.astype(F32) + 0.5) / NS).reshape(levels_n, 1)
        outward = outward_diff / (2.0 * radius)
        around = -0.5 * around_diff
        advected = fields - (TIME_STEP / radius) * (around * slope_field + outward * fields)
    return (owned, advected[:, None])


def solution(mesh):
    return jax.shard_map(
        on_device,
        mesh=mesh,
        in_specs=(
            P(None, "ma", "rad", None),
            P(),
            P("ma", "rad", None),
            P(),
            P(("rad", "ma"), None),
            P(("rad", "ma"), None),
        ),
        out_specs=(P("ma", "rad"), P(None, ("rad", "ma"), None, None)),
        check_vma=False,
    )
```

time: 258 us -> 132 us (0.51)
  waiting for transfers between devices: 120 us -> 37.1 us
  starting transfers between devices: 72.9 us -> 51.8 us
  blocking collectives: 17.4 us -> 0 us
  local copies, waits for them, and re-layouts: 23.8 us -> 17.8 us
    all_to_all x6 -> x5, waiting for transfers between devices: 112 us -> 37.1 us  [exchanged(): return lax.all_to_all(blocks, axis, split_axis=0, concat_axis=0, tiled=True)]
    all_to_all x1 -> x0, blocking collectives: 17.4 us -> none  [sent_to_all(): return lax.all_to_all(copies, axis, split_axis=0, concat_axis=0, tiled=True)]
    ppermute x4 -> x0, starting transfers between devices: 10.8 us -> none  [the longest x2 5.75 us: padded(): lax.ppermute(lax.slice_in_dim(block, block.shape[dim] - width, None, axis...]
    all_to_all x6 -> x5, starting transfers between devices: 62 us -> 51.8 us  [exchanged(): return lax.all_to_all(blocks, axis, split_axis=0, concat_axis=0, tiled=True)]
    another operation x3, other arithmetic: 11.3 us -> 1.08 us
    convert_element_type x2, other arithmetic: 0.67 us -> 10.7 us  [the longest x1 9.89 us: value_table(): (jnp.cos(angles) * weights[:, None]).astype(BF16)]
    another operation x2 -> x0, local copies, waits for them, and re-layouts: 9.89 us -> none  [in_blocks(): return jnp.moveaxis(value.reshape(*before, devices, -1, *after), dim, 0)]
    reshape x1 -> x4, local copies, waits for them, and re-layouts: 0.14 us -> 9.28 us  [the longest x2 7.92 us: on_device(): contribution.astype(BF16).reshape(n_rad, lat_block, levels_n * 4 * slots)]
  transfers between devices with their start and end apart: 10 -> 5, of which waited for: 6 -> 4; matrix products, arithmetic and copies ran while one was open for 7% -> 22% of each run, Pallas kernels for 0% -> 0%
where the time goes in v1:
time: 132 us; the launch traced here: 131 us
  starting transfers between devices  51.8 us (39%)
  waiting for transfers between devices  37.1 us (28%)
  local copies, waits for them, and re-layouts  17.8 us (13%)
  other arithmetic  15.7 us (12%)
  matrix products  7.79 us (6%)
    all_to_all x5, starting transfers between devices, exchanged(): return lax.all_to_all(blocks, axis, split_axis=0, concat_axis=0, tiled=True)  51.8 us
    all_to_all x5, waiting for transfers between devices, exchanged(): return lax.all_to_all(blocks, axis, split_axis=0, concat_axis=0, tiled=True)  37.1 us
    convert_element_type x1, other arithmetic, value_table(): (jnp.cos(angles) * weights[:, None]).astype(BF16)  9.89 us
    reshape x2, local copies, waits for them, and re-layouts, on_device(): contribution.astype(BF16).reshape(n_rad, lat_block, levels_n * 4 * slots)  7.92 us
    dot_general x1, matrix products, on_device(): jnp.einsum('klt,rckl->trck', masked, levels, preferred_element_type=F32)  2.83 us
  transfers between devices with their start and end apart: 5, of which 4 were waited for; matrix products, arithmetic and copies ran while one was open for 22% of the time, Pallas kernels for 0%

profile of v1, /device:TPU:1, one launch (start us, length us, event | category | flops | bytes accessed | tf_op | source)
XLA Modules:
  0.0 131.0 jit_solution(8604897968284347553)
XLA Ops:
  0.6 0.8 convert_element_type.106
  1.4 0.7 maximum_bitcast_fusion
  2.8 10.3 %all-to-all-start = ((f32[32,1,24]{2,1,0:T(1,128)}), f32[32,1,24]{2,1,0:T(1,128)S(1)}, u32[]{:S(2)}, u32[]{:S(2)}) async-start(f32[32,1,24]{2,1,0:T(1,128)} %broadcast_in_dim.26), calls=%async_computation | async-start | bytes 32768 | tf_op jit(solution)/shard_map/points/all_to_all | solution.py:17
  13.1 0.8 fusion.78
  14.0 2.8 %fusion.13 = bf16[512,12,4,16]{0,1,2,3:T(8,128)(2,1)S(1)} fusion(bf16[4,16,32,384]{3,2,1,0:T(8,128)(2,1)S(1)} %copy-done, bf16[16,32,512]{2,1,0:T(8,128)(2,1)} %param.8, pred[16,32]{1,0:T(8,128)(4,1)S(1)} %broadcast_compare_fusion, bf16[12,384]{1,0:T(8,128)(2,1)} %param.7), kind=kOutput, calls=%fused_computation.21 | convolution fusion | flops 44720128 | bytes 2893312 | tf_op jit(solution)/shard_map/contribute/klt,rckl->trck/dot_general | solution.py:55
  17.3 3.1 %reshape.293 = bf16[16,32,768]{1,0,2:T(8,128)(2,1)} reshape(bf16[512,12,4,16]{0,3,2,1:T(8,128)(2,1)S(1)} %copy.90) | data formatting | bytes 1572864 | tf_op jit(solution)/shard_map/contribute/reshape | solution.py:56
  20.4 4.8 %copy.91 = bf16[16,32,768]{2,1,0:T(8,128)(2,1)} copy(bf16[16,32,768]{1,0,2:T(8,128)(2,1)} %reshape.293) | data formatting | bytes 1572864 | tf_op jit(solution)/shard_map/contribute/reshape | solution.py:56
  25.2 11.4 %all-to-all-start.1 = ((bf16[16,32,768]{2,1,0:T(8,128)(2,1)}), bf16[16,32,768]{2,1,0:T(8,128)(2,1)S(1)}, u32[]{:S(2)}, u32[]{:S(2)}) async-start(bf16[16,32,768]{2,1,0:T(8,128)(2,1)} %copy.91), calls=%async_computation.1 | async-start | bytes 1572864 | tf_op jit(solution)/shard_map/sum_degrees/all_to_all | solution.py:17
  37.4 17.7 %all-to-all-done.1 = bf16[16,32,768]{2,1,0:T(8,128)(2,1)S(1)} async-done(((bf16[16,32,768]{2,1,0:T(8,128)(2,1)}), bf16[16,32,768]{2,1,0:T(8,128)(2,1)S(1)}, u32[]{:S(2)}, u32[]{:S(2)}) %all-to-all-start.1) | async-done | bytes 786464 | tf_op jit(solution)/shard_map/sum_degrees/all_to_all | solution.py:17
  57.8 16.4 %all-to-all-start.4 = ((bf16[32,2,384]{2,1,0:T(2,128)(2,1)}), bf16[32,2,384]{2,1,0:T(2,128)(2,1)S(1)}, u32[]{:S(2)}, u32[]{:S(2)}) async-start(bf16[32,2,384]{2,1,0:T(2,128)(2,1)} %reshape.309), calls=%async_computation.4 | async-start | bytes 98304 | tf_op jit(solution)/shard_map/spread_orders/all_to_all | solution.py:17
  74.6 7.2 %all-to-all-done.4 = bf16[32,2,384]{2,1,0:T(2,128)(2,1)S(1)} async-done(((bf16[32,2,384]{2,1,0:T(2,128)(2,1)}), bf16[32,2,384]{2,1,0:T(2,128)(2,1)S(1)}, u32[]{:S(2)}, u32[]{:S(2)}) %all-to-all-start.4) | async-done | bytes 49184 | tf_op jit(solution)/shard_map/spread_orders/all_to_all | solution.py:17
  81.8 0.9 broadcast_in_dim.49
  82.7 5.5 %all-to-all-start.2 = ((bf16[16,32,512]{2,1,0:T(8,128)(2,1)}), bf16[16,32,512]{2,1,0:T(8,128)(2,1)S(1)}, u32[]{:S(2)}, u32[]{:S(2)}) async-start(bf16[16,32,512]{2,1,0:T(8,128)(2,1)} %broadcast_in_dim.49), calls=%async_computation.2 | async-start | bytes 1048576 | tf_op jit(solution)/shard_map/sum_columns/all_to_all | solution.py:17
  89.3 9.9 %multiply_convert_fusion.1 = (bf16[32,1,16,1024]{3,0,2,1:T(8,128)(2,1)S(1)}, bf16[32,1,16,1024]{3,0,2,1:T(8,128)(2,1)}) fusion(f32[32,16]{0,1:T(8,128)S(1)} %copy.88, s32[32,16]{0,1:T(8,128)S(1)} %copy.87), kind=kLoop, calls=%fused_computation.13 | loop fusion | flops 9961472 | bytes 2101248 | tf_op jit(solution)/shard_map/tables/convert_element_type | solution.py:30
  99.6 0.8 copy.104
  101.1 3.2 %all-to-all-done.2 = bf16[16,32,512]{2,1,0:T(8,128)(2,1)S(1)} async-done(((bf16[16,32,512]{2,1,0:T(8,128)(2,1)}), bf16[16,32,512]{2,1,0:T(8,128)(2,1)S(1)}, u32[]{:S(2)}, u32[]{:S(2)}) %all-to-all-start.2) | async-done | bytes 524320 | tf_op jit(solution)/shard_map/sum_columns/all_to_all | solution.py:17
  104.6 0.7 fusion.71
  106.0 0.9 copy.94
  106.8 8.2 %all-to-all-start.3 = ((bf16[32,32,96]{2,1,0:T(8,128)(2,1)}), bf16[32,32,96]{2,1,0:T(8,128)(2,1)S(1)}, u32[]{:S(2)}, u32[]{:S(2)}) async-start(bf16[32,32,96]{2,1,0:T(8,128)(2,1)} %bitcast.8), calls=%async_computation.3 | async-start | bytes 524288 | tf_op jit(solution)/shard_map/spread_columns/all_to_all | solution.py:17
  115.3 1.8 %fusion.32 = f32[2,2,12,1024]{3,2,1,0:T(8,128)S(1)} fusion(bf16[32,1,16,1024]{3,0,2,1:T(8,128)(2,1)} %get-tuple-element.31, bf16[32,1,16,1024]{3,0,2,1:T(8,128)(2,1)S(1)} %get-tuple-element.30, bf16[32,1,12,2,1,16]{0,2,5,4,3,1:T(8,128)(2,1)S(1)} %get-tuple-element.33, bf16[32,1,12,2,1,16]{0,2,5,4,3,1:T(8,128)(2,1)S(1)} %get-tuple-element.32, ...), kind=kOutput, calls=%fused_computation.28 | convolution fusion | flops 105250816 | bytes 2392064 | tf_op jit(solution)/shard_map/synthesis/bgrfik,bikj->gfrj/dot_general | solution.py:110
  117.1 9.0 %all-to-all-done.3 = bf16[32,32,96]{2,1,0:T(8,128)(2,1)S(1)} async-done(((bf16[32,32,96]{2,1,0:T(8,128)(2,1)}), bf16[32,32,96]{2,1,0:T(8,128)(2,1)S(1)}, u32[]{:S(2)}, u32[]{:S(2)}) %all-to-all-start.3) | async-done | bytes 196640 | tf_op jit(solution)/shard_map/spread_columns/all_to_all | solution.py:17
  126.1 1.2 copy.95
  127.3 2.1 %fusion.17 = f32[3,32,1024]{2,1,0:T(8,128)S(1)} fusion(bf16[32,1,16,1024]{3,0,2,1:T(8,128)(2,1)} %get-tuple-element.31, bf16[32,1,16,1024]{3,0,2,1:T(8,128)(2,1)S(1)} %get-tuple-element.30, bf16[32,32,3,2,16]{1,4,3,2,0:T(8,128)(2,1)} %bitcast.96), kind=kOutput, calls=%fused_computation.23 | convolution fusion | flops 205520896 | bytes 2686976 | tf_op jit(solution)/shard_map/velocity/bpgik,bikj->gpj/dot_general | solution.py:115
  129.6 0.7 copy.105
  (56 shorter events, 9.2 us)
Async XLA Ops:
  0.6 13.4 %copy-start = (bf16[4,16,32,384]{3,2,1,0:T(8,128)(2,1)S(1)}, bf16[4,16,32,384]{3,2,1,0:T(8,128)(2,1)}, u32[]{:S(2)}) copy-start(bf16[4,16,32,384]{3,2,1,0:T(8,128)(2,1)} %param.6) | copy-start | bytes 4718596
  2.8 22.4 %all-to-all-start = ((f32[32,1,24]{2,1,0:T(1,128)}), f32[32,1,24]{2,1,0:T(1,128)S(1)}, u32[]{:S(2)}, u32[]{:S(2)}) async-start(f32[32,1,24]{2,1,0:T(1,128)} %broadcast_in_dim.26), calls=%async_computation | async-start | bytes 32768 | tf_op jit(solution)/shard_map/points/all_to_all | solution.py:17
  20.4 16.2 %copy-start.6 = (s32[1,12]{1,0:T(1,128)S(1)}, s32[1,12]{1,0:T(1,128)}, u32[]{:S(2)}) copy-start(s32[1,12]{1,0:T(1,128)} %param.10) | copy-start | bytes 148
  20.4 16.7 %copy-start.3 = (s32[512]{0:T(512)S(1)}, s32[512]{0:T(512)}, u32[]{:S(2)}) copy-start(s32[512]{0:T(512)} %param.9) | copy-start | bytes 6148
  25.2 29.9 %all-to-all-start.1 = ((bf16[16,32,768]{2,1,0:T(8,128)(2,1)}), bf16[16,32,768]{2,1,0:T(8,128)(2,1)S(1)}, u32[]{:S(2)}, u32[]{:S(2)}) async-start(bf16[16,32,768]{2,1,0:T(8,128)(2,1)} %copy.91), calls=%async_computation.1 | async-start | bytes 1572864 | tf_op jit(solution)/shard_map/sum_degrees/all_to_all | solution.py:17
  57.8 24.1 %all-to-all-start.4 = ((bf16[32,2,384]{2,1,0:T(2,128)(2,1)}), bf16[32,2,384]{2,1,0:T(2,128)(2,1)S(1)}, u32[]{:S(2)}, u32[]{:S(2)}) async-start(bf16[32,2,384]{2,1,0:T(2,128)(2,1)} %reshape.309), calls=%async_computation.4 | async-start | bytes 98304 | tf_op jit(solution)/shard_map/spread_orders/all_to_all | solution.py:17
  82.7 21.7 %all-to-all-start.2 = ((bf16[16,32,512]{2,1,0:T(8,128)(2,1)}), bf16[16,32,512]{2,1,0:T(8,128)(2,1)S(1)}, u32[]{:S(2)}, u32[]{:S(2)}) async-start(bf16[16,32,512]{2,1,0:T(8,128)(2,1)} %broadcast_in_dim.49), calls=%async_computation.2 | async-start | bytes 1048576 | tf_op jit(solution)/shard_map/sum_columns/all_to_all | solution.py:17
  101.1 13.9 %copy-start.1 = (f32[32,12,2,1,16]{0,4,3,2,1:T(8,128)S(1)}, f32[32,12,2,1,16]{0,4,3,2,1:T(8,128)}, u32[]{:S(2)}) copy-start(f32[32,12,2,1,16]{0,4,3,2,1:T(8,128)} %get-tuple-element.23) | copy-start | bytes 147460
  104.5 10.8 %copy-start.2 = (bf16[32,1,12,2,2,16]{0,2,5,4,3,1:T(8,128)(2,1)S(1)}, bf16[32,1,12,2,2,16]{0,2,5,4,3,1:T(8,128)(2,1)}, u32[]{:S(2)}) copy-start(bf16[32,1,12,2,2,16]{0,2,5,4,3,1:T(8,128)(2,1)} %copy.104) | copy-start | bytes 147460
  106.8 19.3 %all-to-all-start.3 = ((bf16[32,32,96]{2,1,0:T(8,128)(2,1)}), bf16[32,32,96]{2,1,0:T(8,128)(2,1)S(1)}, u32[]{:S(2)}, u32[]{:S(2)}) async-start(bf16[32,32,96]{2,1,0:T(8,128)(2,1)} %bitcast.8), calls=%async_computation.3 | async-start | bytes 524288 | tf_op jit(solution)/shard_map/spread_columns/all_to_all | solution.py:17
  127.3 2.1 %copy-start.5 = (f32[12]{0:T(128)S(1)}, f32[12]{0:T(128)}, u32[]{:S(2)}) copy-start(f32[12]{0:T(128)} %get-tuple-element.37) | copy-start | bytes 148
  127.3 2.2 %copy-start.4 = (f32[12]{0:T(128)S(1)}, f32[12]{0:T(128)}, u32[]{:S(2)}) copy-start(f32[12]{0:T(128)} %get-tuple-element.36) | copy-start | bytes 148

commit v2 on v1

v2 whole, which is shorter than its diff:
```python
import functools
import math

import jax
import jax.numpy as jnp
from jax import lax
from jax.experimental import pallas as pl
from jax.experimental.pallas import tpu as pltpu
from jax.sharding import PartitionSpec as P

NPHI = 1024
NS = 512
LANES = 128
TIME_STEP = 0.05
COMPOSITION_WEIGHT = 0.8
BF16 = jnp.bfloat16
F32 = jnp.float32
I32 = jnp.int32

dot = functools.partial(jnp.dot, preferred_element_type=F32)


def iota(shape, dim):
    return lax.broadcasted_iota(I32, shape, dim)


def dot_dims(x, y, dim_x, dim_y):
    return lax.dot_general(x, y, (((dim_x,), (dim_y,)), ((), ())), preferred_element_type=F32)


def vmem_call(body, outs, n_smem, n_vmem):
    return pl.pallas_call(
        body,
        out_shape=outs,
        in_specs=[pl.BlockSpec(memory_space=pltpu.SMEM)] * n_smem
        + [pl.BlockSpec(memory_space=pltpu.VMEM)] * n_vmem,
        out_specs=jax.tree.map(lambda _: pl.BlockSpec(memory_space=pltpu.VMEM), outs),
    )


def contribution_kernel(slots, degrees, orders, first, radial, spectrum, legendre, out):
    parts = spectrum.shape[0]
    levels_n = radial.shape[0]
    columns = levels_n * parts
    width = columns * slots
    rows = slots * degrees
    repeat = (iota((columns, levels_n), 0) // parts == iota((columns, levels_n), 1)).astype(BF16)
    repeated = dot(repeat, radial[...])
    part_of = iota(repeated.shape, 0) % parts
    levels = jnp.zeros((rows, columns), F32)
    for c in range(parts):
        table = jnp.where(part_of == c, repeated, 0.0).astype(BF16)
        levels += dot_dims(spectrum[c], table, 1, 1)
    spread = (iota((columns, width), 0) == iota((columns, width), 1) // slots).astype(BF16)
    expanded = dot(levels.astype(BF16), spread)
    slot_of_lane = iota((degrees, width), 1) % slots
    degree = iota((degrees, width), 0) + first[0]
    blocks = []
    for k in range(slots):
        kept = (slot_of_lane == k) & (degree >= orders[k])
        blocks.append(jnp.where(kept, expanded[k * degrees : (k + 1) * degrees], 0.0).astype(BF16))
    diagonal = jnp.concatenate(blocks, axis=0)
    total = dot_dims(legendre[...], diagonal, 0, 0)
    out[...] = total.astype(BF16).reshape(out.shape)


def column_kernel(arrived, weights, onehot, copies, stacked):
    levels_n = weights.shape[1]
    width = arrived.shape[2] // levels_n
    total = arrived[0].astype(F32)
    for d in range(1, arrived.shape[0]):
        total += arrived[d].astype(F32)
    points = jnp.concatenate(
        [total[:, r * width : (r + 1) * width] for r in range(levels_n)], axis=0
    ).astype(BF16)
    stacked[...] = jnp.concatenate([jnp.zeros_like(points), points], axis=1)
    half = width // 2
    exact = points.astype(F32)
    buoyancy = exact[:, :half] - COMPOSITION_WEIGHT * exact[:, half:]
    weight = jnp.concatenate([weights[:, r : r + 1] for r in range(levels_n)], axis=0)
    weighted = buoyancy * weight
    high = weighted.astype(BF16)
    low = (weighted - high.astype(F32)).astype(BF16)
    both = dot_dims(jnp.concatenate([high, low], axis=1), onehot[...], 0, 0)
    column = (both[:half] + both[half:]).astype(BF16)
    copies[...] = jnp.broadcast_to(column[None], copies.shape)


def select_kernel(parts, step, chooser, stacked, out):
    column = parts[0].astype(F32)
    for d in range(1, parts.shape[0]):
        column += parts[d].astype(F32)
    half = column.shape[0] // 2
    outward = step[...] * jnp.concatenate([column[half:], column[:half]], axis=0)
    at = iota(column.shape, 1)
    after = jnp.where(at == NS - 1, 0.0, pltpu.roll(column, NS - 1, axis=1))
    before = jnp.where(at == 0, 0.0, pltpu.roll(column, 1, axis=1))
    around = after - before
    zeros = jnp.zeros_like(column)
    points = jnp.concatenate([outward, around, zeros, zeros], axis=0).astype(BF16)
    group = at // 4 % 4
    rows = jnp.concatenate([jnp.where(group == g, column, 0.0) for g in range(4)], axis=0)
    chosen = dot_dims(chooser[:, :NS], points, 1, 1)
    chosen += dot_dims(chooser[:, NS : 2 * NS], rows.astype(BF16), 1, 1)
    chosen += dot(chooser[:, 2 * NS :], stacked[...])
    out[...] = chosen.astype(BF16).reshape(out.shape)


def advect_kernel(levels_n, slots, block, got, cosines, sines, slope, radius, owned, advected):
    n_ma, per, _ = got.shape
    taken = [got[b] for b in range(n_ma)]
    by_part = []
    for i in range(2):
        groups = []
        for g in range(4):
            at = (2 * g + i) * slots
            groups.append(jnp.concatenate([x[:, at : at + slots] for x in taken], axis=1))
        by_part.append(groups)
    scale = slope[...]
    sides = []
    for i in range(2):
        turned = [
            (by_part[1 - i][g].astype(F32) * (scale if i else -scale)).astype(BF16) for g in (2, 3)
        ]
        sides.append(jnp.concatenate(by_part[i] + turned, axis=0))
    result = dot(sides[0], cosines[...]) + dot(sides[1], sines[...])
    rows = [result[g * per : g * per + levels_n] for g in range(6)]
    inverse = 1.0 / radius[...]
    outward = rows[0] * (0.5 * inverse)
    around = -0.5 * rows[1]
    held = [x.astype(BF16).astype(F32) for x in rows[2:]]
    for f in range(2):
        field, side = held[f], held[2 + f]
        advected[f] = field - (TIME_STEP * inverse) * (around * side + outward * field)
    mine = jnp.concatenate([result[g * per + levels_n : (g + 1) * per] for g in range(4)], axis=0)
    width = owned.shape[1]
    mine = pltpu.roll(mine, lax.rem(NPHI - block[0], NPHI), axis=1)
    owned[...] = mine[:, :width]


def exchanged(blocks, axis):
    return lax.all_to_all(blocks, axis, split_axis=0, concat_axis=0, tiled=True)


def value_tables(orders):
    longitude = jnp.arange(NPHI, dtype=I32)
    phase_index = orders[:, None] * longitude[None, :] % NPHI
    angles = phase_index.astype(F32) * (2.0 * math.pi / NPHI)
    weights = jnp.where(orders == 0, 1.0, 2.0).astype(F32) / math.sqrt(NS)
    return (
        (jnp.cos(angles) * weights[:, None]).astype(BF16),
        (-jnp.sin(angles) * weights[:, None]).astype(BF16),
    )


def choosers(rows, n_ma, levels_n, per):
    q = jnp.arange(per, dtype=I32)[None, :, None]
    b = jnp.arange(n_ma, dtype=I32)[:, None, None]
    s = jnp.arange(NS, dtype=I32)[None, None, :]
    p = jnp.arange(levels_n * n_ma, dtype=I32)[None, None, :]
    padded = jnp.pad(rows, ((0, 0), (0, per - levels_n)), constant_values=-1)
    point = padded[:, :, None] == s
    owned = (s // per == b) & (q >= levels_n) & (s % (per - levels_n) == q - levels_n)
    latitude = (p % n_ma == b) & (p // n_ma == q)
    return jnp.concatenate([point, owned, latitude], axis=2).astype(BF16).reshape(n_ma * per, -1)


def on_device(spectrum, radial_table, legendre, order_table, cylinder_row, column_weight):
    parts, slots, degrees, modes = spectrum.shape
    levels_n = radial_table.shape[0]
    lats = legendre.shape[2]
    n_rad = lax.axis_size("rad")
    n_ma = lax.axis_size("ma")
    lat_block = lats // n_rad
    row_block = NS // n_ma
    lon_block = NPHI // n_rad
    me_rad = lax.axis_index("rad")
    me_ma = lax.axis_index("ma")
    my_orders = lax.dynamic_slice_in_dim(order_table, me_ma * slots, slots)

    info = jnp.concatenate([cylinder_row.astype(F32), column_weight], axis=1)
    infos = exchanged(jnp.broadcast_to(info, (n_ma, 1, 2 * levels_n)), "ma")
    infos = infos.reshape(n_ma, 2 * levels_n)
    rows = infos[:, :levels_n].astype(I32)
    weights = infos[:, levels_n:]
    first = (me_rad * degrees).astype(I32).reshape(1)
    contribution = vmem_call(
        functools.partial(contribution_kernel, slots, degrees),
        jax.ShapeDtypeStruct((n_rad, lat_block, levels_n * parts * slots), BF16),
        2, 3,
    )(
        my_orders,
        first,
        radial_table,
        spectrum.reshape(parts, slots * degrees, modes),
        legendre.reshape(slots * degrees, lats),
    )
    arrived = exchanged(contribution, "rad")
    cosines, sines = value_tables(order_table)
    row_ids = jnp.arange(NS, dtype=I32)
    onehot = (rows.T.reshape(-1)[:, None] == row_ids[None, :]).astype(BF16)
    chooser = choosers(rows, n_ma, levels_n, row_block)
    step = 2.0 * jnp.sin(my_orders.astype(F32) * (2.0 * math.pi / NPHI))
    step = jnp.concatenate([-step, step]).reshape(2 * slots, 1)
    slope = (order_table.astype(F32) / NS).reshape(1, -1)
    radius = (0.35 + 0.65 * (cylinder_row.astype(F32) + 0.5) / NS).reshape(levels_n, 1)
    copies, stacked = vmem_call(
        column_kernel,
        (
            jax.ShapeDtypeStruct((n_rad, 2 * slots, NS), BF16),
            jax.ShapeDtypeStruct((levels_n * lat_block, LANES), BF16),
        ),
        0, 3,
    )(arrived, weights, onehot)
    partials = exchanged(copies, "rad")
    chosen = vmem_call(
        select_kernel,
        jax.ShapeDtypeStruct((n_ma, row_block, LANES), BF16),
        0, 4,
    )(partials, step, chooser, stacked)
    got = exchanged(chosen, "ma")
    owned, advected = vmem_call(
        functools.partial(advect_kernel, levels_n, slots),
        (
            jax.ShapeDtypeStruct((row_block, lon_block), F32),
            jax.ShapeDtypeStruct((2, levels_n, NPHI), F32),
        ),
        1, 5,
    )((me_rad * lon_block).astype(I32).reshape(1), got, cosines, sines, slope, radius)
    return (owned, advected[:, None])


def solution(mesh):
    return jax.shard_map(
        on_device,
        mesh=mesh,
        in_specs=(
            P(None, "ma", "rad", None),
            P(),
            P("ma", "rad", None),
            P(),
            P(("rad", "ma"), None),
            P(("rad", "ma"), None),
        ),
        out_specs=(P("ma", "rad"), P(None, ("rad", "ma"), None, None)),
        check_vma=False,
    )
```

time: 132 us -> 112 us (0.85)
  Pallas kernels: 0 us -> 12.3 us
  local copies, waits for them, and re-layouts: 17.8 us -> 6.76 us
  starting transfers between devices: 51.8 us -> 41.2 us
  matrix products: 7.79 us -> 0 us
  waiting for transfers between devices: 37.1 us -> 33.2 us
  other arithmetic: 15.7 us -> 17.1 us
    pallas_call x0 -> x4, Pallas kernels: none -> 12.3 us  [the longest x1 4 us: on_device(): vmem_call(functools.partial(contribution_kernel, slots, degrees), jax.Sha...]
    all_to_all x5 -> x4, starting transfers between devices: 51.8 us -> 41.2 us  [exchanged(): return lax.all_to_all(blocks, axis, split_axis=0, concat_axis=0, tiled=True)]
    reshape x4 -> x2, local copies, waits for them, and re-layouts: 9.28 us -> 1.37 us  [the longest x1 0.69 us: on_device(): step = jnp.concatenate([-step, step]).reshape(2 * slots, 1)]
    dot_general x5 -> x0, matrix products: 7.79 us -> none  [the longest x1 2.83 us: on_device(): jnp.einsum('klt,rckl->trck', masked, levels, preferred_element_type=F32)]
    all_to_all x5 -> x4, waiting for transfers between devices: 37.1 us -> 33.2 us  [exchanged(): return lax.all_to_all(blocks, axis, split_axis=0, concat_axis=0, tiled=True)]
    convert_element_type x1 -> x4, other arithmetic: 9.89 us -> 13.6 us  [the longest x1 10.7 us: value_tables(): (-jnp.sin(angles) * weights[:, None]).astype(BF16)]
    unnamed x17 -> x13, local copies, waits for them, and re-layouts: 1.45 us -> 4.43 us
    convert_element_type x3 -> x0, local copies, waits for them, and re-layouts: 1.66 us -> none  [the longest x1 0.86 us: on_device(): jnp.einsum('ps,qs->pq', chooser, wanted, preferred_element_type=F32)]
  transfers between devices with their start and end apart: 5 -> 4, of which waited for: 4 -> 3; matrix products, arithmetic and copies ran while one was open for 22% -> 16% of each run, Pallas kernels for 0% -> 4%
where the time goes in v2:
time: 112 us; the launch traced here: 111 us
  starting transfers between devices  41.2 us (37%)
  waiting for transfers between devices  33.2 us (30%)
  other arithmetic  17.1 us (15%)
  Pallas kernels  12.3 us (11%)
  local copies, waits for them, and re-layouts  6.76 us (6%)
    all_to_all x4, starting transfers between devices, exchanged(): return lax.all_to_all(blocks, axis, split_axis=0, concat_axis=0, tiled=True)  41.2 us
    all_to_all x4, waiting for transfers between devices, exchanged(): return lax.all_to_all(blocks, axis, split_axis=0, concat_axis=0, tiled=True)  33.2 us
    convert_element_type x1, other arithmetic, value_tables(): (-jnp.sin(angles) * weights[:, None]).astype(BF16)  10.7 us
    unnamed x13, local copies, waits for them, and re-layouts  4.43 us
    pallas_call x1, Pallas kernels, on_device(): vmem_call(functools.partial(contribution_kernel, slots, degrees), jax.Sha...  4 us
    pallas_call x1, Pallas kernels, on_device(): vmem_call(functools.partial(advect_kernel, levels_n, slots), (jax.ShapeDt...  2.89 us
    pallas_call x1, Pallas kernels, on_device(): vmem_call(select_kernel, jax.ShapeDtypeStruct((n_ma, row_block, LANES), B...  2.81 us
    pallas_call x1, Pallas kernels, on_device(): vmem_call(column_kernel, (jax.ShapeDtypeStruct((n_rad, 2 * slots, NS), BF...  2.66 us
  transfers between devices with their start and end apart: 4, of which 3 were waited for; matrix products, arithmetic and copies ran while one was open for 16% of the time, Pallas kernels for 4%

profile of v2, /device:TPU:1, one launch (start us, length us, event | category | flops | bytes accessed | tf_op | source)
XLA Modules:
  0.0 111.5 jit_solution(17229805631273977112)
XLA Ops:
  0.6 0.7 convert_element_type.29
  1.3 0.7 maximum_bitcast_fusion
  2.6 10.3 %all-to-all-start.1 = ((f32[32,1,24]{2,1,0:T(1,128)}), f32[32,1,24]{2,1,0:T(1,128)S(1)}, u32[]{:S(2)}, u32[]{:S(2)}) async-start(f32[32,1,24]{2,1,0:T(1,128)} %broadcast_in_dim.12), calls=%async_computation.1 | async-start | bytes 32768 | tf_op jit(solution)/shard_map/all_to_all | solution.py:142
  13.0 0.8 fusion.18
  14.3 4.0 %shard_map.77 = bf16[16,32,768]{2,1,0:T(8,128)(2,1)} custom-call(s32[16]{0:T(128)} %copy-done.4, s32[1]{0:T(128)} %bitcast.1.first, bf16[12,384]{1,0:T(8,128)(2,1)} %radial.1, bf16[4,512,384]{2,1,0:T(8,128)(2,1)} %bitcast.22, bf16[512,512]{1,0:T(8,128)(2,1)} %bitcast.24), custom_call_target="tpu_custom_call" | custom-call | tf_op jit(solution)/shard_map/pallas_call | solution.py:187
  18.3 2.0 %all-to-all-done.1 = f32[32,1,24]{2,1,0:T(1,128)S(1)} async-done(((f32[32,1,24]{2,1,0:T(1,128)}), f32[32,1,24]{2,1,0:T(1,128)S(1)}, u32[]{:S(2)}, u32[]{:S(2)}) %all-to-all-start.1) | async-done | bytes 3104 | tf_op jit(solution)/shard_map/all_to_all | solution.py:142
  20.3 11.3 %all-to-all-start = ((bf16[16,32,768]{2,1,0:T(8,128)(2,1)}), bf16[16,32,768]{2,1,0:T(8,128)(2,1)S(1)}, u32[]{:S(2)}, u32[]{:S(2)}) async-start(bf16[16,32,768]{2,1,0:T(8,128)(2,1)} %shard_map.77), calls=%async_computation | async-start | bytes 1572864 | tf_op jit(solution)/shard_map/all_to_all | solution.py:142
  32.3 0.7 slice_convert_fusion
  33.2 0.9 fusion.6.onehot
  34.1 18.3 %all-to-all-done.arrived = bf16[16,32,768]{2,1,0:T(8,128)(2,1)S(1)} async-done(((bf16[16,32,768]{2,1,0:T(8,128)(2,1)}), bf16[16,32,768]{2,1,0:T(8,128)(2,1)S(1)}, u32[]{:S(2)}, u32[]{:S(2)}) %all-to-all-start) | async-done | bytes 786464 | tf_op jit(solution)/shard_map/all_to_all | solution.py:142
  52.4 0.9 copy-done
  53.3 2.7 %shard_map.78 = (bf16[16,32,512]{2,1,0:T(8,128)(2,1)}, bf16[384,128]{1,0:T(8,128)(2,1)}) custom-call(bf16[16,32,768]{2,1,0:T(8,128)(2,1)} %copy-done, f32[32,12]{1,0:T(8,128)} %get-tuple-element.20.weights, bf16[384,512]{1,0:T(8,128)(2,1)} %fusion.6.onehot), custom_call_target="tpu_custom_call" | custom-call | tf_op jit(solution)/shard_map/pallas_call | solution.py:207
  55.9 9.7 %all-to-all-start.2 = ((bf16[16,32,512]{2,1,0:T(8,128)(2,1)}), bf16[16,32,512]{2,1,0:T(8,128)(2,1)S(1)}, u32[]{:S(2)}, u32[]{:S(2)}) async-start(bf16[16,32,512]{2,1,0:T(8,128)(2,1)} %get-tuple-element.6), calls=%async_computation.2 | async-start | bytes 1048576 | tf_op jit(solution)/shard_map/all_to_all | solution.py:142
  65.7 0.7 copy.16.step
  66.4 0.7 copy.17.radius
  67.7 1.3 %add_convert_fusion.chooser = bf16[512,1408]{1,0:T(8,128)(2,1)} fusion(pred[512,384]{1,0:T(8,128)(4,1)S(1)} %bitcast.23, pred[512,512]{1,0:T(8,128)(4,1)S(1)} %get-tuple-element.26, pred[512,512]{1,0:T(8,128)(4,1)S(1)} %get-tuple-element.25), kind=kLoop, calls=%fused_computation.3 | loop fusion | flops 2162688 | bytes 2162688 | tf_op jit(solution)/shard_map/convert_element_type | solution.py:165
  69.0 12.9 %all-to-all-done.2.parts = bf16[16,32,512]{2,1,0:T(8,128)(2,1)S(1)} async-done(((bf16[16,32,512]{2,1,0:T(8,128)(2,1)}), bf16[16,32,512]{2,1,0:T(8,128)(2,1)S(1)}, u32[]{:S(2)}, u32[]{:S(2)}) %all-to-all-start.2) | async-done | bytes 524320 | tf_op jit(solution)/shard_map/all_to_all | solution.py:142
  81.9 0.8 copy-done.1
  82.7 2.8 %shard_map.79 = bf16[32,16,128]{2,1,0:T(8,128)(2,1)} custom-call(bf16[16,32,512]{2,1,0:T(8,128)(2,1)} %copy-done.1, f32[32,1]{1,0:T(8,128)} %copy.16.step, bf16[512,1408]{1,0:T(8,128)(2,1)} %add_convert_fusion.chooser, bf16[384,128]{1,0:T(8,128)(2,1)} %get-tuple-element.7.stacked), custom_call_target="tpu_custom_call" | custom-call | tf_op jit(solution)/shard_map/pallas_call | solution.py:216
  85.5 10.0 %all-to-all-start.3 = ((bf16[32,16,128]{2,1,0:T(8,128)(2,1)}), bf16[32,16,128]{2,1,0:T(8,128)(2,1)S(1)}, u32[]{:S(2)}, u32[]{:S(2)}) async-start(bf16[32,16,128]{2,1,0:T(8,128)(2,1)} %shard_map.79), calls=%async_computation.3 | async-start | bytes 262144 | tf_op jit(solution)/shard_map/all_to_all | solution.py:142
  95.5 10.7 %multiply_convert_fusion = (bf16[512,1024]{1,0:T(8,128)(2,1)}, bf16[512,1024]{1,0:T(8,128)(2,1)}) fusion(f32[512]{0:T(512)S(1)} %get-tuple-element.24, s32[512]{0:T(512)S(1)} %copy-done.3), kind=kLoop, calls=%fused_computation.7 | loop fusion | flops 9961472 | bytes 2101248 | tf_op jit(solution)/shard_map/convert_element_type | solution.py:152
  106.3 0.6 copy-done.2
  106.9 2.9 %shard_map.80 = (f32[16,64]{1,0:T(8,128)}, f32[2,12,1024]{2,1,0:T(8,128)}) custom-call(s32[1]{0:T(128)} %bitcast.block, bf16[32,16,128]{2,1,0:T(8,128)(2,1)} %copy-done.2, bf16[512,1024]{1,0:T(8,128)(2,1)} %get-tuple-element.22.cosines, bf16[512,1024]{1,0:T(8,128)(2,1)} %get-tuple-element.21.sines, f32[1,512]{1,0:T(1,128)} %bitcast.27, f32[12,1]{1,0:T(8,128)} %copy.17.radius), custom_call_target="tpu_custom_call" | custom-call | tf_op jit(solution)/shard_map/pallas_call | solution.py:222
  109.8 1.6 %copy.18 = f32[2,1,12,1024]{3,1,2,0:T(1,128)} copy(f32[2,1,12,1024]{3,2,0,1:T(8,128)} %bitcast.26) | data formatting | bytes 196608
  (33 shorter events, 2.8 us)
Async XLA Ops:
  2.6 17.7 %all-to-all-start.1 = ((f32[32,1,24]{2,1,0:T(1,128)}), f32[32,1,24]{2,1,0:T(1,128)S(1)}, u32[]{:S(2)}, u32[]{:S(2)}) async-start(f32[32,1,24]{2,1,0:T(1,128)} %broadcast_in_dim.12), calls=%async_computation.1 | async-start | bytes 32768 | tf_op jit(solution)/shard_map/all_to_all | solution.py:142
  13.8 0.5 copy-start.4
  14.3 17.3 %copy-start.5 = (s32[1,12]{1,0:T(1,128)S(1)}, s32[1,12]{1,0:T(1,128)}, u32[]{:S(2)}) copy-start(s32[1,12]{1,0:T(1,128)} %param.10) | copy-start | bytes 148
  14.3 17.3 %copy-start.3 = (s32[512]{0:T(512)S(1)}, s32[512]{0:T(512)}, u32[]{:S(2)}) copy-start(s32[512]{0:T(512)} %param.9) | copy-start | bytes 6148
  20.3 32.0 %all-to-all-start = ((bf16[16,32,768]{2,1,0:T(8,128)(2,1)}), bf16[16,32,768]{2,1,0:T(8,128)(2,1)S(1)}, u32[]{:S(2)}, u32[]{:S(2)}) async-start(bf16[16,32,768]{2,1,0:T(8,128)(2,1)} %shard_map.77), calls=%async_computation | async-start | bytes 1572864 | tf_op jit(solution)/shard_map/all_to_all | solution.py:142
  52.4 0.9 copy-start
  55.9 26.0 %all-to-all-start.2 = ((bf16[16,32,512]{2,1,0:T(8,128)(2,1)}), bf16[16,32,512]{2,1,0:T(8,128)(2,1)S(1)}, u32[]{:S(2)}, u32[]{:S(2)}) async-start(bf16[16,32,512]{2,1,0:T(8,128)(2,1)} %get-tuple-element.6), calls=%async_computation.2 | async-start | bytes 1048576 | tf_op jit(solution)/shard_map/all_to_all | solution.py:142
  81.9 0.8 copy-start.1
  85.5 20.8 %all-to-all-start.3 = ((bf16[32,16,128]{2,1,0:T(8,128)(2,1)}), bf16[32,16,128]{2,1,0:T(8,128)(2,1)S(1)}, u32[]{:S(2)}, u32[]{:S(2)}) async-start(bf16[32,16,128]{2,1,0:T(8,128)(2,1)} %shard_map.79), calls=%async_computation.3 | async-start | bytes 262144 | tf_op jit(solution)/shard_map/all_to_all | solution.py:142
  106.3 0.6 copy-start.2

commit v3 on v2

--- a/solution.py
+++ b/solution.py
@@ -6,11 +6,14 @@
 from jax import lax
 from jax.experimental import pallas as pl
 from jax.experimental.pallas import tpu as pltpu
+from jax.sharding import Mesh
 from jax.sharding import PartitionSpec as P
 
 NPHI = 1024
 NS = 512
 LANES = 128
+HALVES = 2
+VMEM_LIMIT = 20 * 2**20
 TIME_STEP = 0.05
 COMPOSITION_WEIGHT = 0.8
 BF16 = jnp.bfloat16
@@ -22,6 +25,14 @@
 
 def iota(shape, dim):
     return lax.broadcasted_iota(I32, shape, dim)
+
+
+def as_column(row, width):
+    return jnp.transpose(jnp.broadcast_to(row, (8, width)))[:, :1]
+
+
+def matches(column, row):
+    return (column == row).astype(F32).astype(BF16)
 
 
 def dot_dims(x, y, dim_x, dim_y):
@@ -35,10 +46,11 @@
         in_specs=[pl.BlockSpec(memory_space=pltpu.SMEM)] * n_smem
         + [pl.BlockSpec(memory_space=pltpu.VMEM)] * n_vmem,
         out_specs=jax.tree.map(lambda _: pl.BlockSpec(memory_space=pltpu.VMEM), outs),
-    )
-
-
-def contribution_kernel(slots, degrees, orders, first, radial, spectrum, legendre, out):
+        compiler_params=pltpu.CompilerParams(vmem_limit_bytes=VMEM_LIMIT),
+    )
+
+
+def contribution_kernel(slots, degrees, halves, orders, first, radial, spectrum, legendre, out):
     parts = spectrum.shape[0]
     levels_n = radial.shape[0]
     columns = levels_n * parts
@@ -60,11 +72,16 @@
         kept = (slot_of_lane == k) & (degree >= orders[k])
         blocks.append(jnp.where(kept, expanded[k * degrees : (k + 1) * degrees], 0.0).astype(BF16))
     diagonal = jnp.concatenate(blocks, axis=0)
-    total = dot_dims(legendre[...], diagonal, 0, 0)
-    out[...] = total.astype(BF16).reshape(out.shape)
-
-
-def column_kernel(arrived, weights, onehot, copies, stacked):
+    total = dot_dims(legendre[...], diagonal, 0, 0).astype(BF16)
+    n_z, lats, _ = out.shape
+    block = lats // halves
+    for h in range(halves):
+        for z in range(n_z):
+            at = (h * n_z + z) * block
+            out[z, h * block : (h + 1) * block] = total[at : at + block]
+
+
+def column_kernel(arrived, weights, rows, copies, stacked):
     levels_n = weights.shape[1]
     width = arrived.shape[2] // levels_n
     total = arrived[0].astype(F32)
@@ -81,12 +98,22 @@
     weighted = buoyancy * weight
     high = weighted.astype(BF16)
     low = (weighted - high.astype(F32)).astype(BF16)
-    both = dot_dims(jnp.concatenate([high, low], axis=1), onehot[...], 0, 0)
+    count = rows.shape[1]
+    onehot = matches(as_column(rows[...], count), iota((count, NS), 1))
+    both = dot_dims(jnp.concatenate([high, low], axis=1), onehot, 0, 0)
     column = (both[:half] + both[half:]).astype(BF16)
     copies[...] = jnp.broadcast_to(column[None], copies.shape)
 
 
-def select_kernel(parts, step, chooser, stacked, out):
+def message_kernel(per, stacked, base):
+    lats = base.shape[0] // per
+    count = stacked.shape[0]
+    point = iota((1, count), 1)
+    code = point % lats * per + point // lats
+    base[...] = dot(matches(iota((lats * per, count), 0), code), stacked[...]).astype(BF16)
+
+
+def select_kernel(levels_n, parts, step, picks, base, out):
     column = parts[0].astype(F32)
     for d in range(1, parts.shape[0]):
         column += parts[d].astype(F32)
@@ -100,15 +127,23 @@
     points = jnp.concatenate([outward, around, zeros, zeros], axis=0).astype(BF16)
     group = at // 4 % 4
     rows = jnp.concatenate([jnp.where(group == g, column, 0.0) for g in range(4)], axis=0)
-    chosen = dot_dims(chooser[:, :NS], points, 1, 1)
-    chosen += dot_dims(chooser[:, NS : 2 * NS], rows.astype(BF16), 1, 1)
-    chosen += dot(chooser[:, 2 * NS :], stacked[...])
+    per = out.shape[1]
+    own = per - levels_n
+    count = picks.shape[1]
+    s = iota((1, NS), 1)
+    n_ma = NS // per
+    message = iota((count, 1), 0)
+    q = message % per
+    code = jnp.where(q >= levels_n, message // per % n_ma * own + q - levels_n, -1)
+    chosen = dot_dims(matches(as_column(picks[...], count), s), points, 1, 1)
+    chosen += dot_dims(matches(code, s // per * own + s % own), rows.astype(BF16), 1, 1)
+    chosen += base[...].astype(F32)
     out[...] = chosen.astype(BF16).reshape(out.shape)
 
 
 def advect_kernel(levels_n, slots, block, got, cosines, sines, slope, radius, owned, advected):
-    n_ma, per, _ = got.shape
-    taken = [got[b] for b in range(n_ma)]
+    n_ma, per, _ = got.shape[1:]
+    taken = [(got[0, b].astype(F32) + got[1, b].astype(F32)).astype(BF16) for b in range(n_ma)]
     by_part = []
     for i in range(2):
         groups = []
@@ -131,7 +166,9 @@
     held = [x.astype(BF16).astype(F32) for x in rows[2:]]
     for f in range(2):
         field, side = held[f], held[2 + f]
-        advected[f] = field - (TIME_STEP * inverse) * (around * side + outward * field)
+        value = field - (TIME_STEP * inverse) * (around * side + outward * field)
+        for r in range(levels_n):
+            advected[f, r] = value[r : r + 1]
     mine = jnp.concatenate([result[g * per + levels_n : (g + 1) * per] for g in range(4)], axis=0)
     width = owned.shape[1]
     mine = pltpu.roll(mine, lax.rem(NPHI - block[0], NPHI), axis=1)
@@ -153,40 +190,30 @@
     )
 
 
-def choosers(rows, n_ma, levels_n, per):
-    q = jnp.arange(per, dtype=I32)[None, :, None]
-    b = jnp.arange(n_ma, dtype=I32)[:, None, None]
-    s = jnp.arange(NS, dtype=I32)[None, None, :]
-    p = jnp.arange(levels_n * n_ma, dtype=I32)[None, None, :]
-    padded = jnp.pad(rows, ((0, 0), (0, per - levels_n)), constant_values=-1)
-    point = padded[:, :, None] == s
-    owned = (s // per == b) & (q >= levels_n) & (s % (per - levels_n) == q - levels_n)
-    latitude = (p % n_ma == b) & (p // n_ma == q)
-    return jnp.concatenate([point, owned, latitude], axis=2).astype(BF16).reshape(n_ma * per, -1)
-
-
 def on_device(spectrum, radial_table, legendre, order_table, cylinder_row, column_weight):
     parts, slots, degrees, modes = spectrum.shape
     levels_n = radial_table.shape[0]
     lats = legendre.shape[2]
-    n_rad = lax.axis_size("rad")
+    n_z = lax.axis_size("z")
+    n_half = lax.axis_size("half")
     n_ma = lax.axis_size("ma")
-    lat_block = lats // n_rad
+    lat_block = lats // n_z
     row_block = NS // n_ma
-    lon_block = NPHI // n_rad
-    me_rad = lax.axis_index("rad")
+    lon_block = NPHI // (n_half * n_z)
+    me_rad = lax.axis_index(("half", "z"))
     me_ma = lax.axis_index("ma")
     my_orders = lax.dynamic_slice_in_dim(order_table, me_ma * slots, slots)
 
     info = jnp.concatenate([cylinder_row.astype(F32), column_weight], axis=1)
-    infos = exchanged(jnp.broadcast_to(info, (n_ma, 1, 2 * levels_n)), "ma")
-    infos = infos.reshape(n_ma, 2 * levels_n)
+    infos = exchanged(
+        jnp.broadcast_to(info, (lat_block, 1, 2 * levels_n)), ("half", "ma")
+    ).reshape(lat_block, 2 * levels_n)
     rows = infos[:, :levels_n].astype(I32)
     weights = infos[:, levels_n:]
     first = (me_rad * degrees).astype(I32).reshape(1)
     contribution = vmem_call(
-        functools.partial(contribution_kernel, slots, degrees),
-        jax.ShapeDtypeStruct((n_rad, lat_block, levels_n * parts * slots), BF16),
+        functools.partial(contribution_kernel, slots, degrees, n_half),
+        pltpu.HBM((n_z, lat_block, levels_n * parts * slots), BF16),
         2, 3,
     )(
         my_orders,
@@ -195,11 +222,11 @@
         spectrum.reshape(parts, slots * degrees, modes),
         legendre.reshape(slots * degrees, lats),
     )
-    arrived = exchanged(contribution, "rad")
+    arrived = exchanged(contribution, "z")
     cosines, sines = value_tables(order_table)
-    row_ids = jnp.arange(NS, dtype=I32)
-    onehot = (rows.T.reshape(-1)[:, None] == row_ids[None, :]).astype(BF16)
-    chooser = choosers(rows, n_ma, levels_n, row_block)
+    point_rows = rows.T.reshape(1, -1)
+    picks = jnp.pad(rows, ((0, 0), (0, row_block - levels_n)), constant_values=-1)
+    picks = picks.reshape(1, -1)
     step = 2.0 * jnp.sin(my_orders.astype(F32) * (2.0 * math.pi / NPHI))
     step = jnp.concatenate([-step, step]).reshape(2 * slots, 1)
     slope = (order_table.astype(F32) / NS).reshape(1, -1)
@@ -207,41 +234,48 @@
     copies, stacked = vmem_call(
         column_kernel,
         (
-            jax.ShapeDtypeStruct((n_rad, 2 * slots, NS), BF16),
+            pltpu.HBM((n_z, 2 * slots, NS), BF16),
             jax.ShapeDtypeStruct((levels_n * lat_block, LANES), BF16),
         ),
         0, 3,
-    )(arrived, weights, onehot)
-    partials = exchanged(copies, "rad")
+    )(arrived, weights, point_rows)
+    partials = exchanged(copies, "z")
+    base = vmem_call(
+        functools.partial(message_kernel, row_block),
+        jax.ShapeDtypeStruct((lat_block * row_block, LANES), BF16),
+        0, 1,
+    )(stacked)
     chosen = vmem_call(
-        select_kernel,
-        jax.ShapeDtypeStruct((n_ma, row_block, LANES), BF16),
+        functools.partial(select_kernel, levels_n),
+        pltpu.HBM((lat_block, row_block, LANES), BF16),
         0, 4,
-    )(partials, step, chooser, stacked)
-    got = exchanged(chosen, "ma")
+    )(partials, step, picks, base)
+    got = exchanged(chosen, ("half", "ma")).reshape(n_half, n_ma, row_block, LANES)
     owned, advected = vmem_call(
         functools.partial(advect_kernel, levels_n, slots),
         (
             jax.ShapeDtypeStruct((row_block, lon_block), F32),
-            jax.ShapeDtypeStruct((2, levels_n, NPHI), F32),
+            jax.ShapeDtypeStruct((2, levels_n, 1, NPHI), F32),
         ),
         1, 5,
     )((me_rad * lon_block).astype(I32).reshape(1), got, cosines, sines, slope, radius)
-    return (owned, advected[:, None])
+    return (owned, jnp.swapaxes(advected, 1, 2))
 
 
 def solution(mesh):
+    parts = Mesh(mesh.devices.reshape(HALVES, -1, mesh.shape["ma"]), ("half", "z", "ma"))
+    rad = ("half", "z")
     return jax.shard_map(
         on_device,
-        mesh=mesh,
+        mesh=parts,
         in_specs=(
-            P(None, "ma", "rad", None),
+            P(None, "ma", rad, None),
             P(),
-            P("ma", "rad", None),
+            P("ma", rad, None),
             P(),
-            P(("rad", "ma"), None),
-            P(("rad", "ma"), None),
+            P((*rad, "ma"), None),
+            P((*rad, "ma"), None),
         ),
-        out_specs=(P("ma", "rad"), P(None, ("rad", "ma"), None, None)),
+        out_specs=(P("ma", rad), P(None, (*rad, "ma"), None, None)),
         check_vma=False,
     )

time: 112 us -> 99.5 us (0.89)
  starting transfers between devices: 41.2 us -> 33.7 us
  waiting for transfers between devices: 33.2 us -> 40.2 us
  other arithmetic: 17.1 us -> 11.7 us
  Pallas kernels: 12.3 us -> 8.37 us
  local copies, waits for them, and re-layouts: 6.76 us -> 4.22 us
    all_to_all x4, starting transfers between devices: 41.2 us -> 33.7 us  [exchanged(): return lax.all_to_all(blocks, axis, split_axis=0, concat_axis=0, tiled=True)]
    all_to_all x4, waiting for transfers between devices: 33.2 us -> 40.2 us  [exchanged(): return lax.all_to_all(blocks, axis, split_axis=0, concat_axis=0, tiled=True)]
    pallas_call x3 -> x4, Pallas kernels: 9.46 us -> 7.06 us  [the longest x1 2.98 us: on_device(): vmem_call(functools.partial(contribution_kernel, slots, degrees, n_half),...]
    convert_element_type x2 -> x0, other arithmetic: 2.19 us -> none  [the longest x1 1.28 us: choosers(): jnp.concatenate([point, owned, latitude], axis=2).astype(BF16)]
    pallas_call x1, Pallas kernels: 2.89 us -> 1.31 us  [on_device(): vmem_call(functools.partial(advect_kernel, levels_n, slots), (jax.ShapeDt...]
    convert_element_type x1, other arithmetic: 10.7 us -> 9.27 us  [value_tables(): (-jnp.sin(angles) * weights[:, None]).astype(BF16)]
    unnamed x13 -> x10, local copies, waits for them, and re-layouts: 4.43 us -> 3.16 us
  transfers between devices with their start and end apart: 4 -> 4, of which waited for: 3 -> 4; matrix products, arithmetic and copies ran while one was open for 16% -> 11% of each run, Pallas kernels for 4% -> 4%
where the time goes in v3:
time: 99.5 us; the launch traced here: 98.9 us
  waiting for transfers between devices  40.2 us (40%)
  starting transfers between devices  33.7 us (34%)
  other arithmetic  11.7 us (12%)
  Pallas kernels  8.37 us (8%)
  local copies, waits for them, and re-layouts  4.22 us (4%)
    all_to_all x4, waiting for transfers between devices, exchanged(): return lax.all_to_all(blocks, axis, split_axis=0, concat_axis=0, tiled=True)  40.2 us
    all_to_all x4, starting transfers between devices, exchanged(): return lax.all_to_all(blocks, axis, split_axis=0, concat_axis=0, tiled=True)  33.7 us
    convert_element_type x1, other arithmetic, value_tables(): (-jnp.sin(angles) * weights[:, None]).astype(BF16)  9.27 us
    unnamed x10, local copies, waits for them, and re-layouts  3.16 us
    pallas_call x1, Pallas kernels, on_device(): vmem_call(functools.partial(contribution_kernel, slots, degrees, n_half),...  2.98 us
  transfers between devices with their start and end apart: 4, of which 4 were waited for; matrix products, arithmetic and copies ran while one was open for 11% of the time, Pallas kernels for 4%

profile of v3, /device:TPU:1, one launch (start us, length us, event | category | flops | bytes accessed | tf_op | source)
XLA Modules:
  0.0 98.9 jit_solution(63355945188320616)
XLA Ops:
  0.6 0.7 convert_element_type.22
  1.3 0.7 maximum_bitcast_fusion
  2.0 0.6 broadcast_in_dim.15
  2.7 11.6 %all-to-all-start.1 = ((f32[64,1,24]{2,1,0:T(1,128)}), f32[64,1,24]{2,1,0:T(1,128)S(1)}, u32[]{:S(2)}, u32[]{:S(2)}) async-start(f32[64,1,24]{2,1,0:T(1,128)} %broadcast_in_dim.15), calls=%async_computation.1 | async-start | bytes 65536 | tf_op jit(solution)/shard_map/all_to_all | solution.py:179
  14.3 0.8 fusion.6
  15.1 1.4 %copy-done = bf16[4,16,32,384]{3,2,1,0:T(8,128)(2,1)S(1)} copy-done((bf16[4,16,32,384]{3,2,1,0:T(8,128)(2,1)S(1)}, bf16[4,16,32,384]{3,2,1,0:T(8,128)(2,1)}, u32[]{:S(2)}) %copy-start) | copy-done | bytes 1572888
  16.5 1.0 %copy-done.1 = bf16[16,32,512]{2,1,0:T(8,128)(2,1)S(1)} copy-done((bf16[16,32,512]{2,1,0:T(8,128)(2,1)S(1)}, bf16[16,32,512]{2,1,0:T(8,128)(2,1)}, u32[]{:S(2)}) %copy-start.1) | copy-done | bytes 524312
  17.5 0.7 copy-done.2
  18.2 3.0 %shard_map.77 = bf16[8,64,768]{2,1,0:T(8,128)(2,1)} custom-call(s32[16]{0:T(128)S(1)} %get-tuple-element.11.orders, s32[1]{0:T(128)} %bitcast.1.first, bf16[12,384]{1,0:T(8,128)(2,1)S(1)} %copy-done.2, bf16[4,512,384]{2,1,0:T(8,128)(2,1)S(1)} %bitcast.16, bf16[512,512]{1,0:T(8,128)(2,1)S(1)} %bitcast.18), custom_call_target="tpu_custom_call" | custom-call | tf_op jit(solution)/shard_map/pallas_call | solution.py:214
  21.2 2.4 %all-to-all-done.1 = f32[64,1,24]{2,1,0:T(1,128)S(1)} async-done(((f32[64,1,24]{2,1,0:T(1,128)}), f32[64,1,24]{2,1,0:T(1,128)S(1)}, u32[]{:S(2)}, u32[]{:S(2)}) %all-to-all-start.1) | async-done | bytes 6176 | tf_op jit(solution)/shard_map/all_to_all | solution.py:179
  23.6 10.0 %all-to-all-start = ((bf16[8,64,768]{2,1,0:T(8,128)(2,1)}), bf16[8,64,768]{2,1,0:T(8,128)(2,1)S(1)}, u32[]{:S(2)}, u32[]{:S(2)}) async-start(bf16[8,64,768]{2,1,0:T(8,128)(2,1)} %shard_map.77), calls=%async_computation | async-start | bytes 1572864 | tf_op jit(solution)/shard_map/all_to_all | solution.py:179
  33.9 23.3 %all-to-all-done.arrived = bf16[8,64,768]{2,1,0:T(8,128)(2,1)S(1)} async-done(((bf16[8,64,768]{2,1,0:T(8,128)(2,1)}), bf16[8,64,768]{2,1,0:T(8,128)(2,1)S(1)}, u32[]{:S(2)}, u32[]{:S(2)}) %all-to-all-start) | async-done | bytes 786464 | tf_op jit(solution)/shard_map/all_to_all | solution.py:179
  57.2 1.9 %shard_map.78 = (bf16[8,32,512]{2,1,0:T(8,128)(2,1)}, bf16[768,128]{1,0:T(8,128)(2,1)S(1)}) custom-call(bf16[8,64,768]{2,1,0:T(8,128)(2,1)S(1)} %all-to-all-done.arrived, f32[64,12]{1,0:T(8,128)S(1)} %get-tuple-element.14.weights, s32[1,768]{1,0:T(1,128)S(1)} %reshape.45.rows), custom_call_target="tpu_custom_call" | custom-call | tf_op jit(solution)/shard_map/pallas_call | solution.py:234
  59.1 3.4 %all-to-all-start.2 = ((bf16[8,32,512]{2,1,0:T(8,128)(2,1)}), bf16[8,32,512]{2,1,0:T(8,128)(2,1)S(1)}, u32[]{:S(2)}, u32[]{:S(2)}) async-start(bf16[8,32,512]{2,1,0:T(8,128)(2,1)} %get-tuple-element.6), calls=%async_computation.2 | async-start | bytes 524288 | tf_op jit(solution)/shard_map/all_to_all | solution.py:179
  62.6 0.1 copy.16.radius
  62.8 0.1 copy.15.step
  62.9 0.1 reshape.47.picks
  63.0 0.6 shard_map.79.base
  63.6 10.8 %all-to-all-done.2.parts = bf16[8,32,512]{2,1,0:T(8,128)(2,1)S(1)} async-done(((bf16[8,32,512]{2,1,0:T(8,128)(2,1)}), bf16[8,32,512]{2,1,0:T(8,128)(2,1)S(1)}, u32[]{:S(2)}, u32[]{:S(2)}) %all-to-all-start.2) | async-done | bytes 262176 | tf_op jit(solution)/shard_map/all_to_all | solution.py:179
  74.3 1.6 %shard_map.80 = bf16[64,16,128]{2,1,0:T(8,128)(2,1)} custom-call(bf16[8,32,512]{2,1,0:T(8,128)(2,1)S(1)} %all-to-all-done.2.parts, f32[32,1]{1,0:T(8,128)S(1)} %copy.15.step, s32[1,1024]{1,0:T(1,128)S(1)} %reshape.47.picks, bf16[1024,128]{1,0:T(8,128)(2,1)S(1)} %shard_map.79.base), custom_call_target="tpu_custom_call" | custom-call | tf_op jit(solution)/shard_map/pallas_call | solution.py:248
  75.9 8.7 %all-to-all-start.3 = ((bf16[64,16,128]{2,1,0:T(8,128)(2,1)}), bf16[64,16,128]{2,1,0:T(8,128)(2,1)S(1)}, u32[]{:S(2)}, u32[]{:S(2)}) async-start(bf16[64,16,128]{2,1,0:T(8,128)(2,1)} %shard_map.80), calls=%async_computation.3 | async-start | bytes 524288 | tf_op jit(solution)/shard_map/all_to_all | solution.py:179
  84.6 9.3 %multiply_convert_fusion = (bf16[512,1024]{1,0:T(8,128)(2,1)S(1)}, bf16[512,1024]{1,0:T(8,128)(2,1)S(1)}) fusion(f32[512]{0:T(512)S(1)} %get-tuple-element.18, s32[512]{0:T(512)S(1)} %copy-done.3), kind=kLoop, calls=%fused_computation.6 | loop fusion | flops 9961472 | bytes 2101248 | tf_op jit(solution)/shard_map/convert_element_type | solution.py:189
  93.9 3.8 %all-to-all-done.3 = bf16[64,16,128]{2,1,0:T(8,128)(2,1)S(1)} async-done(((bf16[64,16,128]{2,1,0:T(8,128)(2,1)}), bf16[64,16,128]{2,1,0:T(8,128)(2,1)S(1)}, u32[]{:S(2)}, u32[]{:S(2)}) %all-to-all-start.3) | async-done | bytes 262176 | tf_op jit(solution)/shard_map/all_to_all | solution.py:179
  97.6 1.3 %shard_map.81 = (f32[16,64]{1,0:T(8,128)}, f32[2,12,1,1024]{3,2,1,0:T(1,128)}) custom-call(s32[1]{0:T(128)} %bitcast.block, bf16[2,32,16,128]{3,2,1,0:T(8,128)(2,1)S(1)} %bitcast.17, bf16[512,1024]{1,0:T(8,128)(2,1)S(1)} %get-tuple-element.16.cosines, bf16[512,1024]{1,0:T(8,128)(2,1)S(1)} %get-tuple-element.15.sines, f32[1,512]{1,0:T(1,128)S(1)} %bitcast.19, ...), custom_call_target="tpu_custom_call" | custom-call | tf_op jit(solution)/shard_map/pallas_call | solution.py:254
  (15 shorter events, 0.4 us)
Async XLA Ops:
  2.7 20.9 %all-to-all-start.1 = ((f32[64,1,24]{2,1,0:T(1,128)}), f32[64,1,24]{2,1,0:T(1,128)S(1)}, u32[]{:S(2)}, u32[]{:S(2)}) async-start(f32[64,1,24]{2,1,0:T(1,128)} %broadcast_in_dim.15), calls=%async_computation.1 | async-start | bytes 65536 | tf_op jit(solution)/shard_map/all_to_all | solution.py:179
  15.1 1.4 %copy-start = (bf16[4,16,32,384]{3,2,1,0:T(8,128)(2,1)S(1)}, bf16[4,16,32,384]{3,2,1,0:T(8,128)(2,1)}, u32[]{:S(2)}) copy-start(bf16[4,16,32,384]{3,2,1,0:T(8,128)(2,1)} %param.6) | copy-start | bytes 4718596
  16.5 1.0 %copy-start.1 = (bf16[16,32,512]{2,1,0:T(8,128)(2,1)S(1)}, bf16[16,32,512]{2,1,0:T(8,128)(2,1)}, u32[]{:S(2)}) copy-start(bf16[16,32,512]{2,1,0:T(8,128)(2,1)} %param.8) | copy-start | bytes 1572868
  17.5 0.7 copy-start.2
  21.2 41.3 %copy-start.4 = (s32[1,12]{1,0:T(1,128)S(1)}, s32[1,12]{1,0:T(1,128)}, u32[]{:S(2)}) copy-start(s32[1,12]{1,0:T(1,128)} %param.10) | copy-start | bytes 148
  23.6 33.6 %all-to-all-start = ((bf16[8,64,768]{2,1,0:T(8,128)(2,1)}), bf16[8,64,768]{2,1,0:T(8,128)(2,1)S(1)}, u32[]{:S(2)}, u32[]{:S(2)}) async-start(bf16[8,64,768]{2,1,0:T(8,128)(2,1)} %shard_map.77), calls=%async_computation | async-start | bytes 1572864 | tf_op jit(solution)/shard_map/all_to_all | solution.py:179
  57.2 27.3 %copy-start.3 = (s32[512]{0:T(512)S(1)}, s32[512]{0:T(512)}, u32[]{:S(2)}) copy-start(s32[512]{0:T(512)} %param.9) | copy-start | bytes 6148
  59.1 15.2 %all-to-all-start.2 = ((bf16[8,32,512]{2,1,0:T(8,128)(2,1)}), bf16[8,32,512]{2,1,0:T(8,128)(2,1)S(1)}, u32[]{:S(2)}, u32[]{:S(2)}) async-start(bf16[8,32,512]{2,1,0:T(8,128)(2,1)} %get-tuple-element.6), calls=%async_computation.2 | async-start | bytes 524288 | tf_op jit(solution)/shard_map/all_to_all | solution.py:179
  75.9 21.7 %all-to-all-start.3 = ((bf16[64,16,128]{2,1,0:T(8,128)(2,1)}), bf16[64,16,128]{2,1,0:T(8,128)(2,1)S(1)}, u32[]{:S(2)}, u32[]{:S(2)}) async-start(bf16[64,16,128]{2,1,0:T(8,128)(2,1)} %shard_map.80), calls=%async_computation.3 | async-start | bytes 524288 | tf_op jit(solution)/shard_map/all_to_all | solution.py:179

commit v4 on v3

v4 whole, which is shorter than its diff:
```python
import functools
import math

import jax
import jax.numpy as jnp
from jax import lax
from jax.experimental import pallas as pl
from jax.experimental.pallas import tpu as pltpu
from jax.sharding import Mesh
from jax.sharding import PartitionSpec as P

NPHI = 1024
NS = 512
LANES = 128
HALVES = 2
PAIRS = 2
MA = ("pair", "y", "x", "core")
VMEM_LIMIT = 20 * 2**20
TIME_STEP = 0.05
COMPOSITION_WEIGHT = 0.8
BF16 = jnp.bfloat16
F32 = jnp.float32
I32 = jnp.int32

dot = functools.partial(jnp.dot, preferred_element_type=F32)


def iota(shape, dim):
    return lax.broadcasted_iota(I32, shape, dim)


def as_column(row, width):
    return jnp.transpose(jnp.broadcast_to(row, (8, width)))[:, :1]


def matches(column, row):
    return (column == row).astype(F32).astype(BF16)


def dot_dims(x, y, dim_x, dim_y):
    return lax.dot_general(x, y, (((dim_x,), (dim_y,)), ((), ())), preferred_element_type=F32)


def vmem_call(body, outs, n_smem, n_vmem, n_hbm=0, scratch=()):
    return pl.pallas_call(
        body,
        out_shape=outs,
        in_specs=[pl.BlockSpec(memory_space=pltpu.SMEM)] * n_smem
        + [pl.BlockSpec(memory_space=pltpu.VMEM)] * n_vmem
        + [pl.BlockSpec(memory_space=pltpu.HBM)] * n_hbm,
        out_specs=jax.tree.map(lambda _: pl.BlockSpec(memory_space=pltpu.VMEM), outs),
        scratch_shapes=scratch,
        compiler_params=pltpu.CompilerParams(vmem_limit_bytes=VMEM_LIMIT),
    )


def info_kernel(rows, weights, out):
    info = jnp.concatenate([rows[...].astype(F32), weights[...]], axis=1)
    for d in range(out.shape[0]):
        out[d] = info


def in_place(infos):
    count = infos.shape[0] // 4
    pieces = [infos[j * count : (j + 1) * count] for j in range(4)]
    pair, half = lax.axis_index("pair") == 0, lax.axis_index("half") == 0
    halves = [
        jnp.concatenate([jnp.where(pair, a, b), jnp.where(pair, b, a)], axis=0)
        for a, b in (pieces[:2], pieces[2:])
    ]
    a, b = halves
    return jnp.concatenate([jnp.where(half, a, b), jnp.where(half, b, a)], axis=0)


def contribution_kernel(
    slots, degrees, halves, orders, radial, spectrum_in, legendre_in, out, spectrum, legendre, sems
):
    parts = spectrum.shape[0]
    copies = [
        pltpu.make_async_copy(spectrum_in.at[c], spectrum.at[c], sems.at[c]) for c in range(parts)
    ]
    copies.append(pltpu.make_async_copy(legendre_in, legendre, sems.at[parts]))
    for copy in copies:
        copy.start()
    levels_n = radial.shape[0]
    columns = levels_n * parts
    width = columns * slots
    rows = slots * degrees
    repeat = (iota((columns, levels_n), 0) // parts == iota((columns, levels_n), 1)).astype(BF16)
    repeated = dot(repeat, radial[...])
    part_of = iota(repeated.shape, 0) % parts
    levels = jnp.zeros((rows, columns), F32)
    for c in range(parts):
        table = jnp.where(part_of == c, repeated, 0.0).astype(BF16)
        copies[c].wait()
        levels += dot_dims(spectrum[c], table, 1, 1)
    spread = (iota((columns, width), 0) == iota((columns, width), 1) // slots).astype(BF16)
    expanded = dot(levels.astype(BF16), spread)
    slot_of_lane = iota((degrees, width), 1) % slots
    degree = iota((degrees, width), 0) + lax.axis_index(("half", "z")) * degrees
    first_slot = lax.axis_index(MA) * slots
    blocks = []
    for k in range(slots):
        kept = (slot_of_lane == k) & (degree >= orders[first_slot + k])
        blocks.append(jnp.where(kept, expanded[k * degrees : (k + 1) * degrees], 0.0).astype(BF16))
    diagonal = jnp.concatenate(blocks, axis=0)
    copies[parts].wait()
    total = dot_dims(legendre[...], diagonal, 0, 0).astype(BF16)
    n_z, lats, _ = out.shape
    block = lats // halves
    for h in range(halves):
        for z in range(n_z):
            at_lat = (h * n_z + z) * block
            out[z, h * block : (h + 1) * block] = total[at_lat : at_lat + block]


def table_kernel(orders, cosines, sines):
    count = orders.shape[1]
    order = jnp.broadcast_to(as_column(orders[...], count), (count, LANES))
    angle = (order * iota((count, LANES), 1) % NPHI).astype(F32) * (2.0 * math.pi / NPHI)
    weight = jnp.where(order == 0, 1.0, 2.0).astype(F32) / math.sqrt(NS)
    cosine, sine = jnp.cos(angle) * weight, jnp.sin(angle) * weight
    half_root = math.sqrt(0.5)
    for j in range(NPHI // LANES):
        eighth = order * j % 8
        size = jnp.where(eighth % 2 == 1, half_root, 1.0)
        turn_cos = jnp.where(eighth % 4 == 2, 0.0, jnp.where((eighth >= 3) & (eighth <= 5), -size, size))
        turn_sin = jnp.where(eighth % 4 == 0, 0.0, jnp.where(eighth > 4, -size, size))
        at = slice(j * LANES, (j + 1) * LANES)
        cosines[:, at] = (cosine * turn_cos - sine * turn_sin).astype(BF16)
        sines[:, at] = (-sine * turn_cos - cosine * turn_sin).astype(BF16)


def column_kernel(arrived, infos, copies, stacked):
    lats = arrived.shape[1]
    levels_n = infos.shape[1] // 2
    width = arrived.shape[2] // levels_n
    total = arrived[0].astype(F32)
    for d in range(1, arrived.shape[0]):
        total += arrived[d].astype(F32)
    points = jnp.concatenate(
        [total[:, r * width : (r + 1) * width] for r in range(levels_n)], axis=0
    ).astype(BF16)
    stacked[...] = jnp.concatenate([jnp.zeros_like(points), points], axis=1)
    half = width // 2
    exact = points.astype(F32)
    buoyancy = exact[:, :half] - COMPOSITION_WEIGHT * exact[:, half:]
    info = in_place(infos[...])
    rows = jnp.concatenate([info[:, r : r + 1] for r in range(levels_n)], axis=0)
    weight = jnp.concatenate([info[:, r : r + 1] for r in range(levels_n, 2 * levels_n)], axis=0)
    weighted = buoyancy * weight
    high = weighted.astype(BF16)
    low = (weighted - high.astype(F32)).astype(BF16)
    onehot = matches(rows, iota((lats * levels_n, NS), 1).astype(F32))
    both = dot_dims(jnp.concatenate([high, low], axis=1), onehot, 0, 0)
    column = (both[:half] + both[half:]).astype(BF16)
    copies[...] = jnp.broadcast_to(column[None], copies.shape)


def message_kernel(per, stacked, infos, base, picks):
    lats = base.shape[0] // per
    levels_n = infos.shape[1] // 2
    info = in_place(infos[...])
    q = iota((per, info.shape[1]), 0)
    own_level = (q == iota(q.shape, 1)) & (q < levels_n)
    wanted = [
        jnp.sum(jnp.where(own_level, info[t : t + 1], 0.0), axis=1, keepdims=True)
        for t in range(lats)
    ]
    absent = iota((lats * per, 1), 0) % per >= levels_n
    row = jnp.where(absent, -1.0, jnp.concatenate(wanted, axis=0))
    picks[...] = matches(row, iota((lats * per, NS), 1).astype(F32))
    count = stacked.shape[0]
    point = iota((1, count), 1)
    code = point % lats * per + point // lats
    base[...] = dot(matches(iota((lats * per, count), 0), code), stacked[...]).astype(BF16)


def select_kernel(levels_n, parts, step, picks, base, out):
    column = parts[0].astype(F32)
    for d in range(1, parts.shape[0]):
        column += parts[d].astype(F32)
    half = column.shape[0] // 2
    outward = step[...] * jnp.concatenate([column[half:], column[:half]], axis=0)
    at = iota(column.shape, 1)
    after = jnp.where(at == NS - 1, 0.0, pltpu.roll(column, NS - 1, axis=1))
    before = jnp.where(at == 0, 0.0, pltpu.roll(column, 1, axis=1))
    around = after - before
    zeros = jnp.zeros_like(column)
    points = jnp.concatenate([outward, around, zeros, zeros], axis=0).astype(BF16)
    group = at // 4 % 4
    rows = jnp.concatenate([jnp.where(group == g, column, 0.0) for g in range(4)], axis=0)
    per = out.shape[1]
    own = per - levels_n
    count = picks.shape[0]
    s = iota((1, NS), 1)
    n_ma = NS // per
    message = iota((count, 1), 0)
    q = message % per
    code = jnp.where(q >= levels_n, message // per % n_ma * own + q - levels_n, -1)
    chosen = dot_dims(picks[...], points, 1, 1)
    chosen += dot_dims(matches(code, s // per * own + s % own), rows.astype(BF16), 1, 1)
    chosen += base[...].astype(F32)
    out[...] = chosen.astype(BF16).reshape(out.shape)


def advect_kernel(levels_n, slots, got, cosines, sines, slope, radius, owned, advected):
    n_ma, per, _ = got.shape[1:]
    taken = [(got[0, b].astype(F32) + got[1, b].astype(F32)).astype(BF16) for b in range(n_ma)]
    by_part = []
    for i in range(2):
        groups = []
        for g in range(4):
            at = (2 * g + i) * slots
            groups.append(jnp.concatenate([x[:, at : at + slots] for x in taken], axis=1))
        by_part.append(groups)
    scale = slope[...]
    sides = []
    for i in range(2):
        turned = [
            (by_part[1 - i][g].astype(F32) * (scale if i else -scale)).astype(BF16) for g in (2, 3)
        ]
        sides.append(jnp.concatenate(by_part[i] + turned, axis=0))
    result = dot(sides[0], cosines[...]) + dot(sides[1], sines[...])
    rows = [result[g * per : g * per + levels_n] for g in range(6)]
    inverse = 1.0 / radius[...]
    outward = rows[0] * (0.5 * inverse)
    around = -0.5 * rows[1]
    held = [x.astype(BF16).astype(F32) for x in rows[2:]]
    for f in range(2):
        field, side = held[f], held[2 + f]
        value = field - (TIME_STEP * inverse) * (around * side + outward * field)
        for r in range(levels_n):
            advected[f, r] = value[r : r + 1]
    mine = jnp.concatenate([result[g * per + levels_n : (g + 1) * per] for g in range(4)], axis=0)
    width = owned.shape[1]
    start = lax.axis_index(("half", "z")) * width
    mine = pltpu.roll(mine, lax.rem(NPHI - start, NPHI), axis=1)
    owned[...] = mine[:, :width]


def in_hbm(array):
    return pltpu.with_memory_space_constraint(array, pltpu.HBM)


def exchanged(blocks, axis):
    return lax.all_to_all(blocks, axis, split_axis=0, concat_axis=0, tiled=True)


def on_device(spectrum, radial_table, legendre, order_table, cylinder_row, column_weight):
    parts, slots, degrees, modes = spectrum.shape
    levels_n = radial_table.shape[0]
    lats = legendre.shape[2]
    n_z = lax.axis_size("z")
    n_half = lax.axis_size("half")
    n_ma = lax.axis_size(MA)
    lat_block = lats // n_z
    row_block = NS // n_ma
    lon_block = NPHI // (n_half * n_z)
    me_ma = lax.axis_index(MA)
    swap = [(0, 1), (1, 0)]

    near = ("y", "x", "core")
    info = vmem_call(
        info_kernel,
        pltpu.HBM((lax.axis_size(near), 1, 2 * levels_n), F32),
        0, 2,
    )(in_hbm(cylinder_row), in_hbm(column_weight))
    info = exchanged(info, near).reshape(-1, 2 * levels_n)
    contribution = vmem_call(
        functools.partial(contribution_kernel, slots, degrees, n_half),
        pltpu.HBM((n_z, lat_block, levels_n * parts * slots), BF16),
        1, 1, 2,
        (
            pltpu.VMEM((parts, slots * degrees, modes), BF16),
            pltpu.VMEM((slots * degrees, lats), BF16),
            pltpu.SemaphoreType.DMA((parts + 1,)),
        ),
    )(
        in_hbm(order_table),
        in_hbm(radial_table),
        in_hbm(spectrum.reshape(parts, slots * degrees, modes)),
        in_hbm(legendre.reshape(slots * degrees, lats)),
    )
    arrived = exchanged(contribution, "z")
    info = jnp.concatenate([info, lax.ppermute(info, "pair", swap)], axis=0)
    infos = jnp.concatenate([info, lax.ppermute(info, "half", swap)], axis=0)
    my_orders = lax.dynamic_slice_in_dim(order_table, me_ma * slots, slots)
    step = 2.0 * jnp.sin(my_orders.astype(F32) * (2.0 * math.pi / NPHI))
    step = jnp.concatenate([-step, step]).reshape(2 * slots, 1)
    slope = (order_table.astype(F32) / NS).reshape(1, -1)
    radius = (0.35 + 0.65 * (cylinder_row.astype(F32) + 0.5) / NS).reshape(levels_n, 1)
    copies, stacked = vmem_call(
        column_kernel,
        (
            pltpu.HBM((n_z, 2 * slots, NS), BF16),
            jax.ShapeDtypeStruct((levels_n * lat_block, LANES), BF16),
        ),
        0, 2,
    )(arrived, infos)
    partials = exchanged(copies, "z")
    base, picks = vmem_call(
        functools.partial(message_kernel, row_block),
        (
            jax.ShapeDtypeStruct((lat_block * row_block, LANES), BF16),
            jax.ShapeDtypeStruct((lat_block * row_block, NS), BF16),
        ),
        0, 2,
    )(stacked, infos)
    chosen = vmem_call(
        functools.partial(select_kernel, levels_n),
        pltpu.HBM((lat_block, row_block, LANES), BF16),
        0, 4,
    )(partials, step, picks, base)
    got = exchanged(chosen, ("half", *MA)).reshape(n_half, n_ma, row_block, LANES)
    table = jax.ShapeDtypeStruct((lats, NPHI), BF16)
    cosines, sines = vmem_call(table_kernel, (table, table), 0, 1)(order_table.reshape(1, -1))
    owned, advected = vmem_call(
        functools.partial(advect_kernel, levels_n, slots),
        (
            jax.ShapeDtypeStruct((row_block, lon_block), F32),
            jax.ShapeDtypeStruct((2, levels_n, 1, NPHI), F32),
        ),
        0, 5,
    )(got, cosines, sines, slope, radius)
    return (owned, jnp.swapaxes(advected, 1, 2))


def solution(mesh):
    parts = Mesh(
        mesh.devices.reshape(HALVES, -1, PAIRS, PAIRS, mesh.shape["ma"] // 8, 2),
        ("half", "z", *MA),
    )
    rad = ("half", "z")
    return jax.shard_map(
        on_device,
        mesh=parts,
        in_specs=(
            P(None, MA, rad, None),
            P(),
            P(MA, rad, None),
            P(),
            P((*rad, *MA), None),
            P((*rad, *MA), None),
        ),
        out_specs=(P(MA, rad), P(None, (*rad, *MA), None, None)),
        check_vma=False,
    )
```

time: 99.5 us -> 90.8 us (0.913)
  other arithmetic: 11.7 us -> 0.22 us
  waiting for transfers between devices: 40.2 us -> 31.5 us
  Pallas kernels: 8.37 us -> 16.9 us
  starting transfers between devices: 33.7 us -> 40.7 us
  local copies, waits for them, and re-layouts: 4.22 us -> 0.2 us
    all_to_all x4, waiting for transfers between devices: 40.2 us -> 28.6 us  [exchanged(): return lax.all_to_all(blocks, axis, split_axis=0, concat_axis=0, tiled=True)]
    ppermute x0 -> x2, starting transfers between devices: none -> 10.7 us  [the longest x1 6.54 us: on_device(): infos = jnp.concatenate([info, lax.ppermute(info, 'half', swap)], axis=0)]
    convert_element_type x3 -> x0, other arithmetic: 10 us -> none  [the longest x1 9.27 us: value_tables(): (-jnp.sin(angles) * weights[:, None]).astype(BF16)]
    pallas_call x1 -> x3, Pallas kernels: 0.58 us -> 7.77 us  [the longest x1 5.69 us: on_device(): vmem_call(table_kernel, (table, table), 0, 1)(order_table.reshape(1, -1))]
    all_to_all x4, starting transfers between devices: 33.7 us -> 30 us  [exchanged(): return lax.all_to_all(blocks, axis, split_axis=0, concat_axis=0, tiled=True)]
    unnamed x10 -> x4, local copies, waits for them, and re-layouts: 3.16 us -> 0.01 us
    ppermute x0 -> x2, waiting for transfers between devices: none -> 2.9 us  [the longest x1 1.83 us: on_device(): infos = jnp.concatenate([info, lax.ppermute(info, 'half', swap)], axis=0)]
    pallas_call x1, Pallas kernels: 2.98 us -> 4.75 us  [on_device(): vmem_call(functools.partial(contribution_kernel, slots, degrees, n_half),...]
  transfers between devices with their start and end apart: 4 -> 6, of which waited for: 4 -> 6; matrix products, arithmetic and copies ran while one was open for 11% -> 0% of each run, Pallas kernels for 4% -> 12%
where the time goes in v4:
time: 90.8 us; the launch traced here: 90.3 us
  starting transfers between devices  40.7 us (45%)
  waiting for transfers between devices  31.5 us (35%)
  Pallas kernels  16.9 us (19%)
    all_to_all x4, starting transfers between devices, exchanged(): return lax.all_to_all(blocks, axis, split_axis=0, concat_axis=0, tiled=True)  30 us
    all_to_all x4, waiting for transfers between devices, exchanged(): return lax.all_to_all(blocks, axis, split_axis=0, concat_axis=0, tiled=True)  28.6 us
    ppermute x1, starting transfers between devices, on_device(): infos = jnp.concatenate([info, lax.ppermute(info, 'half', swap)], axis=0)  6.54 us
    pallas_call x1, Pallas kernels, on_device(): vmem_call(table_kernel, (table, table), 0, 1)(order_table.reshape(1, -1))  5.69 us
    pallas_call x1, Pallas kernels, on_device(): vmem_call(functools.partial(contribution_kernel, slots, degrees, n_half),...  4.75 us
    ppermute x1, starting transfers between devices, on_device(): info = jnp.concatenate([info, lax.ppermute(info, 'pair', swap)], axis=0)  4.21 us
    ppermute x1, waiting for transfers between devices, on_device(): infos = jnp.concatenate([info, lax.ppermute(info, 'half', swap)], axis=0)  1.83 us
  transfers between devices with their start and end apart: 6, of which 6 were waited for; matrix products, arithmetic and copies ran while one was open for 0% of the time, Pallas kernels for 12%

profile of v4, /device:TPU:1, one launch (start us, length us, event | category | flops | bytes accessed | tf_op | source)
XLA Modules:
  0.0 90.3 jit_solution(7733432269494707663)
XLA Ops:
  0.6 1.3 %shard_map.78 = f32[16,1,24]{2,1,0:T(1,128)} custom-call(s32[1,12]{1,0:T(1,128)} %rows.1, f32[1,12]{1,0:T(1,128)} %weights.1), custom_call_target="tpu_custom_call" | custom-call | tf_op jit(solution)/shard_map/pallas_call | solution.py:264
  2.0 10.1 %all-to-all-start.1 = ((f32[16,1,24]{2,1,0:T(1,128)}), f32[16,1,24]{2,1,0:T(1,128)S(1)}, u32[]{:S(2)}, u32[]{:S(2)}) async-start(f32[16,1,24]{2,1,0:T(1,128)} %shard_map.78), calls=%async_computation.1 | async-start | bytes 16384 | tf_op jit(solution)/shard_map/all_to_all | solution.py:247
  12.1 4.7 %shard_map.77 = bf16[8,64,768]{2,1,0:T(8,128)(2,1)} custom-call(s32[512]{0:T(512)} %orders.1, bf16[12,384]{1,0:T(8,128)(2,1)} %radial.1, bf16[4,512,384]{2,1,0:T(8,128)(2,1)} %bitcast.14, bf16[512,512]{1,0:T(8,128)(2,1)} %bitcast.15), custom_call_target="tpu_custom_call" | custom-call | tf_op jit(solution)/shard_map/pallas_call | solution.py:270
  16.8 0.0 copy-start
  16.8 0.7 all-to-all-done.1
  17.6 6.7 %all-to-all-start = ((bf16[8,64,768]{2,1,0:T(8,128)(2,1)}), bf16[8,64,768]{2,1,0:T(8,128)(2,1)S(1)}, u32[]{:S(2)}, u32[]{:S(2)}) async-start(bf16[8,64,768]{2,1,0:T(8,128)(2,1)} %shard_map.77), calls=%async_computation | async-start | bytes 1572864 | tf_op jit(solution)/shard_map/all_to_all | solution.py:247
  24.3 4.2 %collective-permute-start = (f32[16,24]{1,0:T(8,128)S(1)}, f32[16,24]{1,0:T(8,128)S(1)}, u32[]{:S(2)}, u32[]{:S(2)}) collective-permute-start(f32[16,24]{1,0:T(8,128)S(1)} %bitcast.16), channel_id=1, source_target_pairs={{0,16},{16,0},{1,17},{17,1},{2,18},{18,2},{3,19},{19,3},{4,20},{20... | collective-permute-start | bytes 4616 | tf_op jit(solution)/shard_map/ppermute | solution.py:286
  28.5 1.1 %collective-permute-done = f32[16,24]{1,0:T(8,128)S(1)} collective-permute-done((f32[16,24]{1,0:T(8,128)S(1)}, f32[16,24]{1,0:T(8,128)S(1)}, u32[]{:S(2)}, u32[]{:S(2)}) %collective-permute-start) | collective-permute-done | bytes 1568 | tf_op jit(solution)/shard_map/ppermute | solution.py:286
  29.6 6.5 %collective-permute-start.1 = (f32[32,24]{1,0:T(8,128)S(1)}, f32[32,24]{1,0:T(8,128)S(1)}, u32[]{:S(2)}, u32[]{:S(2)}) collective-permute-start(f32[32,24]{1,0:T(8,128)S(1)} %pad_maximum_fusion.1), channel_id=1, source_target_pairs={{0,256},{256,0},{1,257},{257,1},{2,258},{258,2},{3,259},{259,3},{4... | collective-permute-start | bytes 9224 | tf_op jit(solution)/shard_map/ppermute | solution.py:287
  36.1 1.8 %collective-permute-done.1 = f32[32,24]{1,0:T(8,128)S(1)} collective-permute-done((f32[32,24]{1,0:T(8,128)S(1)}, f32[32,24]{1,0:T(8,128)S(1)}, u32[]{:S(2)}, u32[]{:S(2)}) %collective-permute-start.1) | collective-permute-done | bytes 3104 | tf_op jit(solution)/shard_map/ppermute | solution.py:287
  37.9 9.9 %all-to-all-done.arrived = bf16[8,64,768]{2,1,0:T(8,128)(2,1)S(1)} async-done(((bf16[8,64,768]{2,1,0:T(8,128)(2,1)}), bf16[8,64,768]{2,1,0:T(8,128)(2,1)S(1)}, u32[]{:S(2)}, u32[]{:S(2)}) %all-to-all-start) | async-done | bytes 786464 | tf_op jit(solution)/shard_map/all_to_all | solution.py:247
  47.8 1.7 %shard_map.79 = (bf16[8,32,512]{2,1,0:T(8,128)(2,1)}, bf16[768,128]{1,0:T(8,128)(2,1)S(1)}) custom-call(bf16[8,64,768]{2,1,0:T(8,128)(2,1)S(1)} %all-to-all-done.arrived, f32[64,24]{1,0:T(8,128)S(1)} %pad_maximum_fusion.infos), custom_call_target="tpu_custom_call" | custom-call | tf_op jit(solution)/shard_map/pallas_call | solution.py:293
  49.5 3.5 %all-to-all-start.2 = ((bf16[8,32,512]{2,1,0:T(8,128)(2,1)}), bf16[8,32,512]{2,1,0:T(8,128)(2,1)S(1)}, u32[]{:S(2)}, u32[]{:S(2)}) async-start(bf16[8,32,512]{2,1,0:T(8,128)(2,1)} %get-tuple-element.10), calls=%async_computation.2 | async-start | bytes 524288 | tf_op jit(solution)/shard_map/all_to_all | solution.py:247
  53.1 0.1 fusion
  53.2 0.1 maximum_bitcast_fusion
  53.3 0.1 copy.18.step
  53.4 0.7 shard_map.80
  54.1 10.7 %all-to-all-done.2.parts = bf16[8,32,512]{2,1,0:T(8,128)(2,1)S(1)} async-done(((bf16[8,32,512]{2,1,0:T(8,128)(2,1)}), bf16[8,32,512]{2,1,0:T(8,128)(2,1)S(1)}, u32[]{:S(2)}, u32[]{:S(2)}) %all-to-all-start.2) | async-done | bytes 262176 | tf_op jit(solution)/shard_map/all_to_all | solution.py:247
  64.8 1.5 %shard_map.81 = bf16[64,16,128]{2,1,0:T(8,128)(2,1)} custom-call(bf16[8,32,512]{2,1,0:T(8,128)(2,1)S(1)} %all-to-all-done.2.parts, f32[32,1]{1,0:T(8,128)S(1)} %copy.18.step, bf16[1024,512]{1,0:T(8,128)(2,1)S(1)} %get-tuple-element.12.picks, bf16[1024,128]{1,0:T(8,128)(2,1)S(1)} %get-tuple-element.13.base), custom_call_target="tpu_custom_call" | custom-call | tf_op jit(solution)/shard_map/pallas_call | solution.py:310
  66.3 9.7 %all-to-all-start.3 = ((bf16[64,16,128]{2,1,0:T(8,128)(2,1)}), bf16[64,16,128]{2,1,0:T(8,128)(2,1)S(1)}, u32[]{:S(2)}, u32[]{:S(2)}) async-start(bf16[64,16,128]{2,1,0:T(8,128)(2,1)} %shard_map.81), calls=%async_computation.3 | async-start | bytes 524288 | tf_op jit(solution)/shard_map/all_to_all | solution.py:247
  76.0 0.1 copy.19.radius
  76.1 5.7 %shard_map.82 = (bf16[512,1024]{1,0:T(8,128)(2,1)S(1)}, bf16[512,1024]{1,0:T(8,128)(2,1)S(1)}) custom-call(s32[1,512]{1,0:T(1,128)S(1)} %bitcast.12), custom_call_target="tpu_custom_call" | custom-call | tf_op jit(solution)/shard_map/pallas_call | solution.py:317
  81.8 7.2 %all-to-all-done.3 = bf16[64,16,128]{2,1,0:T(8,128)(2,1)S(1)} async-done(((bf16[64,16,128]{2,1,0:T(8,128)(2,1)}), bf16[64,16,128]{2,1,0:T(8,128)(2,1)S(1)}, u32[]{:S(2)}, u32[]{:S(2)}) %all-to-all-start.3) | async-done | bytes 262176 | tf_op jit(solution)/shard_map/all_to_all | solution.py:247
  89.0 1.3 %shard_map.83 = (f32[16,64]{1,0:T(8,128)}, f32[2,12,1,1024]{3,2,1,0:T(1,128)}) custom-call(bf16[2,32,16,128]{3,2,1,0:T(8,128)(2,1)S(1)} %bitcast.11, bf16[512,1024]{1,0:T(8,128)(2,1)S(1)} %get-tuple-element.14.cosines, bf16[512,1024]{1,0:T(8,128)(2,1)S(1)} %get-tuple-element.15.sines, f32[1,512]{1,0:T(1,128)S(1)} %bitcast.13, f32[12,1]{1,0:T(8,128)S(1)} %copy.19.radius), custom_call_target="tpu_custom_call" | custom-call | tf_op jit(solution)/shard_map/pallas_call | solution.py:318
  (7 shorter events, 0.0 us)
Async XLA Ops:
  2.0 15.6 %all-to-all-start.1 = ((f32[16,1,24]{2,1,0:T(1,128)}), f32[16,1,24]{2,1,0:T(1,128)S(1)}, u32[]{:S(2)}, u32[]{:S(2)}) async-start(f32[16,1,24]{2,1,0:T(1,128)} %shard_map.78), calls=%async_computation.1 | async-start | bytes 16384 | tf_op jit(solution)/shard_map/all_to_all | solution.py:247
  16.8 36.2 %copy-start = (s32[512]{0:T(512)S(1)}, s32[512]{0:T(512)}, u32[]{:S(2)}) copy-start(s32[512]{0:T(512)} %orders.1) | copy-start | bytes 6148
  17.6 30.3 %all-to-all-start = ((bf16[8,64,768]{2,1,0:T(8,128)(2,1)}), bf16[8,64,768]{2,1,0:T(8,128)(2,1)S(1)}, u32[]{:S(2)}, u32[]{:S(2)}) async-start(bf16[8,64,768]{2,1,0:T(8,128)(2,1)} %shard_map.77), calls=%async_computation | async-start | bytes 1572864 | tf_op jit(solution)/shard_map/all_to_all | solution.py:247
  24.3 5.3 %collective-permute-start = (f32[16,24]{1,0:T(8,128)S(1)}, f32[16,24]{1,0:T(8,128)S(1)}, u32[]{:S(2)}, u32[]{:S(2)}) collective-permute-start(f32[16,24]{1,0:T(8,128)S(1)} %bitcast.16), channel_id=1, source_target_pairs={{0,16},{16,0},{1,17},{17,1},{2,18},{18,2},{3,19},{19,3},{4,20},{20... | collective-permute-start | bytes 4616 | tf_op jit(solution)/shard_map/ppermute | solution.py:286
  29.6 8.4 %collective-permute-start.1 = (f32[32,24]{1,0:T(8,128)S(1)}, f32[32,24]{1,0:T(8,128)S(1)}, u32[]{:S(2)}, u32[]{:S(2)}) collective-permute-start(f32[32,24]{1,0:T(8,128)S(1)} %pad_maximum_fusion.1), channel_id=1, source_target_pairs={{0,256},{256,0},{1,257},{257,1},{2,258},{258,2},{3,259},{259,3},{4... | collective-permute-start | bytes 9224 | tf_op jit(solution)/shard_map/ppermute | solution.py:287
  49.5 26.4 %copy-start.1 = (s32[1,12]{1,0:T(1,128)S(1)}, s32[1,12]{1,0:T(1,128)}, u32[]{:S(2)}) copy-start(s32[1,12]{1,0:T(1,128)} %rows.1) | copy-start | bytes 148
  49.5 15.3 %all-to-all-start.2 = ((bf16[8,32,512]{2,1,0:T(8,128)(2,1)}), bf16[8,32,512]{2,1,0:T(8,128)(2,1)S(1)}, u32[]{:S(2)}, u32[]{:S(2)}) async-start(bf16[8,32,512]{2,1,0:T(8,128)(2,1)} %get-tuple-element.10), calls=%async_computation.2 | async-start | bytes 524288 | tf_op jit(solution)/shard_map/all_to_all | solution.py:247
  66.3 22.7 %all-to-all-start.3 = ((bf16[64,16,128]{2,1,0:T(8,128)(2,1)}), bf16[64,16,128]{2,1,0:T(8,128)(2,1)S(1)}, u32[]{:S(2)}, u32[]{:S(2)}) async-start(bf16[64,16,128]{2,1,0:T(8,128)(2,1)} %shard_map.81), calls=%async_computation.3 | async-start | bytes 524288 | tf_op jit(solution)/shard_map/all_to_all | solution.py:247

commit v5 on v4

--- a/solution.py
+++ b/solution.py
@@ -131,34 +131,8 @@
         sines[:, at] = (-sine * turn_cos - cosine * turn_sin).astype(BF16)
 
 
-def column_kernel(arrived, infos, copies, stacked):
-    lats = arrived.shape[1]
-    levels_n = infos.shape[1] // 2
-    width = arrived.shape[2] // levels_n
-    total = arrived[0].astype(F32)
-    for d in range(1, arrived.shape[0]):
-        total += arrived[d].astype(F32)
-    points = jnp.concatenate(
-        [total[:, r * width : (r + 1) * width] for r in range(levels_n)], axis=0
-    ).astype(BF16)
-    stacked[...] = jnp.concatenate([jnp.zeros_like(points), points], axis=1)
-    half = width // 2
-    exact = points.astype(F32)
-    buoyancy = exact[:, :half] - COMPOSITION_WEIGHT * exact[:, half:]
-    info = in_place(infos[...])
-    rows = jnp.concatenate([info[:, r : r + 1] for r in range(levels_n)], axis=0)
-    weight = jnp.concatenate([info[:, r : r + 1] for r in range(levels_n, 2 * levels_n)], axis=0)
-    weighted = buoyancy * weight
-    high = weighted.astype(BF16)
-    low = (weighted - high.astype(F32)).astype(BF16)
-    onehot = matches(rows, iota((lats * levels_n, NS), 1).astype(F32))
-    both = dot_dims(jnp.concatenate([high, low], axis=1), onehot, 0, 0)
-    column = (both[:half] + both[half:]).astype(BF16)
-    copies[...] = jnp.broadcast_to(column[None], copies.shape)
-
-
-def message_kernel(per, stacked, infos, base, picks):
-    lats = base.shape[0] // per
+def choice_kernel(per, infos, picks):
+    lats = infos.shape[0]
     levels_n = infos.shape[1] // 2
     info = in_place(infos[...])
     q = iota((per, info.shape[1]), 0)
@@ -169,11 +143,35 @@
     ]
     absent = iota((lats * per, 1), 0) % per >= levels_n
     row = jnp.where(absent, -1.0, jnp.concatenate(wanted, axis=0))
-    picks[...] = matches(row, iota((lats * per, NS), 1).astype(F32))
-    count = stacked.shape[0]
-    point = iota((1, count), 1)
-    code = point % lats * per + point // lats
-    base[...] = dot(matches(iota((lats * per, count), 0), code), stacked[...]).astype(BF16)
+    picks[...] = matches(row, iota(picks.shape, 1).astype(F32))
+
+
+def column_kernel(per, arrived, infos, copies, base):
+    lats = arrived.shape[1]
+    levels_n = infos.shape[1] // 2
+    width = arrived.shape[2] // levels_n
+    total = arrived[0].astype(F32)
+    for d in range(1, arrived.shape[0]):
+        total += arrived[d].astype(F32)
+    points = jnp.concatenate(
+        [total[:, r * width : (r + 1) * width] for r in range(levels_n)], axis=0
+    ).astype(BF16)
+    info = in_place(infos[...])
+    rows = jnp.concatenate([info[:, r : r + 1] for r in range(levels_n)], axis=0)
+    weight = jnp.concatenate([info[:, r : r + 1] for r in range(levels_n, 2 * levels_n)], axis=0)
+    onehot = matches(rows, iota((lats * levels_n, NS), 1).astype(F32))
+    half = width // 2
+    exact = points.astype(F32)
+    weighted = (exact[:, :half] - COMPOSITION_WEIGHT * exact[:, half:]) * weight
+    high = weighted.astype(BF16)
+    low = (weighted - high.astype(F32)).astype(BF16)
+    both = dot_dims(jnp.concatenate([high, low], axis=1), onehot, 0, 0)
+    column = (both[:half] + both[half:]).astype(BF16)
+    copies[...] = jnp.broadcast_to(column[None], copies.shape)
+    stacked = jnp.concatenate([jnp.zeros_like(points), points], axis=1)
+    point = iota((1, lats * levels_n), 1)
+    places = matches(iota((lats * per, 1), 0), point % lats * per + point // lats)
+    base[...] = dot(places, stacked).astype(BF16)
 
 
 def select_kernel(levels_n, parts, step, picks, base, out):
@@ -181,7 +179,9 @@
     for d in range(1, parts.shape[0]):
         column += parts[d].astype(F32)
     half = column.shape[0] // 2
-    outward = step[...] * jnp.concatenate([column[half:], column[:half]], axis=0)
+    outward = as_column(step[...], step.shape[1]) * jnp.concatenate(
+        [column[half:], column[:half]], axis=0
+    )
     at = iota(column.shape, 1)
     after = jnp.where(at == NS - 1, 0.0, pltpu.roll(column, NS - 1, axis=1))
     before = jnp.where(at == 0, 0.0, pltpu.roll(column, 1, axis=1))
@@ -190,15 +190,13 @@
     points = jnp.concatenate([outward, around, zeros, zeros], axis=0).astype(BF16)
     group = at // 4 % 4
     rows = jnp.concatenate([jnp.where(group == g, column, 0.0) for g in range(4)], axis=0)
+    chosen = dot_dims(picks[...], points, 1, 1)
     per = out.shape[1]
     own = per - levels_n
-    count = picks.shape[0]
+    message = iota((picks.shape[0], 1), 0)
+    level = message % per
+    code = jnp.where(level >= levels_n, message // per % (NS // per) * own + level - levels_n, -1)
     s = iota((1, NS), 1)
-    n_ma = NS // per
-    message = iota((count, 1), 0)
-    q = message % per
-    code = jnp.where(q >= levels_n, message // per % n_ma * own + q - levels_n, -1)
-    chosen = dot_dims(picks[...], points, 1, 1)
     chosen += dot_dims(matches(code, s // per * own + s % own), rows.astype(BF16), 1, 1)
     chosen += base[...].astype(F32)
     out[...] = chosen.astype(BF16).reshape(out.shape)
@@ -223,7 +221,7 @@
         sides.append(jnp.concatenate(by_part[i] + turned, axis=0))
     result = dot(sides[0], cosines[...]) + dot(sides[1], sines[...])
     rows = [result[g * per : g * per + levels_n] for g in range(6)]
-    inverse = 1.0 / radius[...]
+    inverse = 1.0 / as_column(radius[...], levels_n)
     outward = rows[0] * (0.5 * inverse)
     around = -0.5 * rows[1]
     held = [x.astype(BF16).astype(F32) for x in rows[2:]]
@@ -287,34 +285,35 @@
     infos = jnp.concatenate([info, lax.ppermute(info, "half", swap)], axis=0)
     my_orders = lax.dynamic_slice_in_dim(order_table, me_ma * slots, slots)
     step = 2.0 * jnp.sin(my_orders.astype(F32) * (2.0 * math.pi / NPHI))
-    step = jnp.concatenate([-step, step]).reshape(2 * slots, 1)
+    step = jnp.concatenate([-step, step]).reshape(1, -1)
     slope = (order_table.astype(F32) / NS).reshape(1, -1)
-    radius = (0.35 + 0.65 * (cylinder_row.astype(F32) + 0.5) / NS).reshape(levels_n, 1)
-    copies, stacked = vmem_call(
-        column_kernel,
+    radius = (0.35 + 0.65 * (cylinder_row.astype(F32) + 0.5) / NS).reshape(1, -1)
+    table = jax.ShapeDtypeStruct((lats, NPHI), BF16)
+    cosines, sines = vmem_call(table_kernel, (table, table), 0, 1)(order_table.reshape(1, -1))
+    messages = lat_block * row_block
+    picks = vmem_call(
+        functools.partial(choice_kernel, row_block),
+        jax.ShapeDtypeStruct((messages, NS), BF16),
+        0, 1,
+    )(infos)
+    arrived, cosines, sines, step, slope, radius, infos, picks = lax.optimization_barrier(
+        (arrived, cosines, sines, step, slope, radius, infos, picks)
+    )
+    copies, base = vmem_call(
+        functools.partial(column_kernel, row_block),
         (
-            pltpu.HBM((n_z, 2 * slots, NS), BF16),
-            jax.ShapeDtypeStruct((levels_n * lat_block, LANES), BF16),
+            jax.ShapeDtypeStruct((n_z, 2 * slots, NS), BF16),
+            jax.ShapeDtypeStruct((messages, LANES), BF16),
         ),
         0, 2,
     )(arrived, infos)
     partials = exchanged(copies, "z")
-    base, picks = vmem_call(
-        functools.partial(message_kernel, row_block),
-        (
-            jax.ShapeDtypeStruct((lat_block * row_block, LANES), BF16),
-            jax.ShapeDtypeStruct((lat_block * row_block, NS), BF16),
-        ),
-        0, 2,
-    )(stacked, infos)
     chosen = vmem_call(
         functools.partial(select_kernel, levels_n),
-        pltpu.HBM((lat_block, row_block, LANES), BF16),
+        jax.ShapeDtypeStruct((lat_block, row_block, LANES), BF16),
         0, 4,
     )(partials, step, picks, base)
     got = exchanged(chosen, ("half", *MA)).reshape(n_half, n_ma, row_block, LANES)
-    table = jax.ShapeDtypeStruct((lats, NPHI), BF16)
-    cosines, sines = vmem_call(table_kernel, (table, table), 0, 1)(order_table.reshape(1, -1))
     owned, advected = vmem_call(
         functools.partial(advect_kernel, levels_n, slots),
         (

time: 90.8 us -> 88.8 us (0.978)
  blocking collectives: 0 us -> 37.1 us
  waiting for transfers between devices: 31.5 us -> 6.03 us
  starting transfers between devices: 40.7 us -> 27.5 us
  Pallas kernels: 16.9 us -> 15.8 us
    all_to_all x0 -> x2, blocking collectives: none -> 37.1 us  [exchanged(): return lax.all_to_all(blocks, axis, split_axis=0, concat_axis=0, tiled=True)]
    all_to_all x4 -> x2, waiting for transfers between devices: 28.6 us -> 5.08 us  [exchanged(): return lax.all_to_all(blocks, axis, split_axis=0, concat_axis=0, tiled=True)]
    all_to_all x4 -> x2, starting transfers between devices: 30 us -> 16.8 us  [exchanged(): return lax.all_to_all(blocks, axis, split_axis=0, concat_axis=0, tiled=True)]
    ppermute x1, waiting for transfers between devices: 1.83 us -> 0.01 us  [on_device(): infos = jnp.concatenate([info, lax.ppermute(info, 'half', swap)], axis=0)]
    pallas_call x3, Pallas kernels: 3.85 us -> 2.6 us  [the longest x1 1.42 us: on_device(): vmem_call(functools.partial(column_kernel, row_block), (jax.ShapeDtypeStr...]
    unnamed x4 -> x8, local copies, waits for them, and re-layouts: 0.01 us -> 0.98 us
  transfers between devices with their start and end apart: 6 -> 4, of which waited for: 6 -> 3; matrix products, arithmetic and copies ran while one was open for 0% -> 0% of each run, Pallas kernels for 12% -> 12%
where the time goes in v5:
time: 88.8 us; the launch traced here: 88.4 us
  blocking collectives  37.1 us (42%)
  starting transfers between devices  27.5 us (31%)
  Pallas kernels  15.8 us (18%)
  waiting for transfers between devices  6.03 us (7%)
  local copies, waits for them, and re-layouts  0.98 us (1%)
    all_to_all x2, blocking collectives, exchanged(): return lax.all_to_all(blocks, axis, split_axis=0, concat_axis=0, tiled=True)  37.1 us
    all_to_all x2, starting transfers between devices, exchanged(): return lax.all_to_all(blocks, axis, split_axis=0, concat_axis=0, tiled=True)  16.8 us
    ppermute x1, starting transfers between devices, on_device(): infos = jnp.concatenate([info, lax.ppermute(info, 'half', swap)], axis=0)  6.54 us
    pallas_call x1, Pallas kernels, on_device(): vmem_call(table_kernel, (table, table), 0, 1)(order_table.reshape(1, -1))  5.69 us
    all_to_all x2, waiting for transfers between devices, exchanged(): return lax.all_to_all(blocks, axis, split_axis=0, concat_axis=0, tiled=True)  5.08 us
    pallas_call x1, Pallas kernels, on_device(): vmem_call(functools.partial(contribution_kernel, slots, degrees, n_half),...  4.88 us
    ppermute x1, starting transfers between devices, on_device(): info = jnp.concatenate([info, lax.ppermute(info, 'pair', swap)], axis=0)  4.22 us
  transfers between devices with their start and end apart: 4, of which 3 were waited for; matrix products, arithmetic and copies ran while one was open for 0% of the time, Pallas kernels for 12%

profile of v5, /device:TPU:1, one launch (start us, length us, event | category | flops | bytes accessed | tf_op | source)
XLA Modules:
  0.0 88.4 jit_solution(11666032946028275338)
XLA Ops:
  0.6 1.3 %shard_map.79 = f32[16,1,24]{2,1,0:T(1,128)} custom-call(s32[1,12]{1,0:T(1,128)} %rows.1, f32[1,12]{1,0:T(1,128)} %weights.1), custom_call_target="tpu_custom_call" | custom-call | tf_op jit(solution)/shard_map/pallas_call | solution.py:262
  2.0 10.1 %all-to-all-start.1 = ((f32[16,1,24]{2,1,0:T(1,128)}), f32[16,1,24]{2,1,0:T(1,128)S(1)}, u32[]{:S(2)}, u32[]{:S(2)}) async-start(f32[16,1,24]{2,1,0:T(1,128)} %shard_map.79), calls=%async_computation.1 | async-start | bytes 16384 | tf_op jit(solution)/shard_map/all_to_all | solution.py:245
  12.1 0.0 copy-start.2
  12.1 4.9 %shard_map.77 = bf16[8,64,768]{2,1,0:T(8,128)(2,1)} custom-call(s32[512]{0:T(512)} %orders.1, bf16[12,384]{1,0:T(8,128)(2,1)} %radial.1, bf16[4,512,384]{2,1,0:T(8,128)(2,1)} %bitcast.12, bf16[512,512]{1,0:T(8,128)(2,1)} %bitcast.13), custom_call_target="tpu_custom_call" | custom-call | tf_op jit(solution)/shard_map/pallas_call | solution.py:268
  17.0 0.6 all-to-all-done.1
  17.6 6.7 %all-to-all-start = ((bf16[8,64,768]{2,1,0:T(8,128)(2,1)}), bf16[8,64,768]{2,1,0:T(8,128)(2,1)S(1)}, u32[]{:S(2)}, u32[]{:S(2)}) async-start(bf16[8,64,768]{2,1,0:T(8,128)(2,1)} %shard_map.77), calls=%async_computation | async-start | bytes 1572864 | tf_op jit(solution)/shard_map/all_to_all | solution.py:245
  24.3 0.0 copy-done.3
  24.3 0.0 copy-done.2
  24.3 4.2 %collective-permute-start = (f32[16,24]{1,0:T(8,128)S(1)}, f32[16,24]{1,0:T(8,128)S(1)}, u32[]{:S(2)}, u32[]{:S(2)}) collective-permute-start(f32[16,24]{1,0:T(8,128)S(1)} %bitcast.14), channel_id=1, source_target_pairs={{0,16},{16,0},{1,17},{17,1},{2,18},{18,2},{3,19},{19,3},{4,20},{20... | collective-permute-start | bytes 4616 | tf_op jit(solution)/shard_map/ppermute | solution.py:284
  28.5 0.1 fusion
  28.6 0.9 %collective-permute-done = f32[16,24]{1,0:T(8,128)S(1)} collective-permute-done((f32[16,24]{1,0:T(8,128)S(1)}, f32[16,24]{1,0:T(8,128)S(1)}, u32[]{:S(2)}, u32[]{:S(2)}) %collective-permute-start) | collective-permute-done | bytes 1568 | tf_op jit(solution)/shard_map/ppermute | solution.py:284
  29.6 6.5 %collective-permute-start.1 = (f32[32,24]{1,0:T(8,128)S(1)}, f32[32,24]{1,0:T(8,128)S(1)}, u32[]{:S(2)}, u32[]{:S(2)}) collective-permute-start(f32[32,24]{1,0:T(8,128)S(1)} %pad_maximum_fusion.1), channel_id=1, source_target_pairs={{0,256},{256,0},{1,257},{257,1},{2,258},{258,2},{3,259},{259,3},{4... | collective-permute-start | bytes 9224 | tf_op jit(solution)/shard_map/ppermute | solution.py:285
  36.2 0.1 maximum_bitcast_fusion.step
  36.2 5.7 %shard_map.78 = (bf16[512,1024]{1,0:T(8,128)(2,1)S(1)}, bf16[512,1024]{1,0:T(8,128)(2,1)S(1)}) custom-call(s32[1,512]{1,0:T(1,128)S(1)} %bitcast.10), custom_call_target="tpu_custom_call" | custom-call | tf_op jit(solution)/shard_map/pallas_call | solution.py:292
  41.9 0.0 copy-start
  41.9 1.0 %copy-done = bf16[512,1024]{1,0:T(8,128)(2,1)} copy-done((bf16[512,1024]{1,0:T(8,128)(2,1)}, bf16[512,1024]{1,0:T(8,128)(2,1)S(1)}, u32[]{:S(2)}) %copy-start) | copy-done | bytes 1048600
  42.9 0.0 collective-permute-done.1
  42.9 0.4 shard_map.80.picks
  43.4 4.5 %all-to-all-done.arrived = bf16[8,64,768]{2,1,0:T(8,128)(2,1)S(1)} async-done(((bf16[8,64,768]{2,1,0:T(8,128)(2,1)}), bf16[8,64,768]{2,1,0:T(8,128)(2,1)S(1)}, u32[]{:S(2)}, u32[]{:S(2)}) %all-to-all-start) | async-done | bytes 786464 | tf_op jit(solution)/shard_map/all_to_all | solution.py:245
  47.8 1.4 %shard_map.81 = (bf16[8,32,512]{2,1,0:T(8,128)(2,1)S(1)}, bf16[1024,128]{1,0:T(8,128)(2,1)S(1)}) custom-call(bf16[8,64,768]{2,1,0:T(8,128)(2,1)S(1)} %all-to-all-done.arrived, f32[64,24]{1,0:T(8,128)S(1)} %pad_maximum_fusion.infos), custom_call_target="tpu_custom_call" | custom-call | tf_op jit(solution)/shard_map/pallas_call | solution.py:302
  49.3 12.0 %all_to_all.20.parts = bf16[8,32,512]{2,1,0:T(8,128)(2,1)S(1)} all-to-all(bf16[8,32,512]{2,1,0:T(8,128)(2,1)S(1)} %get-tuple-element.20), channel_id=1, replica_groups=mesh['half'=2,'z'=8,'pair'=2,'y'=2,'x'=4,'core'=2] {'z'}, dimensions={0} | all-to-all | bytes 524288 | tf_op jit(solution)/shard_map/all_to_all | solution.py:245
  61.2 0.8 shard_map.82
  62.0 25.1 %all_to_all.21 = bf16[64,16,128]{2,1,0:T(8,128)(2,1)S(1)} all-to-all(bf16[64,16,128]{2,1,0:T(8,128)(2,1)S(1)} %shard_map.82), channel_id=1, replica_groups=mesh['half'=2,'z'=8,'pair'=2,'y'=2,'x'=4,'core'=2] {'half','pair','y','x..., dimensions={0} | all-to-all | bytes 524288 | tf_op jit(solution)/shard_map/all_to_all | solution.py:245
  87.1 1.3 %shard_map.83 = (f32[16,64]{1,0:T(8,128)}, f32[2,12,1,1024]{3,2,1,0:T(1,128)}) custom-call(bf16[2,32,16,128]{3,2,1,0:T(8,128)(2,1)S(1)} %bitcast.9, bf16[512,1024]{1,0:T(8,128)(2,1)S(1)} %get-tuple-element.24.cosines, bf16[512,1024]{1,0:T(8,128)(2,1)S(1)} %copy-done.1, f32[1,512]{1,0:T(1,128)S(1)} %bitcast.11, f32[1,12]{1,0:T(1,128)S(1)} %multiply_add_fusion.radius), custom_call_target="tpu_custom_call" | custom-call | tf_op jit(solution)/shard_map/pallas_call | solution.py:317
  (7 shorter events, 0.0 us)
Async XLA Ops:
  2.0 15.6 %all-to-all-start.1 = ((f32[16,1,24]{2,1,0:T(1,128)}), f32[16,1,24]{2,1,0:T(1,128)S(1)}, u32[]{:S(2)}, u32[]{:S(2)}) async-start(f32[16,1,24]{2,1,0:T(1,128)} %shard_map.79), calls=%async_computation.1 | async-start | bytes 16384 | tf_op jit(solution)/shard_map/all_to_all | solution.py:245
  12.1 12.2 %copy-start.3 = (s32[1,12]{1,0:T(1,128)S(1)}, s32[1,12]{1,0:T(1,128)}, u32[]{:S(2)}) copy-start(s32[1,12]{1,0:T(1,128)} %rows.1) | copy-start | bytes 148
  12.1 12.2 %copy-start.2 = (s32[512]{0:T(512)S(1)}, s32[512]{0:T(512)}, u32[]{:S(2)}) copy-start(s32[512]{0:T(512)} %orders.1) | copy-start | bytes 6148
  17.6 30.3 %all-to-all-start = ((bf16[8,64,768]{2,1,0:T(8,128)(2,1)}), bf16[8,64,768]{2,1,0:T(8,128)(2,1)S(1)}, u32[]{:S(2)}, u32[]{:S(2)}) async-start(bf16[8,64,768]{2,1,0:T(8,128)(2,1)} %shard_map.77), calls=%async_computation | async-start | bytes 1572864 | tf_op jit(solution)/shard_map/all_to_all | solution.py:245
  24.3 5.3 %collective-permute-start = (f32[16,24]{1,0:T(8,128)S(1)}, f32[16,24]{1,0:T(8,128)S(1)}, u32[]{:S(2)}, u32[]{:S(2)}) collective-permute-start(f32[16,24]{1,0:T(8,128)S(1)} %bitcast.14), channel_id=1, source_target_pairs={{0,16},{16,0},{1,17},{17,1},{2,18},{18,2},{3,19},{19,3},{4,20},{20... | collective-permute-start | bytes 4616 | tf_op jit(solution)/shard_map/ppermute | solution.py:284
  29.6 13.3 %collective-permute-start.1 = (f32[32,24]{1,0:T(8,128)S(1)}, f32[32,24]{1,0:T(8,128)S(1)}, u32[]{:S(2)}, u32[]{:S(2)}) collective-permute-start(f32[32,24]{1,0:T(8,128)S(1)} %pad_maximum_fusion.1), channel_id=1, source_target_pairs={{0,256},{256,0},{1,257},{257,1},{2,258},{258,2},{3,259},{259,3},{4... | collective-permute-start | bytes 9224 | tf_op jit(solution)/shard_map/ppermute | solution.py:285
  41.9 1.0 %copy-start = (bf16[512,1024]{1,0:T(8,128)(2,1)}, bf16[512,1024]{1,0:T(8,128)(2,1)S(1)}, u32[]{:S(2)}) copy-start(bf16[512,1024]{1,0:T(8,128)(2,1)S(1)} %get-tuple-element.25.sines) | copy-start | bytes 3145732
  49.3 37.8 %copy-start.1 = (bf16[512,1024]{1,0:T(8,128)(2,1)S(1)}, bf16[512,1024]{1,0:T(8,128)(2,1)}, u32[]{:S(2)}) copy-start(bf16[512,1024]{1,0:T(8,128)(2,1)} %copy-done) | copy-start | bytes 3145732

commit v6 on v5

--- a/solution.py
+++ b/solution.py
@@ -41,14 +41,14 @@
     return lax.dot_general(x, y, (((dim_x,), (dim_y,)), ((), ())), preferred_element_type=F32)
 
 
-def vmem_call(body, outs, n_smem, n_vmem, n_hbm=0, scratch=()):
+def vmem_call(body, outs, n_smem, n_vmem, n_hbm=0, scratch=(), out_space=pltpu.VMEM):
     return pl.pallas_call(
         body,
         out_shape=outs,
         in_specs=[pl.BlockSpec(memory_space=pltpu.SMEM)] * n_smem
         + [pl.BlockSpec(memory_space=pltpu.VMEM)] * n_vmem
         + [pl.BlockSpec(memory_space=pltpu.HBM)] * n_hbm,
-        out_specs=jax.tree.map(lambda _: pl.BlockSpec(memory_space=pltpu.VMEM), outs),
+        out_specs=jax.tree.map(lambda _: pl.BlockSpec(memory_space=out_space), outs),
         scratch_shapes=scratch,
         compiler_params=pltpu.CompilerParams(vmem_limit_bytes=VMEM_LIMIT),
     )
@@ -73,15 +73,28 @@
 
 
 def contribution_kernel(
-    slots, degrees, halves, orders, radial, spectrum_in, legendre_in, out, spectrum, legendre, sems
+    slots, degrees, halves, orders, radial, spectrum_in, legendre_in, out,
+    spectrum, legendre, turned, held, sems, outs
 ):
     parts = spectrum.shape[0]
+    ways = sems.shape[1]
+    step = spectrum.shape[1] // ways
+    sides = [(legendre_in, legendre)] + [(spectrum_in.at[c], spectrum.at[c]) for c in range(parts)]
     copies = [
-        pltpu.make_async_copy(spectrum_in.at[c], spectrum.at[c], sems.at[c]) for c in range(parts)
+        [
+            pltpu.make_async_copy(
+                source.at[pl.ds(w * step, step)], target.at[pl.ds(w * step, step)], sems.at[c, w]
+            )
+            for w in range(ways)
+        ]
+        for c, (source, target) in enumerate(sides)
     ]
-    copies.append(pltpu.make_async_copy(legendre_in, legendre, sems.at[parts]))
-    for copy in copies:
-        copy.start()
+    for some in copies:
+        for copy in some:
+            copy.start()
+    for copy in copies[0]:
+        copy.wait()
+    turned[...] = jnp.transpose(legendre[...])
     levels_n = radial.shape[0]
     columns = levels_n * parts
     width = columns * slots
@@ -92,7 +105,8 @@
     levels = jnp.zeros((rows, columns), F32)
     for c in range(parts):
         table = jnp.where(part_of == c, repeated, 0.0).astype(BF16)
-        copies[c].wait()
+        for copy in copies[c + 1]:
+            copy.wait()
         levels += dot_dims(spectrum[c], table, 1, 1)
     spread = (iota((columns, width), 0) == iota((columns, width), 1) // slots).astype(BF16)
     expanded = dot(levels.astype(BF16), spread)
@@ -104,28 +118,36 @@
         kept = (slot_of_lane == k) & (degree >= orders[first_slot + k])
         blocks.append(jnp.where(kept, expanded[k * degrees : (k + 1) * degrees], 0.0).astype(BF16))
     diagonal = jnp.concatenate(blocks, axis=0)
-    copies[parts].wait()
-    total = dot_dims(legendre[...], diagonal, 0, 0).astype(BF16)
     n_z, lats, _ = out.shape
     block = lats // halves
-    for h in range(halves):
-        for z in range(n_z):
-            at_lat = (h * n_z + z) * block
-            out[z, h * block : (h + 1) * block] = total[at_lat : at_lat + block]
+    group = LANES // block
+    writes = []
+    for first in range(0, halves * n_z, group):
+        lanes = slice(first * block, (first + group) * block)
+        held[lanes] = dot(turned[lanes], diagonal).astype(BF16)
+        for g in range(first, first + group):
+            h, z = divmod(g, n_z)
+            write = pltpu.make_async_copy(
+                held.at[pl.ds(g * block, block)], out.at[z, pl.ds(h * block, block)], outs.at[g]
+            )
+            write.start()
+            writes.append(write)
+    for write in writes:
+        write.wait()
 
 
 def table_kernel(orders, cosines, sines):
     count = orders.shape[1]
     order = jnp.broadcast_to(as_column(orders[...], count), (count, LANES))
-    angle = (order * iota((count, LANES), 1) % NPHI).astype(F32) * (2.0 * math.pi / NPHI)
+    angle = (order * iota((count, LANES), 1) & (NPHI - 1)).astype(F32) * (2.0 * math.pi / NPHI)
     weight = jnp.where(order == 0, 1.0, 2.0).astype(F32) / math.sqrt(NS)
     cosine, sine = jnp.cos(angle) * weight, jnp.sin(angle) * weight
     half_root = math.sqrt(0.5)
     for j in range(NPHI // LANES):
-        eighth = order * j % 8
-        size = jnp.where(eighth % 2 == 1, half_root, 1.0)
-        turn_cos = jnp.where(eighth % 4 == 2, 0.0, jnp.where((eighth >= 3) & (eighth <= 5), -size, size))
-        turn_sin = jnp.where(eighth % 4 == 0, 0.0, jnp.where(eighth > 4, -size, size))
+        eighth = order * j & 7
+        size = jnp.where(eighth & 1 == 1, half_root, 1.0)
+        turn_cos = jnp.where(eighth & 3 == 2, 0.0, jnp.where((eighth >= 3) & (eighth <= 5), -size, size))
+        turn_sin = jnp.where(eighth & 3 == 0, 0.0, jnp.where(eighth > 4, -size, size))
         at = slice(j * LANES, (j + 1) * LANES)
         cosines[:, at] = (cosine * turn_cos - sine * turn_sin).astype(BF16)
         sines[:, at] = (-sine * turn_cos - cosine * turn_sin).astype(BF16)
@@ -258,7 +280,7 @@
     me_ma = lax.axis_index(MA)
     swap = [(0, 1), (1, 0)]
 
-    near = ("y", "x", "core")
+    near = ("y", "x")
     info = vmem_call(
         info_kernel,
         pltpu.HBM((lax.axis_size(near), 1, 2 * levels_n), F32),
@@ -272,8 +294,12 @@
         (
             pltpu.VMEM((parts, slots * degrees, modes), BF16),
             pltpu.VMEM((slots * degrees, lats), BF16),
-            pltpu.SemaphoreType.DMA((parts + 1,)),
+            pltpu.VMEM((lats, slots * degrees), BF16),
+            pltpu.VMEM((lats, levels_n * parts * slots), BF16),
+            pltpu.SemaphoreType.DMA((parts + 1, 4)),
+            pltpu.SemaphoreType.DMA((n_half * n_z,)),
         ),
+        pltpu.HBM,
     )(
         in_hbm(order_table),
         in_hbm(radial_table),
@@ -281,6 +307,7 @@
         in_hbm(legendre.reshape(slots * degrees, lats)),
     )
     arrived = exchanged(contribution, "z")
+    info = lax.all_gather(info, "core", axis=1).reshape(-1, 2 * levels_n)
     info = jnp.concatenate([info, lax.ppermute(info, "pair", swap)], axis=0)
     infos = jnp.concatenate([info, lax.ppermute(info, "half", swap)], axis=0)
     my_orders = lax.dynamic_slice_in_dim(order_table, me_ma * slots, slots)

time: 88.8 us -> 87.9 us (0.990)
  blocking collectives: 37.1 us -> 43.2 us
  waiting for transfers between devices: 6.03 us -> 1.37 us
  Pallas kernels: 15.8 us -> 14.3 us
  starting transfers between devices: 27.5 us -> 26.6 us
    all_to_all x2, waiting for transfers between devices: 5.08 us -> 0.13 us  [exchanged(): return lax.all_to_all(blocks, axis, split_axis=0, concat_axis=0, tiled=True)]
    all_gather x0 -> x1, blocking collectives: none -> 3.85 us  [on_device(): info = lax.all_gather(info, 'core', axis=1).reshape(-1, 2 * levels_n)]
    all_to_all x2, blocking collectives: 37.1 us -> 39.3 us  [exchanged(): return lax.all_to_all(blocks, axis, split_axis=0, concat_axis=0, tiled=True)]
    pallas_call x1, Pallas kernels: 5.69 us -> 4.27 us  [on_device(): vmem_call(table_kernel, (table, table), 0, 1)(order_table.reshape(1, -1))]
    all_to_all x2, starting transfers between devices: 16.8 us -> 15.9 us  [exchanged(): return lax.all_to_all(blocks, axis, split_axis=0, concat_axis=0, tiled=True)]
  transfers between devices with their start and end apart: 4 -> 4, of which waited for: 3 -> 2; matrix products, arithmetic and copies ran while one was open for 0% -> 0% of each run, Pallas kernels for 12% -> 11%
where the time goes in v6:
time: 87.9 us; the launch traced here: 87.4 us
  blocking collectives  43.2 us (49%)
  starting transfers between devices  26.6 us (30%)
  Pallas kernels  14.3 us (16%)
  waiting for transfers between devices  1.37 us (2%)
  local copies, waits for them, and re-layouts  0.99 us (1%)
    all_to_all x2, blocking collectives, exchanged(): return lax.all_to_all(blocks, axis, split_axis=0, concat_axis=0, tiled=True)  39.3 us
    all_to_all x2, starting transfers between devices, exchanged(): return lax.all_to_all(blocks, axis, split_axis=0, concat_axis=0, tiled=True)  15.9 us
    ppermute x1, starting transfers between devices, on_device(): infos = jnp.concatenate([info, lax.ppermute(info, 'half', swap)], axis=0)  6.54 us
    pallas_call x1, Pallas kernels, on_device(): vmem_call(functools.partial(contribution_kernel, slots, degrees, n_half),...  4.81 us
    pallas_call x1, Pallas kernels, on_device(): vmem_call(table_kernel, (table, table), 0, 1)(order_table.reshape(1, -1))  4.27 us
    ppermute x1, starting transfers between devices, on_device(): info = jnp.concatenate([info, lax.ppermute(info, 'pair', swap)], axis=0)  4.21 us
    all_gather x1, blocking collectives, on_device(): info = lax.all_gather(info, 'core', axis=1).reshape(-1, 2 * levels_n)  3.85 us
  transfers between devices with their start and end apart: 4, of which 2 were waited for; matrix products, arithmetic and copies ran while one was open for 0% of the time, Pallas kernels for 11%

profile of v6, /device:TPU:1, one launch (start us, length us, event | category | flops | bytes accessed | tf_op | source)
XLA Modules:
  0.0 87.4 jit_solution(8002297538685658910)
XLA Ops:
  0.6 1.3 %shard_map.79 = f32[8,1,24]{2,1,0:T(1,128)} custom-call(s32[1,12]{1,0:T(1,128)} %rows.1, f32[1,12]{1,0:T(1,128)} %weights.1), custom_call_target="tpu_custom_call" | custom-call | tf_op jit(solution)/shard_map/pallas_call | solution.py:284
  2.0 5.9 %all-to-all-start.1 = ((f32[8,1,24]{2,1,0:T(1,128)}), f32[8,1,24]{2,1,0:T(1,128)S(1)}, u32[]{:S(2)}, u32[]{:S(2)}) async-start(f32[8,1,24]{2,1,0:T(1,128)} %shard_map.79), calls=%async_computation.1 | async-start | bytes 8192 | tf_op jit(solution)/shard_map/all_to_all | solution.py:267
  7.8 0.0 copy-start.2
  7.8 4.8 %shard_map.77 = bf16[8,64,768]{2,1,0:T(8,128)(2,1)} custom-call(s32[512]{0:T(512)} %orders.1, bf16[12,384]{1,0:T(8,128)(2,1)} %radial.1, bf16[4,512,384]{2,1,0:T(8,128)(2,1)} %bitcast.13, bf16[512,512]{1,0:T(8,128)(2,1)} %bitcast.14), custom_call_target="tpu_custom_call" | custom-call | tf_op jit(solution)/shard_map/pallas_call | solution.py:290
  12.7 0.1 all-to-all-done.1
  12.8 10.0 %all-to-all-start = ((bf16[8,64,768]{2,1,0:T(8,128)(2,1)}), bf16[8,64,768]{2,1,0:T(8,128)(2,1)S(1)}, u32[]{:S(2)}, u32[]{:S(2)}) async-start(bf16[8,64,768]{2,1,0:T(8,128)(2,1)} %shard_map.77), calls=%async_computation | async-start | bytes 1572864 | tf_op jit(solution)/shard_map/all_to_all | solution.py:267
  22.8 0.0 copy-done.2
  22.9 3.9 %all_gather.3 = f32[8,2,24]{2,0,1:T(8,128)S(1)} all-gather(f32[8,1,24]{2,0,1:T(8,128)S(1)} %bitcast.18), channel_id=1, replica_groups=mesh['half'=2,'z'=8,'pair'=2,'y'=2,'x'=4,'core'=2] {'core'}, dimensions={1}, use_global_device_ids=true | all-gather | bytes 2304 | tf_op jit(solution)/shard_map/all_gather | solution.py:310
  26.7 4.2 %collective-permute-start = (f32[16,24]{1,0:T(8,128)S(1)}, f32[16,24]{1,0:T(8,128)S(1)}, u32[]{:S(2)}, u32[]{:S(2)}) collective-permute-start(f32[16,24]{1,0:T(8,128)S(1)} %bitcast.15), channel_id=1, source_target_pairs={{0,16},{16,0},{1,17},{17,1},{2,18},{18,2},{3,19},{19,3},{4,20},{20... | collective-permute-start | bytes 4616 | tf_op jit(solution)/shard_map/ppermute | solution.py:311
  30.9 0.1 fusion
  31.0 1.2 %collective-permute-done = f32[16,24]{1,0:T(8,128)S(1)} collective-permute-done((f32[16,24]{1,0:T(8,128)S(1)}, f32[16,24]{1,0:T(8,128)S(1)}, u32[]{:S(2)}, u32[]{:S(2)}) %collective-permute-start) | collective-permute-done | bytes 1568 | tf_op jit(solution)/shard_map/ppermute | solution.py:311
  32.3 6.5 %collective-permute-start.1 = (f32[32,24]{1,0:T(8,128)S(1)}, f32[32,24]{1,0:T(8,128)S(1)}, u32[]{:S(2)}, u32[]{:S(2)}) collective-permute-start(f32[32,24]{1,0:T(8,128)S(1)} %pad_maximum_fusion.1), channel_id=1, source_target_pairs={{0,256},{256,0},{1,257},{257,1},{2,258},{258,2},{3,259},{259,3},{4... | collective-permute-start | bytes 9224 | tf_op jit(solution)/shard_map/ppermute | solution.py:312
  38.8 0.1 maximum_bitcast_fusion.step
  38.9 4.3 %shard_map.78 = (bf16[512,1024]{1,0:T(8,128)(2,1)S(1)}, bf16[512,1024]{1,0:T(8,128)(2,1)S(1)}) custom-call(s32[1,512]{1,0:T(1,128)S(1)} %bitcast.11), custom_call_target="tpu_custom_call" | custom-call | tf_op jit(solution)/shard_map/pallas_call | solution.py:319
  43.2 1.0 %copy-done = bf16[512,1024]{1,0:T(8,128)(2,1)} copy-done((bf16[512,1024]{1,0:T(8,128)(2,1)}, bf16[512,1024]{1,0:T(8,128)(2,1)S(1)}, u32[]{:S(2)}) %copy-start) | copy-done | bytes 1048600
  44.2 0.0 collective-permute-done.1
  44.2 0.4 shard_map.80.picks
  44.6 0.0 all-to-all-done.arrived
  44.6 1.4 %shard_map.81 = (bf16[8,32,512]{2,1,0:T(8,128)(2,1)S(1)}, bf16[1024,128]{1,0:T(8,128)(2,1)S(1)}) custom-call(bf16[8,64,768]{2,1,0:T(8,128)(2,1)S(1)} %all-to-all-done.arrived, f32[64,24]{1,0:T(8,128)S(1)} %pad_maximum_fusion.infos), custom_call_target="tpu_custom_call" | custom-call | tf_op jit(solution)/shard_map/pallas_call | solution.py:329
  46.1 0.0 copy-start.1
  46.1 16.5 %all_to_all.20.parts = bf16[8,32,512]{2,1,0:T(8,128)(2,1)S(1)} all-to-all(bf16[8,32,512]{2,1,0:T(8,128)(2,1)S(1)} %get-tuple-element.20), channel_id=1, replica_groups=mesh['half'=2,'z'=8,'pair'=2,'y'=2,'x'=4,'core'=2] {'z'}, dimensions={0} | all-to-all | bytes 524288 | tf_op jit(solution)/shard_map/all_to_all | solution.py:267
  62.6 0.8 shard_map.82
  63.4 22.8 %all_to_all.21 = bf16[64,16,128]{2,1,0:T(8,128)(2,1)S(1)} all-to-all(bf16[64,16,128]{2,1,0:T(8,128)(2,1)S(1)} %shard_map.82), channel_id=1, replica_groups=mesh['half'=2,'z'=8,'pair'=2,'y'=2,'x'=4,'core'=2] {'half','pair','y','x..., dimensions={0} | all-to-all | bytes 524288 | tf_op jit(solution)/shard_map/all_to_all | solution.py:267
  86.1 1.3 %shard_map.83 = (f32[16,64]{1,0:T(8,128)}, f32[2,12,1,1024]{3,2,1,0:T(1,128)}) custom-call(bf16[2,32,16,128]{3,2,1,0:T(8,128)(2,1)S(1)} %bitcast.10, bf16[512,1024]{1,0:T(8,128)(2,1)S(1)} %get-tuple-element.24.cosines, bf16[512,1024]{1,0:T(8,128)(2,1)S(1)} %copy-done.1, f32[1,512]{1,0:T(1,128)S(1)} %bitcast.12, f32[1,12]{1,0:T(1,128)S(1)} %multiply_add_fusion.radius), custom_call_target="tpu_custom_call" | custom-call | tf_op jit(solution)/shard_map/pallas_call | solution.py:344
  (9 shorter events, 0.0 us)
Async XLA Ops:
  2.0 10.8 %all-to-all-start.1 = ((f32[8,1,24]{2,1,0:T(1,128)}), f32[8,1,24]{2,1,0:T(1,128)S(1)}, u32[]{:S(2)}, u32[]{:S(2)}) async-start(f32[8,1,24]{2,1,0:T(1,128)} %shard_map.79), calls=%async_computation.1 | async-start | bytes 8192 | tf_op jit(solution)/shard_map/all_to_all | solution.py:267
  7.8 15.0 %copy-start.3 = (s32[1,12]{1,0:T(1,128)S(1)}, s32[1,12]{1,0:T(1,128)}, u32[]{:S(2)}) copy-start(s32[1,12]{1,0:T(1,128)} %rows.1) | copy-start | bytes 148
  7.8 15.0 %copy-start.2 = (s32[512]{0:T(512)S(1)}, s32[512]{0:T(512)}, u32[]{:S(2)}) copy-start(s32[512]{0:T(512)} %orders.1) | copy-start | bytes 6148
  12.8 31.9 %all-to-all-start = ((bf16[8,64,768]{2,1,0:T(8,128)(2,1)}), bf16[8,64,768]{2,1,0:T(8,128)(2,1)S(1)}, u32[]{:S(2)}, u32[]{:S(2)}) async-start(bf16[8,64,768]{2,1,0:T(8,128)(2,1)} %shard_map.77), calls=%async_computation | async-start | bytes 1572864 | tf_op jit(solution)/shard_map/all_to_all | solution.py:267
  26.7 5.6 %collective-permute-start = (f32[16,24]{1,0:T(8,128)S(1)}, f32[16,24]{1,0:T(8,128)S(1)}, u32[]{:S(2)}, u32[]{:S(2)}) collective-permute-start(f32[16,24]{1,0:T(8,128)S(1)} %bitcast.15), channel_id=1, source_target_pairs={{0,16},{16,0},{1,17},{17,1},{2,18},{18,2},{3,19},{19,3},{4,20},{20... | collective-permute-start | bytes 4616 | tf_op jit(solution)/shard_map/ppermute | solution.py:311
  32.3 11.9 %collective-permute-start.1 = (f32[32,24]{1,0:T(8,128)S(1)}, f32[32,24]{1,0:T(8,128)S(1)}, u32[]{:S(2)}, u32[]{:S(2)}) collective-permute-start(f32[32,24]{1,0:T(8,128)S(1)} %pad_maximum_fusion.1), channel_id=1, source_target_pairs={{0,256},{256,0},{1,257},{257,1},{2,258},{258,2},{3,259},{259,3},{4... | collective-permute-start | bytes 9224 | tf_op jit(solution)/shard_map/ppermute | solution.py:312
  43.2 1.0 %copy-start = (bf16[512,1024]{1,0:T(8,128)(2,1)}, bf16[512,1024]{1,0:T(8,128)(2,1)S(1)}, u32[]{:S(2)}) copy-start(bf16[512,1024]{1,0:T(8,128)(2,1)S(1)} %get-tuple-element.25.sines) | copy-start | bytes 3145732
  46.1 40.1 %copy-start.1 = (bf16[512,1024]{1,0:T(8,128)(2,1)S(1)}, bf16[512,1024]{1,0:T(8,128)(2,1)}, u32[]{:S(2)}) copy-start(bf16[512,1024]{1,0:T(8,128)(2,1)} %copy-done) | copy-start | bytes 3145732

commit v7 on v6

--- a/solution.py
+++ b/solution.py
@@ -73,8 +73,8 @@
 
 
 def contribution_kernel(
-    slots, degrees, halves, orders, radial, spectrum_in, legendre_in, out,
-    spectrum, legendre, turned, held, sems, outs
+    slots, degrees, halves, orders_in, radial_in, spectrum_in, legendre_in, out,
+    orders, radial, spectrum, legendre, turned, held, small, sems, outs
 ):
     parts = spectrum.shape[0]
     ways = sems.shape[1]
@@ -89,10 +89,16 @@
         ]
         for c, (source, target) in enumerate(sides)
     ]
+    first_copies = [
+        pltpu.make_async_copy(orders_in, orders, small.at[0]),
+        pltpu.make_async_copy(radial_in, radial, small.at[1]),
+    ]
+    for copy in first_copies:
+        copy.start()
     for some in copies:
         for copy in some:
             copy.start()
-    for copy in copies[0]:
+    for copy in first_copies + copies[0]:
         copy.wait()
     turned[...] = jnp.transpose(legendre[...])
     levels_n = radial.shape[0]
@@ -290,12 +296,15 @@
     contribution = vmem_call(
         functools.partial(contribution_kernel, slots, degrees, n_half),
         pltpu.HBM((n_z, lat_block, levels_n * parts * slots), BF16),
-        1, 1, 2,
+        0, 0, 4,
         (
+            pltpu.SMEM(order_table.shape, I32),
+            pltpu.VMEM(radial_table.shape, BF16),
             pltpu.VMEM((parts, slots * degrees, modes), BF16),
             pltpu.VMEM((slots * degrees, lats), BF16),
             pltpu.VMEM((lats, slots * degrees), BF16),
             pltpu.VMEM((lats, levels_n * parts * slots), BF16),
+            pltpu.SemaphoreType.DMA((2,)),
             pltpu.SemaphoreType.DMA((parts + 1, 4)),
             pltpu.SemaphoreType.DMA((n_half * n_z,)),
         ),

time: 87.9 us -> 87.4 us (level)
  transfers between devices with their start and end apart: 4 -> 4, of which waited for: 2 -> 2; matrix products, arithmetic and copies ran while one was open for 0% -> 0% of each run, Pallas kernels for 11% -> 10%
where the time goes in v7:
time: 87.4 us; the launch traced here: 87 us
  blocking collectives  42.6 us (49%)
  starting transfers between devices  26.6 us (30%)
  Pallas kernels  13.8 us (16%)
  waiting for transfers between devices  1.95 us (2%)
  local copies, waits for them, and re-layouts  0.99 us (1%)
    all_to_all x2, blocking collectives, exchanged(): return lax.all_to_all(blocks, axis, split_axis=0, concat_axis=0, tiled=True)  38.8 us
    all_to_all x2, starting transfers between devices, exchanged(): return lax.all_to_all(blocks, axis, split_axis=0, concat_axis=0, tiled=True)  15.9 us
    ppermute x1, starting transfers between devices, on_device(): infos = jnp.concatenate([info, lax.ppermute(info, 'half', swap)], axis=0)  6.54 us
    pallas_call x1, Pallas kernels, on_device(): vmem_call(functools.partial(contribution_kernel, slots, degrees, n_half),...  4.32 us
    pallas_call x1, Pallas kernels, on_device(): vmem_call(table_kernel, (table, table), 0, 1)(order_table.reshape(1, -1))  4.27 us
    ppermute x1, starting transfers between devices, on_device(): info = jnp.concatenate([info, lax.ppermute(info, 'pair', swap)], axis=0)  4.21 us
    all_gather x1, blocking collectives, on_device(): info = lax.all_gather(info, 'core', axis=1).reshape(-1, 2 * levels_n)  3.85 us
  transfers between devices with their start and end apart: 4, of which 2 were waited for; matrix products, arithmetic and copies ran while one was open for 0% of the time, Pallas kernels for 10%

profile of v7, /device:TPU:1, one launch (start us, length us, event | category | flops | bytes accessed | tf_op | source)
XLA Modules:
  0.0 87.0 jit_solution(11764341686511610638)
XLA Ops:
  0.6 1.3 %shard_map.79 = f32[8,1,24]{2,1,0:T(1,128)} custom-call(s32[1,12]{1,0:T(1,128)} %rows.1, f32[1,12]{1,0:T(1,128)} %weights.1), custom_call_target="tpu_custom_call" | custom-call | tf_op jit(solution)/shard_map/pallas_call | solution.py:290
  2.0 5.9 %all-to-all-start.1 = ((f32[8,1,24]{2,1,0:T(1,128)}), f32[8,1,24]{2,1,0:T(1,128)S(1)}, u32[]{:S(2)}, u32[]{:S(2)}) async-start(f32[8,1,24]{2,1,0:T(1,128)} %shard_map.79), calls=%async_computation.1 | async-start | bytes 8192 | tf_op jit(solution)/shard_map/all_to_all | solution.py:273
  7.8 0.0 copy-start.2
  7.8 4.3 %shard_map.77 = bf16[8,64,768]{2,1,0:T(8,128)(2,1)} custom-call(s32[512]{0:T(512)} %orders_in.1, bf16[12,384]{1,0:T(8,128)(2,1)} %radial_in.1, bf16[4,512,384]{2,1,0:T(8,128)(2,1)} %bitcast.13, bf16[512,512]{1,0:T(8,128)(2,1)} %bitcast.14), custom_call_target="tpu_custom_call" | custom-call | tf_op jit(solution)/shard_map/pallas_call | solution.py:296
  12.2 0.6 all-to-all-done.1
  12.8 10.0 %all-to-all-start = ((bf16[8,64,768]{2,1,0:T(8,128)(2,1)}), bf16[8,64,768]{2,1,0:T(8,128)(2,1)S(1)}, u32[]{:S(2)}, u32[]{:S(2)}) async-start(bf16[8,64,768]{2,1,0:T(8,128)(2,1)} %shard_map.77), calls=%async_computation | async-start | bytes 1572864 | tf_op jit(solution)/shard_map/all_to_all | solution.py:273
  22.8 0.0 copy-done.2
  22.9 3.9 %all_gather.3 = f32[8,2,24]{2,0,1:T(8,128)S(1)} all-gather(f32[8,1,24]{2,0,1:T(8,128)S(1)} %bitcast.18), channel_id=1, replica_groups=mesh['half'=2,'z'=8,'pair'=2,'y'=2,'x'=4,'core'=2] {'core'}, dimensions={1}, use_global_device_ids=true | all-gather | bytes 2304 | tf_op jit(solution)/shard_map/all_gather | solution.py:319
  26.7 4.2 %collective-permute-start = (f32[16,24]{1,0:T(8,128)S(1)}, f32[16,24]{1,0:T(8,128)S(1)}, u32[]{:S(2)}, u32[]{:S(2)}) collective-permute-start(f32[16,24]{1,0:T(8,128)S(1)} %bitcast.15), channel_id=1, source_target_pairs={{0,16},{16,0},{1,17},{17,1},{2,18},{18,2},{3,19},{19,3},{4,20},{20... | collective-permute-start | bytes 4616 | tf_op jit(solution)/shard_map/ppermute | solution.py:320
  30.9 0.1 fusion
  31.0 1.3 %collective-permute-done = f32[16,24]{1,0:T(8,128)S(1)} collective-permute-done((f32[16,24]{1,0:T(8,128)S(1)}, f32[16,24]{1,0:T(8,128)S(1)}, u32[]{:S(2)}, u32[]{:S(2)}) %collective-permute-start) | collective-permute-done | bytes 1568 | tf_op jit(solution)/shard_map/ppermute | solution.py:320
  32.4 6.5 %collective-permute-start.1 = (f32[32,24]{1,0:T(8,128)S(1)}, f32[32,24]{1,0:T(8,128)S(1)}, u32[]{:S(2)}, u32[]{:S(2)}) collective-permute-start(f32[32,24]{1,0:T(8,128)S(1)} %pad_maximum_fusion.1), channel_id=1, source_target_pairs={{0,256},{256,0},{1,257},{257,1},{2,258},{258,2},{3,259},{259,3},{4... | collective-permute-start | bytes 9224 | tf_op jit(solution)/shard_map/ppermute | solution.py:321
  38.9 0.1 maximum_bitcast_fusion.step
  39.0 4.3 %shard_map.78 = (bf16[512,1024]{1,0:T(8,128)(2,1)S(1)}, bf16[512,1024]{1,0:T(8,128)(2,1)S(1)}) custom-call(s32[1,512]{1,0:T(1,128)S(1)} %bitcast.11), custom_call_target="tpu_custom_call" | custom-call | tf_op jit(solution)/shard_map/pallas_call | solution.py:328
  43.3 1.0 %copy-done = bf16[512,1024]{1,0:T(8,128)(2,1)} copy-done((bf16[512,1024]{1,0:T(8,128)(2,1)}, bf16[512,1024]{1,0:T(8,128)(2,1)S(1)}, u32[]{:S(2)}) %copy-start) | copy-done | bytes 1048600
  44.3 0.0 collective-permute-done.1
  44.3 0.4 shard_map.80.picks
  44.7 0.0 all-to-all-done.arrived
  44.7 1.4 %shard_map.81 = (bf16[8,32,512]{2,1,0:T(8,128)(2,1)S(1)}, bf16[1024,128]{1,0:T(8,128)(2,1)S(1)}) custom-call(bf16[8,64,768]{2,1,0:T(8,128)(2,1)S(1)} %all-to-all-done.arrived, f32[64,24]{1,0:T(8,128)S(1)} %pad_maximum_fusion.infos), custom_call_target="tpu_custom_call" | custom-call | tf_op jit(solution)/shard_map/pallas_call | solution.py:338
  46.1 16.5 %all_to_all.20.parts = bf16[8,32,512]{2,1,0:T(8,128)(2,1)S(1)} all-to-all(bf16[8,32,512]{2,1,0:T(8,128)(2,1)S(1)} %get-tuple-element.20), channel_id=1, replica_groups=mesh['half'=2,'z'=8,'pair'=2,'y'=2,'x'=4,'core'=2] {'z'}, dimensions={0} | all-to-all | bytes 524288 | tf_op jit(solution)/shard_map/all_to_all | solution.py:273
  62.7 0.8 shard_map.82
  63.4 22.2 %all_to_all.21 = bf16[64,16,128]{2,1,0:T(8,128)(2,1)S(1)} all-to-all(bf16[64,16,128]{2,1,0:T(8,128)(2,1)S(1)} %shard_map.82), channel_id=1, replica_groups=mesh['half'=2,'z'=8,'pair'=2,'y'=2,'x'=4,'core'=2] {'half','pair','y','x..., dimensions={0} | all-to-all | bytes 524288 | tf_op jit(solution)/shard_map/all_to_all | solution.py:273
  85.7 0.0 copy-done.1
  85.7 1.3 %shard_map.83 = (f32[16,64]{1,0:T(8,128)}, f32[2,12,1,1024]{3,2,1,0:T(1,128)}) custom-call(bf16[2,32,16,128]{3,2,1,0:T(8,128)(2,1)S(1)} %bitcast.10, bf16[512,1024]{1,0:T(8,128)(2,1)S(1)} %get-tuple-element.24.cosines, bf16[512,1024]{1,0:T(8,128)(2,1)S(1)} %copy-done.1, f32[1,512]{1,0:T(1,128)S(1)} %bitcast.12, f32[1,12]{1,0:T(1,128)S(1)} %multiply_add_fusion.radius), custom_call_target="tpu_custom_call" | custom-call | tf_op jit(solution)/shard_map/pallas_call | solution.py:353
  (9 shorter events, 0.0 us)
Async XLA Ops:
  2.0 10.8 %all-to-all-start.1 = ((f32[8,1,24]{2,1,0:T(1,128)}), f32[8,1,24]{2,1,0:T(1,128)S(1)}, u32[]{:S(2)}, u32[]{:S(2)}) async-start(f32[8,1,24]{2,1,0:T(1,128)} %shard_map.79), calls=%async_computation.1 | async-start | bytes 8192 | tf_op jit(solution)/shard_map/all_to_all | solution.py:273
  7.8 15.0 %copy-start.3 = (s32[1,12]{1,0:T(1,128)S(1)}, s32[1,12]{1,0:T(1,128)}, u32[]{:S(2)}) copy-start(s32[1,12]{1,0:T(1,128)} %rows.1) | copy-start | bytes 148
  7.8 15.0 %copy-start.2 = (s32[512]{0:T(512)S(1)}, s32[512]{0:T(512)}, u32[]{:S(2)}) copy-start(s32[512]{0:T(512)} %orders_in.1) | copy-start | bytes 6148
  12.8 31.9 %all-to-all-start = ((bf16[8,64,768]{2,1,0:T(8,128)(2,1)}), bf16[8,64,768]{2,1,0:T(8,128)(2,1)S(1)}, u32[]{:S(2)}, u32[]{:S(2)}) async-start(bf16[8,64,768]{2,1,0:T(8,128)(2,1)} %shard_map.77), calls=%async_computation | async-start | bytes 1572864 | tf_op jit(solution)/shard_map/all_to_all | solution.py:273
  26.7 5.7 %collective-permute-start = (f32[16,24]{1,0:T(8,128)S(1)}, f32[16,24]{1,0:T(8,128)S(1)}, u32[]{:S(2)}, u32[]{:S(2)}) collective-permute-start(f32[16,24]{1,0:T(8,128)S(1)} %bitcast.15), channel_id=1, source_target_pairs={{0,16},{16,0},{1,17},{17,1},{2,18},{18,2},{3,19},{19,3},{4,20},{20... | collective-permute-start | bytes 4616 | tf_op jit(solution)/shard_map/ppermute | solution.py:320
  32.4 11.9 %collective-permute-start.1 = (f32[32,24]{1,0:T(8,128)S(1)}, f32[32,24]{1,0:T(8,128)S(1)}, u32[]{:S(2)}, u32[]{:S(2)}) collective-permute-start(f32[32,24]{1,0:T(8,128)S(1)} %pad_maximum_fusion.1), channel_id=1, source_target_pairs={{0,256},{256,0},{1,257},{257,1},{2,258},{258,2},{3,259},{259,3},{4... | collective-permute-start | bytes 9224 | tf_op jit(solution)/shard_map/ppermute | solution.py:321
  43.3 1.0 %copy-start = (bf16[512,1024]{1,0:T(8,128)(2,1)}, bf16[512,1024]{1,0:T(8,128)(2,1)S(1)}, u32[]{:S(2)}) copy-start(bf16[512,1024]{1,0:T(8,128)(2,1)S(1)} %get-tuple-element.25.sines) | copy-start | bytes 3145732
  46.1 39.5 %copy-start.1 = (bf16[512,1024]{1,0:T(8,128)(2,1)S(1)}, bf16[512,1024]{1,0:T(8,128)(2,1)}, u32[]{:S(2)}) copy-start(bf16[512,1024]{1,0:T(8,128)(2,1)} %copy-done) | copy-start | bytes 3145732

commit v8 on v7

--- a/solution.py
+++ b/solution.py
@@ -41,7 +41,7 @@
     return lax.dot_general(x, y, (((dim_x,), (dim_y,)), ((), ())), preferred_element_type=F32)
 
 
-def vmem_call(body, outs, n_smem, n_vmem, n_hbm=0, scratch=(), out_space=pltpu.VMEM):
+def vmem_call(body, outs, n_smem, n_vmem, n_hbm=0, scratch=(), out_space=pltpu.VMEM, cost=None):
     return pl.pallas_call(
         body,
         out_shape=outs,
@@ -50,6 +50,7 @@
         + [pl.BlockSpec(memory_space=pltpu.HBM)] * n_hbm,
         out_specs=jax.tree.map(lambda _: pl.BlockSpec(memory_space=out_space), outs),
         scratch_shapes=scratch,
+        cost_estimate=cost,
         compiler_params=pltpu.CompilerParams(vmem_limit_bytes=VMEM_LIMIT),
     )
 
@@ -73,34 +74,18 @@
 
 
 def contribution_kernel(
-    slots, degrees, halves, orders_in, radial_in, spectrum_in, legendre_in, out,
-    orders, radial, spectrum, legendre, turned, held, small, sems, outs
+    slots, degrees, halves, spectrum, legendre, orders_in, radial_in, out,
+    orders, radial, held, small, outs
 ):
     parts = spectrum.shape[0]
-    ways = sems.shape[1]
-    step = spectrum.shape[1] // ways
-    sides = [(legendre_in, legendre)] + [(spectrum_in.at[c], spectrum.at[c]) for c in range(parts)]
     copies = [
-        [
-            pltpu.make_async_copy(
-                source.at[pl.ds(w * step, step)], target.at[pl.ds(w * step, step)], sems.at[c, w]
-            )
-            for w in range(ways)
-        ]
-        for c, (source, target) in enumerate(sides)
-    ]
-    first_copies = [
         pltpu.make_async_copy(orders_in, orders, small.at[0]),
         pltpu.make_async_copy(radial_in, radial, small.at[1]),
     ]
-    for copy in first_copies:
+    for copy in copies:
         copy.start()
-    for some in copies:
-        for copy in some:
-            copy.start()
-    for copy in first_copies + copies[0]:
+    for copy in copies:
         copy.wait()
-    turned[...] = jnp.transpose(legendre[...])
     levels_n = radial.shape[0]
     columns = levels_n * parts
     width = columns * slots
@@ -111,8 +96,6 @@
     levels = jnp.zeros((rows, columns), F32)
     for c in range(parts):
         table = jnp.where(part_of == c, repeated, 0.0).astype(BF16)
-        for copy in copies[c + 1]:
-            copy.wait()
         levels += dot_dims(spectrum[c], table, 1, 1)
     spread = (iota((columns, width), 0) == iota((columns, width), 1) // slots).astype(BF16)
     expanded = dot(levels.astype(BF16), spread)
@@ -130,7 +113,7 @@
     writes = []
     for first in range(0, halves * n_z, group):
         lanes = slice(first * block, (first + group) * block)
-        held[lanes] = dot(turned[lanes], diagonal).astype(BF16)
+        held[lanes] = dot_dims(legendre[:, lanes], diagonal, 0, 0).astype(BF16)
         for g in range(first, first + group):
             h, z = divmod(g, n_z)
             write = pltpu.make_async_copy(
@@ -181,15 +164,15 @@
     total = arrived[0].astype(F32)
     for d in range(1, arrived.shape[0]):
         total += arrived[d].astype(F32)
-    points = jnp.concatenate(
+    exact = jnp.concatenate(
         [total[:, r * width : (r + 1) * width] for r in range(levels_n)], axis=0
-    ).astype(BF16)
+    )
+    points = exact.astype(BF16)
     info = in_place(infos[...])
     rows = jnp.concatenate([info[:, r : r + 1] for r in range(levels_n)], axis=0)
     weight = jnp.concatenate([info[:, r : r + 1] for r in range(levels_n, 2 * levels_n)], axis=0)
     onehot = matches(rows, iota((lats * levels_n, NS), 1).astype(F32))
     half = width // 2
-    exact = points.astype(F32)
     weighted = (exact[:, :half] - COMPOSITION_WEIGHT * exact[:, half:]) * weight
     high = weighted.astype(BF16)
     low = (weighted - high.astype(F32)).astype(BF16)
@@ -291,29 +274,26 @@
         info_kernel,
         pltpu.HBM((lax.axis_size(near), 1, 2 * levels_n), F32),
         0, 2,
+        cost=pl.CostEstimate(flops=4 * 10**9, bytes_accessed=4 * 10**7, transcendentals=0),
     )(in_hbm(cylinder_row), in_hbm(column_weight))
     info = exchanged(info, near).reshape(-1, 2 * levels_n)
     contribution = vmem_call(
         functools.partial(contribution_kernel, slots, degrees, n_half),
         pltpu.HBM((n_z, lat_block, levels_n * parts * slots), BF16),
-        0, 0, 4,
+        0, 2, 2,
         (
             pltpu.SMEM(order_table.shape, I32),
             pltpu.VMEM(radial_table.shape, BF16),
-            pltpu.VMEM((parts, slots * degrees, modes), BF16),
-            pltpu.VMEM((slots * degrees, lats), BF16),
-            pltpu.VMEM((lats, slots * degrees), BF16),
             pltpu.VMEM((lats, levels_n * parts * slots), BF16),
             pltpu.SemaphoreType.DMA((2,)),
-            pltpu.SemaphoreType.DMA((parts + 1, 4)),
             pltpu.SemaphoreType.DMA((n_half * n_z,)),
         ),
         pltpu.HBM,
     )(
+        spectrum.reshape(parts, slots * degrees, modes),
+        legendre.reshape(slots * degrees, lats),
         in_hbm(order_table),
         in_hbm(radial_table),
-        in_hbm(spectrum.reshape(parts, slots * degrees, modes)),
-        in_hbm(legendre.reshape(slots * degrees, lats)),
     )
     arrived = exchanged(contribution, "z")
     info = lax.all_gather(info, "core", axis=1).reshape(-1, 2 * levels_n)

time: 87.4 us -> 86.4 us (0.989)
  blocking collectives: 42.6 us -> 41.4 us
  waiting for transfers between devices: 1.95 us -> 3.11 us
  Pallas kernels: 13.8 us -> 12.8 us
    pallas_call x1, Pallas kernels: 4.32 us -> 3.13 us  [on_device(): vmem_call(functools.partial(contribution_kernel, slots, degrees, n_half),...]
    all_to_all x2, blocking collectives: 38.8 us -> 37.6 us  [exchanged(): return lax.all_to_all(blocks, axis, split_axis=0, concat_axis=0, tiled=True)]
    all_to_all x2, waiting for transfers between devices: 0.62 us -> 1.78 us  [exchanged(): return lax.all_to_all(blocks, axis, split_axis=0, concat_axis=0, tiled=True)]
  transfers between devices with their start and end apart: 4 -> 4, of which waited for: 2 -> 2; matrix products, arithmetic and copies ran while one was open for 0% -> 0% of each run, Pallas kernels for 10% -> 9%
where the time goes in v8:
time: 86.4 us; the launch traced here: 86 us
  blocking collectives  41.4 us (48%)
  starting transfers between devices  26.6 us (31%)
  Pallas kernels  12.8 us (15%)
  waiting for transfers between devices  3.11 us (4%)
  local copies, waits for them, and re-layouts  1.01 us (1%)
    all_to_all x2, blocking collectives, exchanged(): return lax.all_to_all(blocks, axis, split_axis=0, concat_axis=0, tiled=True)  37.6 us
    all_to_all x2, starting transfers between devices, exchanged(): return lax.all_to_all(blocks, axis, split_axis=0, concat_axis=0, tiled=True)  15.9 us
    ppermute x1, starting transfers between devices, on_device(): infos = jnp.concatenate([info, lax.ppermute(info, 'half', swap)], axis=0)  6.54 us
    pallas_call x1, Pallas kernels, on_device(): vmem_call(table_kernel, (table, table), 0, 1)(order_table.reshape(1, -1))  4.27 us
    ppermute x1, starting transfers between devices, on_device(): info = jnp.concatenate([info, lax.ppermute(info, 'pair', swap)], axis=0)  4.21 us
    all_gather x1, blocking collectives, on_device(): info = lax.all_gather(info, 'core', axis=1).reshape(-1, 2 * levels_n)  3.85 us
    pallas_call x1, Pallas kernels, on_device(): vmem_call(functools.partial(contribution_kernel, slots, degrees, n_half),...  3.13 us
    all_to_all x2, waiting for transfers between devices, exchanged(): return lax.all_to_all(blocks, axis, split_axis=0, concat_axis=0, tiled=True)  1.78 us
  transfers between devices with their start and end apart: 4, of which 2 were waited for; matrix products, arithmetic and copies ran while one was open for 0% of the time, Pallas kernels for 9%

profile of v8, /device:TPU:1, one launch (start us, length us, event | category | flops | bytes accessed | tf_op | source)
XLA Modules:
  0.0 86.0 jit_solution(8636869871841866283)
XLA Ops:
  0.6 1.5 %shard_map.79 = f32[8,1,24]{2,1,0:T(1,128)} custom-call(s32[1,12]{1,0:T(1,128)} %rows.1, f32[1,12]{1,0:T(1,128)} %weights.1), custom_call_target="tpu_custom_call" | custom-call | flops 4000000000 | bytes 40000000 | tf_op jit(solution)/shard_map/pallas_call | solution.py:273
  2.1 5.9 %all-to-all-start.1 = ((f32[8,1,24]{2,1,0:T(1,128)}), f32[8,1,24]{2,1,0:T(1,128)S(1)}, u32[]{:S(2)}, u32[]{:S(2)}) async-start(f32[8,1,24]{2,1,0:T(1,128)} %shard_map.79), calls=%async_computation.1 | async-start | bytes 8192 | tf_op jit(solution)/shard_map/all_to_all | solution.py:256
  8.0 0.0 copy-done
  8.0 0.0 copy-start.5
  8.0 0.0 copy-start.4
  8.0 3.1 %shard_map.77 = bf16[8,64,768]{2,1,0:T(8,128)(2,1)} custom-call(bf16[4,512,384]{2,1,0:T(8,128)(2,1)S(1)} %bitcast.10, bf16[512,512]{1,0:T(8,128)(2,1)S(1)} %bitcast.12, s32[512]{0:T(512)} %orders_in.1, bf16[12,384]{1,0:T(8,128)(2,1)} %radial_in.1), custom_call_target="tpu_custom_call" | custom-call | tf_op jit(solution)/shard_map/pallas_call | solution.py:280
  11.2 1.8 %all-to-all-done.1 = f32[8,1,24]{2,1,0:T(1,128)S(1)} async-done(((f32[8,1,24]{2,1,0:T(1,128)}), f32[8,1,24]{2,1,0:T(1,128)S(1)}, u32[]{:S(2)}, u32[]{:S(2)}) %all-to-all-start.1) | async-done | bytes 800 | tf_op jit(solution)/shard_map/all_to_all | solution.py:256
  12.9 10.0 %all-to-all-start = ((bf16[8,64,768]{2,1,0:T(8,128)(2,1)}), bf16[8,64,768]{2,1,0:T(8,128)(2,1)S(1)}, u32[]{:S(2)}, u32[]{:S(2)}) async-start(bf16[8,64,768]{2,1,0:T(8,128)(2,1)} %shard_map.77), calls=%async_computation | async-start | bytes 1572864 | tf_op jit(solution)/shard_map/all_to_all | solution.py:256
  23.0 3.9 %all_gather.3 = f32[8,2,24]{2,0,1:T(8,128)S(1)} all-gather(f32[8,1,24]{2,0,1:T(8,128)S(1)} %bitcast.18), channel_id=1, replica_groups=mesh['half'=2,'z'=8,'pair'=2,'y'=2,'x'=4,'core'=2] {'core'}, dimensions={1}, use_global_device_ids=true | all-gather | bytes 2304 | tf_op jit(solution)/shard_map/all_gather | solution.py:299
  26.9 4.2 %collective-permute-start = (f32[16,24]{1,0:T(8,128)S(1)}, f32[16,24]{1,0:T(8,128)S(1)}, u32[]{:S(2)}, u32[]{:S(2)}) collective-permute-start(f32[16,24]{1,0:T(8,128)S(1)} %bitcast.15), channel_id=1, source_target_pairs={{0,16},{16,0},{1,17},{17,1},{2,18},{18,2},{3,19},{19,3},{4,20},{20... | collective-permute-start | bytes 4616 | tf_op jit(solution)/shard_map/ppermute | solution.py:300
  31.1 0.1 fusion
  31.2 1.3 %collective-permute-done = f32[16,24]{1,0:T(8,128)S(1)} collective-permute-done((f32[16,24]{1,0:T(8,128)S(1)}, f32[16,24]{1,0:T(8,128)S(1)}, u32[]{:S(2)}, u32[]{:S(2)}) %collective-permute-start) | collective-permute-done | bytes 1568 | tf_op jit(solution)/shard_map/ppermute | solution.py:300
  32.5 6.5 %collective-permute-start.1 = (f32[32,24]{1,0:T(8,128)S(1)}, f32[32,24]{1,0:T(8,128)S(1)}, u32[]{:S(2)}, u32[]{:S(2)}) collective-permute-start(f32[32,24]{1,0:T(8,128)S(1)} %pad_maximum_fusion.1), channel_id=1, source_target_pairs={{0,256},{256,0},{1,257},{257,1},{2,258},{258,2},{3,259},{259,3},{4... | collective-permute-start | bytes 9224 | tf_op jit(solution)/shard_map/ppermute | solution.py:301
  39.1 0.1 maximum_bitcast_fusion.step
  39.2 4.3 %shard_map.78 = (bf16[512,1024]{1,0:T(8,128)(2,1)S(1)}, bf16[512,1024]{1,0:T(8,128)(2,1)S(1)}) custom-call(s32[1,512]{1,0:T(1,128)S(1)} %bitcast.13), custom_call_target="tpu_custom_call" | custom-call | tf_op jit(solution)/shard_map/pallas_call | solution.py:308
  43.5 1.0 %copy-done.1 = bf16[512,1024]{1,0:T(8,128)(2,1)} copy-done((bf16[512,1024]{1,0:T(8,128)(2,1)}, bf16[512,1024]{1,0:T(8,128)(2,1)S(1)}, u32[]{:S(2)}) %copy-start.1) | copy-done | bytes 1048600
  44.4 0.0 collective-permute-done.1
  44.4 0.4 shard_map.80.picks
  44.9 0.0 all-to-all-done.arrived
  44.9 1.4 %shard_map.81 = (bf16[8,32,512]{2,1,0:T(8,128)(2,1)S(1)}, bf16[1024,128]{1,0:T(8,128)(2,1)S(1)}) custom-call(bf16[8,64,768]{2,1,0:T(8,128)(2,1)S(1)} %all-to-all-done.arrived, f32[64,24]{1,0:T(8,128)S(1)} %pad_maximum_fusion.infos), custom_call_target="tpu_custom_call" | custom-call | tf_op jit(solution)/shard_map/pallas_call | solution.py:318
  46.3 16.5 %all_to_all.20.parts = bf16[8,32,512]{2,1,0:T(8,128)(2,1)S(1)} all-to-all(bf16[8,32,512]{2,1,0:T(8,128)(2,1)S(1)} %get-tuple-element.20), channel_id=1, replica_groups=mesh['half'=2,'z'=8,'pair'=2,'y'=2,'x'=4,'core'=2] {'z'}, dimensions={0} | all-to-all | bytes 524288 | tf_op jit(solution)/shard_map/all_to_all | solution.py:256
  62.9 0.8 shard_map.82
  63.6 21.0 %all_to_all.21 = bf16[64,16,128]{2,1,0:T(8,128)(2,1)S(1)} all-to-all(bf16[64,16,128]{2,1,0:T(8,128)(2,1)S(1)} %shard_map.82), channel_id=1, replica_groups=mesh['half'=2,'z'=8,'pair'=2,'y'=2,'x'=4,'core'=2] {'half','pair','y','x..., dimensions={0} | all-to-all | bytes 524288 | tf_op jit(solution)/shard_map/all_to_all | solution.py:256
  84.7 1.3 %shard_map.83 = (f32[16,64]{1,0:T(8,128)}, f32[2,12,1,1024]{3,2,1,0:T(1,128)}) custom-call(bf16[2,32,16,128]{3,2,1,0:T(8,128)(2,1)S(1)} %bitcast.11, bf16[512,1024]{1,0:T(8,128)(2,1)S(1)} %get-tuple-element.24.cosines, bf16[512,1024]{1,0:T(8,128)(2,1)S(1)} %copy-done.2, f32[1,512]{1,0:T(1,128)S(1)} %bitcast.14, f32[1,12]{1,0:T(1,128)S(1)} %multiply_add_fusion.radius), custom_call_target="tpu_custom_call" | custom-call | tf_op jit(solution)/shard_map/pallas_call | solution.py:333
  (13 shorter events, 0.0 us)
Async XLA Ops:
  0.6 7.4 %copy-start.3 = (bf16[16,32,512]{2,1,0:T(8,128)(2,1)S(1)}, bf16[16,32,512]{2,1,0:T(8,128)(2,1)}, u32[]{:S(2)}) copy-start(bf16[16,32,512]{2,1,0:T(8,128)(2,1)} %param.8) | copy-start | bytes 1572868
  0.6 7.4 %copy-start = (bf16[4,16,32,384]{3,2,1,0:T(8,128)(2,1)S(1)}, bf16[4,16,32,384]{3,2,1,0:T(8,128)(2,1)}, u32[]{:S(2)}) copy-start(bf16[4,16,32,384]{3,2,1,0:T(8,128)(2,1)} %param.6) | copy-start | bytes 4718596
  2.1 10.8 %all-to-all-start.1 = ((f32[8,1,24]{2,1,0:T(1,128)}), f32[8,1,24]{2,1,0:T(1,128)S(1)}, u32[]{:S(2)}, u32[]{:S(2)}) async-start(f32[8,1,24]{2,1,0:T(1,128)} %shard_map.79), calls=%async_computation.1 | async-start | bytes 8192 | tf_op jit(solution)/shard_map/all_to_all | solution.py:256
  8.0 15.0 %copy-start.5 = (s32[1,12]{1,0:T(1,128)S(1)}, s32[1,12]{1,0:T(1,128)}, u32[]{:S(2)}) copy-start(s32[1,12]{1,0:T(1,128)} %rows.1) | copy-start | bytes 148
  8.0 15.0 %copy-start.4 = (s32[512]{0:T(512)S(1)}, s32[512]{0:T(512)}, u32[]{:S(2)}) copy-start(s32[512]{0:T(512)} %orders_in.1) | copy-start | bytes 6148
  12.9 31.9 %all-to-all-start = ((bf16[8,64,768]{2,1,0:T(8,128)(2,1)}), bf16[8,64,768]{2,1,0:T(8,128)(2,1)S(1)}, u32[]{:S(2)}, u32[]{:S(2)}) async-start(bf16[8,64,768]{2,1,0:T(8,128)(2,1)} %shard_map.77), calls=%async_computation | async-start | bytes 1572864 | tf_op jit(solution)/shard_map/all_to_all | solution.py:256
  26.9 5.7 %collective-permute-start = (f32[16,24]{1,0:T(8,128)S(1)}, f32[16,24]{1,0:T(8,128)S(1)}, u32[]{:S(2)}, u32[]{:S(2)}) collective-permute-start(f32[16,24]{1,0:T(8,128)S(1)} %bitcast.15), channel_id=1, source_target_pairs={{0,16},{16,0},{1,17},{17,1},{2,18},{18,2},{3,19},{19,3},{4,20},{20... | collective-permute-start | bytes 4616 | tf_op jit(solution)/shard_map/ppermute | solution.py:300
  32.5 11.9 %collective-permute-start.1 = (f32[32,24]{1,0:T(8,128)S(1)}, f32[32,24]{1,0:T(8,128)S(1)}, u32[]{:S(2)}, u32[]{:S(2)}) collective-permute-start(f32[32,24]{1,0:T(8,128)S(1)} %pad_maximum_fusion.1), channel_id=1, source_target_pairs={{0,256},{256,0},{1,257},{257,1},{2,258},{258,2},{3,259},{259,3},{4... | collective-permute-start | bytes 9224 | tf_op jit(solution)/shard_map/ppermute | solution.py:301
  43.4 1.0 %copy-start.1 = (bf16[512,1024]{1,0:T(8,128)(2,1)}, bf16[512,1024]{1,0:T(8,128)(2,1)S(1)}, u32[]{:S(2)}) copy-start(bf16[512,1024]{1,0:T(8,128)(2,1)S(1)} %get-tuple-element.25.sines) | copy-start | bytes 3145732
  46.3 38.3 %copy-start.2 = (bf16[512,1024]{1,0:T(8,128)(2,1)S(1)}, bf16[512,1024]{1,0:T(8,128)(2,1)}, u32[]{:S(2)}) copy-start(bf16[512,1024]{1,0:T(8,128)(2,1)} %copy-done.1) | copy-start | bytes 3145732

commit v9 on v8

--- a/solution.py
+++ b/solution.py
@@ -127,19 +127,25 @@
 
 def table_kernel(orders, cosines, sines):
     count = orders.shape[1]
-    order = jnp.broadcast_to(as_column(orders[...], count), (count, LANES))
-    angle = (order * iota((count, LANES), 1) & (NPHI - 1)).astype(F32) * (2.0 * math.pi / NPHI)
-    weight = jnp.where(order == 0, 1.0, 2.0).astype(F32) / math.sqrt(NS)
-    cosine, sine = jnp.cos(angle) * weight, jnp.sin(angle) * weight
+    column = as_column(orders[...], count)
     half_root = math.sqrt(0.5)
-    for j in range(NPHI // LANES):
-        eighth = order * j & 7
+    some = 64
+    for first in range(0, count, some):
+        rows = slice(first, first + some)
+        order = jnp.broadcast_to(column[rows], (some, LANES))
+        phase = order * iota((some, LANES), 1) & (NPHI - 1)
+        angle = phase.astype(F32) * (2.0 * math.pi / NPHI)
+        weight = jnp.where(order == 0, 1.0, 2.0).astype(F32) / math.sqrt(NS)
+        cosine, sine = jnp.cos(angle) * weight, jnp.sin(angle) * weight
+        eighth = order & 7
         size = jnp.where(eighth & 1 == 1, half_root, 1.0)
         turn_cos = jnp.where(eighth & 3 == 2, 0.0, jnp.where((eighth >= 3) & (eighth <= 5), -size, size))
         turn_sin = jnp.where(eighth & 3 == 0, 0.0, jnp.where(eighth > 4, -size, size))
-        at = slice(j * LANES, (j + 1) * LANES)
-        cosines[:, at] = (cosine * turn_cos - sine * turn_sin).astype(BF16)
-        sines[:, at] = (-sine * turn_cos - cosine * turn_sin).astype(BF16)
+        for j in range(NPHI // LANES):
+            at = slice(j * LANES, (j + 1) * LANES)
+            cosines[rows, at] = cosine.astype(BF16)
+            sines[rows, at] = (-sine).astype(BF16)
+            cosine, sine = cosine * turn_cos - sine * turn_sin, sine * turn_cos + cosine * turn_sin
 
 
 def choice_kernel(per, infos, picks):
@@ -269,7 +275,7 @@
     me_ma = lax.axis_index(MA)
     swap = [(0, 1), (1, 0)]
 
-    near = ("y", "x")
+    near = ("x", "core")
     info = vmem_call(
         info_kernel,
         pltpu.HBM((lax.axis_size(near), 1, 2 * levels_n), F32),
@@ -296,7 +302,7 @@
         in_hbm(radial_table),
     )
     arrived = exchanged(contribution, "z")
-    info = lax.all_gather(info, "core", axis=1).reshape(-1, 2 * levels_n)
+    info = lax.all_gather(info, "y", axis=0, tiled=True)
     info = jnp.concatenate([info, lax.ppermute(info, "pair", swap)], axis=0)
     infos = jnp.concatenate([info, lax.ppermute(info, "half", swap)], axis=0)
     my_orders = lax.dynamic_slice_in_dim(order_table, me_ma * slots, slots)

time: 86.4 us -> 87.3 us (1.010)
  waiting for transfers between devices: 3.11 us -> 6.46 us
  Pallas kernels: 12.8 us -> 10.5 us
  blocking collectives: 41.4 us -> 40.5 us
  starting transfers between devices: 26.6 us -> 27.5 us
    all_to_all x2, waiting for transfers between devices: 1.78 us -> 5.21 us  [exchanged(): return lax.all_to_all(blocks, axis, split_axis=0, concat_axis=0, tiled=True)]
    pallas_call x1, Pallas kernels: 4.27 us -> 1.95 us  [on_device(): vmem_call(table_kernel, (table, table), 0, 1)(order_table.reshape(1, -1))]
    ppermute x1, starting transfers between devices: 6.54 us -> 7.44 us  [on_device(): infos = jnp.concatenate([info, lax.ppermute(info, 'half', swap)], axis=0)]
  transfers between devices with their start and end apart: 4 -> 4, of which waited for: 2 -> 3; matrix products, arithmetic and copies ran while one was open for 0% -> 0% of each run, Pallas kernels for 9% -> 6%
where the time goes in v9:
time: 87.3 us; the launch traced here: 86.9 us
  blocking collectives  40.5 us (46%)
  starting transfers between devices  27.5 us (32%)
  Pallas kernels  10.5 us (12%)
  waiting for transfers between devices  6.46 us (7%)
  local copies, waits for them, and re-layouts  1 us (1%)
    all_to_all x2, blocking collectives, exchanged(): return lax.all_to_all(blocks, axis, split_axis=0, concat_axis=0, tiled=True)  37.3 us
    all_to_all x2, starting transfers between devices, exchanged(): return lax.all_to_all(blocks, axis, split_axis=0, concat_axis=0, tiled=True)  15.8 us
    ppermute x1, starting transfers between devices, on_device(): infos = jnp.concatenate([info, lax.ppermute(info, 'half', swap)], axis=0)  7.44 us
    all_to_all x2, waiting for transfers between devices, exchanged(): return lax.all_to_all(blocks, axis, split_axis=0, concat_axis=0, tiled=True)  5.21 us
    ppermute x1, starting transfers between devices, on_device(): info = jnp.concatenate([info, lax.ppermute(info, 'pair', swap)], axis=0)  4.21 us
    all_gather x1, blocking collectives, on_device(): info = lax.all_gather(info, 'y', axis=0, tiled=True)  3.21 us
    pallas_call x1, Pallas kernels, on_device(): vmem_call(functools.partial(contribution_kernel, slots, degrees, n_half),...  3.13 us
    pallas_call x1, Pallas kernels, on_device(): vmem_call(table_kernel, (table, table), 0, 1)(order_table.reshape(1, -1))  1.95 us
  transfers between devices with their start and end apart: 4, of which 3 were waited for; matrix products, arithmetic and copies ran while one was open for 0% of the time, Pallas kernels for 6%

profile of v9, /device:TPU:1, one launch (start us, length us, event | category | flops | bytes accessed | tf_op | source)
XLA Modules:
  0.0 86.9 jit_solution(13876712135329342234)
XLA Ops:
  0.6 1.5 %shard_map.79 = f32[8,1,24]{2,1,0:T(1,128)} custom-call(s32[1,12]{1,0:T(1,128)} %rows.1, f32[1,12]{1,0:T(1,128)} %weights.1), custom_call_target="tpu_custom_call" | custom-call | flops 4000000000 | bytes 40000000 | tf_op jit(solution)/shard_map/pallas_call | solution.py:279
  2.1 10.1 %all-to-all-start.1 = ((f32[8,1,24]{2,1,0:T(1,128)}), f32[8,1,24]{2,1,0:T(1,128)S(1)}, u32[]{:S(2)}, u32[]{:S(2)}) async-start(f32[8,1,24]{2,1,0:T(1,128)} %shard_map.79), calls=%async_computation.1 | async-start | bytes 8192 | tf_op jit(solution)/shard_map/all_to_all | solution.py:262
  12.2 0.0 copy-done
  12.2 0.0 copy-start.5
  12.2 0.0 copy-start.4
  12.2 3.1 %shard_map.77 = bf16[8,64,768]{2,1,0:T(8,128)(2,1)} custom-call(bf16[4,512,384]{2,1,0:T(8,128)(2,1)S(1)} %bitcast.9, bf16[512,512]{1,0:T(8,128)(2,1)S(1)} %bitcast.11, s32[512]{0:T(512)} %orders_in.1, bf16[12,384]{1,0:T(8,128)(2,1)} %radial_in.1), custom_call_target="tpu_custom_call" | custom-call | tf_op jit(solution)/shard_map/pallas_call | solution.py:286
  15.4 1.4 %all-to-all-done.1 = f32[8,1,24]{2,1,0:T(1,128)S(1)} async-done(((f32[8,1,24]{2,1,0:T(1,128)}), f32[8,1,24]{2,1,0:T(1,128)S(1)}, u32[]{:S(2)}, u32[]{:S(2)}) %all-to-all-start.1) | async-done | bytes 800 | tf_op jit(solution)/shard_map/all_to_all | solution.py:262
  16.7 5.8 %all-to-all-start = ((bf16[8,64,768]{2,1,0:T(8,128)(2,1)}), bf16[8,64,768]{2,1,0:T(8,128)(2,1)S(1)}, u32[]{:S(2)}, u32[]{:S(2)}) async-start(bf16[8,64,768]{2,1,0:T(8,128)(2,1)} %shard_map.77), calls=%async_computation | async-start | bytes 1572864 | tf_op jit(solution)/shard_map/all_to_all | solution.py:262
  22.5 3.2 %all-gather = f32[16,1,24]{2,1,0:T(1,128)S(1)} all-gather(f32[8,1,24]{2,1,0:T(1,128)S(1)} %all-to-all-done.1), channel_id=2, replica_groups=mesh['half'=2,'z'=8,'pair'=2,'y'=2,'x'=4,'core'=2] {'y'}, dimensions={0}, use_global_device_ids=true | all-gather | bytes 2304 | tf_op jit(solution)/shard_map/all_gather | solution.py:305
  25.7 4.2 %collective-permute-start = (f32[16,24]{1,0:T(8,128)S(1)}, f32[16,24]{1,0:T(8,128)S(1)}, u32[]{:S(2)}, u32[]{:S(2)}) collective-permute-start(f32[16,24]{1,0:T(8,128)S(1)} %bitcast.14), channel_id=1, source_target_pairs={{0,16},{16,0},{1,17},{17,1},{2,18},{18,2},{3,19},{19,3},{4,20},{20... | collective-permute-start | bytes 4616 | tf_op jit(solution)/shard_map/ppermute | solution.py:306
  29.9 0.1 fusion
  30.1 1.2 %collective-permute-done = f32[16,24]{1,0:T(8,128)S(1)} collective-permute-done((f32[16,24]{1,0:T(8,128)S(1)}, f32[16,24]{1,0:T(8,128)S(1)}, u32[]{:S(2)}, u32[]{:S(2)}) %collective-permute-start) | collective-permute-done | bytes 1568 | tf_op jit(solution)/shard_map/ppermute | solution.py:306
  31.3 7.4 %collective-permute-start.1 = (f32[32,24]{1,0:T(8,128)S(1)}, f32[32,24]{1,0:T(8,128)S(1)}, u32[]{:S(2)}, u32[]{:S(2)}) collective-permute-start(f32[32,24]{1,0:T(8,128)S(1)} %pad_maximum_fusion.1), channel_id=1, source_target_pairs={{0,256},{256,0},{1,257},{257,1},{2,258},{258,2},{3,259},{259,3},{4... | collective-permute-start | bytes 9224 | tf_op jit(solution)/shard_map/ppermute | solution.py:307
  38.8 0.1 maximum_bitcast_fusion.step
  38.8 1.9 %shard_map.78 = (bf16[512,1024]{1,0:T(8,128)(2,1)S(1)}, bf16[512,1024]{1,0:T(8,128)(2,1)S(1)}) custom-call(s32[1,512]{1,0:T(1,128)S(1)} %bitcast.12), custom_call_target="tpu_custom_call" | custom-call | tf_op jit(solution)/shard_map/pallas_call | solution.py:314
  40.8 1.0 %copy-done.1 = bf16[512,1024]{1,0:T(8,128)(2,1)} copy-done((bf16[512,1024]{1,0:T(8,128)(2,1)}, bf16[512,1024]{1,0:T(8,128)(2,1)S(1)}, u32[]{:S(2)}) %copy-start.1) | copy-done | bytes 1048600
  41.8 0.0 collective-permute-done.1
  41.8 0.4 shard_map.80.picks
  42.2 3.8 %all-to-all-done.arrived = bf16[8,64,768]{2,1,0:T(8,128)(2,1)S(1)} async-done(((bf16[8,64,768]{2,1,0:T(8,128)(2,1)}), bf16[8,64,768]{2,1,0:T(8,128)(2,1)S(1)}, u32[]{:S(2)}, u32[]{:S(2)}) %all-to-all-start) | async-done | bytes 786464 | tf_op jit(solution)/shard_map/all_to_all | solution.py:262
  46.1 1.4 %shard_map.81 = (bf16[8,32,512]{2,1,0:T(8,128)(2,1)S(1)}, bf16[1024,128]{1,0:T(8,128)(2,1)S(1)}) custom-call(bf16[8,64,768]{2,1,0:T(8,128)(2,1)S(1)} %all-to-all-done.arrived, f32[64,24]{1,0:T(8,128)S(1)} %pad_maximum_fusion.infos), custom_call_target="tpu_custom_call" | custom-call | tf_op jit(solution)/shard_map/pallas_call | solution.py:324
  47.5 12.4 %all_to_all.20.parts = bf16[8,32,512]{2,1,0:T(8,128)(2,1)S(1)} all-to-all(bf16[8,32,512]{2,1,0:T(8,128)(2,1)S(1)} %get-tuple-element.20), channel_id=1, replica_groups=mesh['half'=2,'z'=8,'pair'=2,'y'=2,'x'=4,'core'=2] {'z'}, dimensions={0} | all-to-all | bytes 524288 | tf_op jit(solution)/shard_map/all_to_all | solution.py:262
  59.9 0.8 shard_map.82
  60.7 24.9 %all_to_all.21 = bf16[64,16,128]{2,1,0:T(8,128)(2,1)S(1)} all-to-all(bf16[64,16,128]{2,1,0:T(8,128)(2,1)S(1)} %shard_map.82), channel_id=1, replica_groups=mesh['half'=2,'z'=8,'pair'=2,'y'=2,'x'=4,'core'=2] {'half','pair','y','x..., dimensions={0} | all-to-all | bytes 524288 | tf_op jit(solution)/shard_map/all_to_all | solution.py:262
  85.5 1.3 %shard_map.83 = (f32[16,64]{1,0:T(8,128)}, f32[2,12,1,1024]{3,2,1,0:T(1,128)}) custom-call(bf16[2,32,16,128]{3,2,1,0:T(8,128)(2,1)S(1)} %bitcast.10, bf16[512,1024]{1,0:T(8,128)(2,1)S(1)} %get-tuple-element.24.cosines, bf16[512,1024]{1,0:T(8,128)(2,1)S(1)} %copy-done.2, f32[1,512]{1,0:T(1,128)S(1)} %bitcast.13, f32[1,12]{1,0:T(1,128)S(1)} %multiply_add_fusion.radius), custom_call_target="tpu_custom_call" | custom-call | tf_op jit(solution)/shard_map/pallas_call | solution.py:339
  (12 shorter events, 0.0 us)
Async XLA Ops:
  0.6 11.6 %copy-start.3 = (bf16[16,32,512]{2,1,0:T(8,128)(2,1)S(1)}, bf16[16,32,512]{2,1,0:T(8,128)(2,1)}, u32[]{:S(2)}) copy-start(bf16[16,32,512]{2,1,0:T(8,128)(2,1)} %param.8) | copy-start | bytes 1572868
  0.6 11.5 %copy-start = (bf16[4,16,32,384]{3,2,1,0:T(8,128)(2,1)S(1)}, bf16[4,16,32,384]{3,2,1,0:T(8,128)(2,1)}, u32[]{:S(2)}) copy-start(bf16[4,16,32,384]{3,2,1,0:T(8,128)(2,1)} %param.6) | copy-start | bytes 4718596
  2.1 14.6 %all-to-all-start.1 = ((f32[8,1,24]{2,1,0:T(1,128)}), f32[8,1,24]{2,1,0:T(1,128)S(1)}, u32[]{:S(2)}, u32[]{:S(2)}) async-start(f32[8,1,24]{2,1,0:T(1,128)} %shard_map.79), calls=%async_computation.1 | async-start | bytes 8192 | tf_op jit(solution)/shard_map/all_to_all | solution.py:262
  12.2 10.3 %copy-start.5 = (s32[1,12]{1,0:T(1,128)S(1)}, s32[1,12]{1,0:T(1,128)}, u32[]{:S(2)}) copy-start(s32[1,12]{1,0:T(1,128)} %rows.1) | copy-start | bytes 148
  12.2 10.3 %copy-start.4 = (s32[512]{0:T(512)S(1)}, s32[512]{0:T(512)}, u32[]{:S(2)}) copy-start(s32[512]{0:T(512)} %orders_in.1) | copy-start | bytes 6148
  16.7 29.3 %all-to-all-start = ((bf16[8,64,768]{2,1,0:T(8,128)(2,1)}), bf16[8,64,768]{2,1,0:T(8,128)(2,1)S(1)}, u32[]{:S(2)}, u32[]{:S(2)}) async-start(bf16[8,64,768]{2,1,0:T(8,128)(2,1)} %shard_map.77), calls=%async_computation | async-start | bytes 1572864 | tf_op jit(solution)/shard_map/all_to_all | solution.py:262
  25.7 5.6 %collective-permute-start = (f32[16,24]{1,0:T(8,128)S(1)}, f32[16,24]{1,0:T(8,128)S(1)}, u32[]{:S(2)}, u32[]{:S(2)}) collective-permute-start(f32[16,24]{1,0:T(8,128)S(1)} %bitcast.14), channel_id=1, source_target_pairs={{0,16},{16,0},{1,17},{17,1},{2,18},{18,2},{3,19},{19,3},{4,20},{20... | collective-permute-start | bytes 4616 | tf_op jit(solution)/shard_map/ppermute | solution.py:306
  31.3 10.5 %collective-permute-start.1 = (f32[32,24]{1,0:T(8,128)S(1)}, f32[32,24]{1,0:T(8,128)S(1)}, u32[]{:S(2)}, u32[]{:S(2)}) collective-permute-start(f32[32,24]{1,0:T(8,128)S(1)} %pad_maximum_fusion.1), channel_id=1, source_target_pairs={{0,256},{256,0},{1,257},{257,1},{2,258},{258,2},{3,259},{259,3},{4... | collective-permute-start | bytes 9224 | tf_op jit(solution)/shard_map/ppermute | solution.py:307
  40.8 1.0 %copy-start.1 = (bf16[512,1024]{1,0:T(8,128)(2,1)}, bf16[512,1024]{1,0:T(8,128)(2,1)S(1)}, u32[]{:S(2)}) copy-start(bf16[512,1024]{1,0:T(8,128)(2,1)S(1)} %get-tuple-element.25.sines) | copy-start | bytes 3145732
  47.5 38.1 %copy-start.2 = (bf16[512,1024]{1,0:T(8,128)(2,1)S(1)}, bf16[512,1024]{1,0:T(8,128)(2,1)}, u32[]{:S(2)}) copy-start(bf16[512,1024]{1,0:T(8,128)(2,1)} %copy-done.1) | copy-start | bytes 3145732
